TPU v7x, 32 devices: a whole 2x2x4 slice. The times are simulated.
32 devices in a mesh: dp: 2 (over x), tp: 4 (over z), sp: 4 (over y, core).
Axes of the slice: x: 2, y: 2, z: 4, core: 2. Of those that a mesh axis runs over, the one named last changes fastest.
Arguments:
- x_in: bfloat16 [16384, 2560], P(('dp', 'sp')), parts along dimension 0
- w_z: bfloat16 [2560, 5120], P(None, 'tp')
- w_x: bfloat16 [2560, 5120], P(None, 'tp')
- w_bc: bfloat16 [2560, 256], replicated
- w_dt: bfloat16 [2560, 80], P(None, 'tp')
- a_neg: float32 [80], P('tp')
- dt_bias: float32 [80], P('tp')
- d_skip: float32 [80], P('tp')
- w_out: bfloat16 [5120, 2560], P('tp')
Outputs:
- output: bfloat16 [16384, 2560], P(('dp', 'sp', 'tp')), parts along dimension 0
There are 2 independent parts. A program takes and returns all parts, laid end to end along the dimension named above; an argument that names none is the same for every part.
All inputs are finite; a program needn't handle non-finite values.
Results may differ from a plain program's by a relative error of at most 0.0112365.
Values are sent between devices in bfloat16 or wider.
A program may use at most 1 GiB of HBM per device.

v0:
```python
import jax
import jax.numpy as jnp
from jax import lax
from jax.sharding import PartitionSpec as P

PIECE_LEN = 64


def local_ssd(x_ssm, dt_step, log_a, b_mat, c_mat):
    tokens, heads, head_dim = x_ssm.shape
    n_state = b_mat.shape[1]
    n_pieces = tokens // PIECE_LEN
    x_pc = x_ssm.reshape(n_pieces, PIECE_LEN, heads, head_dim)
    dt_pc = dt_step.reshape(n_pieces, PIECE_LEN, heads)
    la_pc = log_a.reshape(n_pieces, PIECE_LEN, heads)
    b_pc = b_mat.reshape(n_pieces, PIECE_LEN, n_state)
    c_pc = c_mat.reshape(n_pieces, PIECE_LEN, n_state)
    cum_log = jnp.cumsum(la_pc, axis=1)
    positions = jnp.arange(PIECE_LEN)
    causal = (positions[:, None] >= positions[None, :])[None, :, :, None]
    decay = jnp.where(causal, jnp.exp(jnp.minimum(cum_log[:, :, None, :] - cum_log[:, None, :, :], 0.0)), 0.0)
    gram = jnp.einsum('ctn,csn->cts', c_pc, b_pc, preferred_element_type=jnp.float32)
    weights = gram[:, :, :, None] * decay * dt_pc[:, None, :, :]
    y_intra = jnp.einsum('ctsh,cshp->cthp', weights, x_pc, preferred_element_type=jnp.float32)
    piece_tail = cum_log[:, -1, :]
    to_end = jnp.exp(piece_tail[:, None, :] - cum_log) * dt_pc
    piece_states = jnp.einsum('csh,cshp,csn->chpn', to_end, x_pc, b_pc, preferred_element_type=jnp.float32)
    piece_ends = jnp.cumsum(piece_tail, axis=0)
    piece_starts = piece_ends - piece_tail
    piece_ids = jnp.arange(n_pieces)
    earlier = (piece_ids[:, None] > piece_ids[None, :])[:, :, None]
    pass_w = jnp.where(earlier, jnp.exp(jnp.minimum(piece_starts[:, None, :] - piece_ends[None, :, :], 0.0)), 0.0)
    piece_in = jnp.einsum('cjh,jhpn->chpn', pass_w, piece_states, preferred_element_type=jnp.float32)
    y_pass = jnp.einsum('chpn,ctn->cthp', piece_in, c_pc, preferred_element_type=jnp.float32) * jnp.exp(cum_log)[:, :, :, None]
    block_state = jnp.einsum('jh,jhpn->hpn', jnp.exp(piece_ends[-1][None, :] - piece_ends), piece_states, preferred_element_type=jnp.float32)
    from_start = cum_log + piece_starts[:, None, :]
    y_local = (y_intra + y_pass).reshape(tokens, heads, head_dim)
    return y_local, block_state, piece_ends[-1], from_start.reshape(tokens, heads)


def solution(mesh):
    n_model = mesh.shape['tp']

    def device_fn(x_blk, w_z, w_x, w_bc, w_dt, a_neg, dt_bias, d_skip, w_out):
        tokens = x_blk.shape[0]
        heads = a_neg.shape[0]
        inner = w_x.shape[1]
        head_dim = inner // heads
        n_state = w_bc.shape[1] // 2
        z_gate = jnp.dot(x_blk, w_z, preferred_element_type=jnp.float32).astype(jnp.bfloat16)
        x_proj = jnp.dot(x_blk, w_x, preferred_element_type=jnp.float32).astype(jnp.bfloat16)
        x_ssm = x_proj.astype(jnp.float32).reshape(tokens, heads, head_dim)
        bc_val = jnp.dot(x_blk, w_bc, preferred_element_type=jnp.float32).astype(jnp.bfloat16).astype(jnp.float32)
        b_mat = bc_val[:, :n_state]
        c_mat = bc_val[:, n_state:]
        c_flip = c_mat[::-1]
        dt_step = jax.nn.softplus(jnp.dot(x_blk, w_dt, preferred_element_type=jnp.float32) + dt_bias)
        log_a = dt_step * a_neg
        y_fwd, state_fwd, block_log, from_fwd = local_ssd(x_ssm, dt_step, log_a, b_mat, c_mat)
        y_flip, state_bwd, _, from_bwd = local_ssd(x_ssm[::-1], dt_step[::-1], log_a[::-1], b_mat[::-1], c_flip)
        all_states = lax.all_gather(jnp.stack([state_fwd, state_bwd]), 'sp')
        all_logs = lax.all_gather(block_log, 'sp')
        n_seq = all_logs.shape[0]
        dev_index = lax.axis_index('sp')
        dev_ids = jnp.arange(n_seq)[:, None]
        log_ends = jnp.cumsum(all_logs, axis=0)
        log_starts = log_ends - all_logs
        my_start = jnp.sum(jnp.where(dev_ids < dev_index, all_logs, 0.0), axis=0)
        my_end = my_start + block_log
        w_fwd = jnp.where(dev_ids < dev_index, jnp.exp(jnp.minimum(my_start[None, :] - log_ends, 0.0)), 0.0)
        w_bwd = jnp.where(dev_ids > dev_index, jnp.exp(jnp.minimum(log_starts - my_end[None, :], 0.0)), 0.0)
        h_fwd = jnp.einsum('jh,jhpn->hpn', w_fwd, all_states[:, 0], preferred_element_type=jnp.float32)
        h_bwd = jnp.einsum('jh,jhpn->hpn', w_bwd, all_states[:, 1], preferred_element_type=jnp.float32)
        y_fwd = y_fwd + jnp.exp(from_fwd)[:, :, None] * jnp.einsum('hpn,tn->thp', h_fwd, c_mat, preferred_element_type=jnp.float32)
        y_bwd = (y_flip + jnp.exp(from_bwd)[:, :, None] * jnp.einsum('hpn,tn->thp', h_bwd, c_flip, preferred_element_type=jnp.float32))[::-1]
        y_sum = y_fwd + y_bwd + 2.0 * d_skip[:, None] * x_ssm
        gated = (y_sum.reshape(tokens, inner) * jax.nn.silu(z_gate.astype(jnp.float32))).astype(jnp.bfloat16)
        partial_out = jnp.dot(gated, w_out, preferred_element_type=jnp.float32)
        summed = lax.psum_scatter(partial_out, 'tp', scatter_dimension=0, tiled=True)
        rows = tokens // n_model
        resid = lax.dynamic_slice_in_dim(x_blk, lax.axis_index('tp') * rows, rows, axis=0)
        return (resid.astype(jnp.float32) + summed).astype(jnp.bfloat16)

    in_specs = (P(('dp', 'sp'), None), P(None, 'tp'), P(None, 'tp'), P(None, None), P(None, 'tp'), P('tp'), P('tp'), P('tp'), P('tp', None))
    out_specs = P(('dp', 'sp', 'tp'), None)
    return jax.shard_map(device_fn, mesh=mesh, in_specs=in_specs, out_specs=out_specs, check_vma=False)
```

profile of v0, /device:TPU:0, one launch (start us, length us, event | category | flops | bytes accessed | tf_op | source)
XLA Modules:
  0.0 851.7 jit_solution(2967734727273803117)
XLA Ops:
  6.5 7.0 broadcast_multiply_fusion
  15.6 5.4 rev.19
  23.0 6.6 fusion.104
  41.8 6.1 all-gather.1
  60.0 6.9 convolution_convert_fusion.2
  68.1 6.5 rev.21
  74.6 20.2 %convolution_convert_fusion.1 = bf16[2048,1280]{0,1:T(8,128)(2,1)} fusion(bf16[2048,2560]{1,0:T(8,128)(2,1)} %param.9, bf16[2560,1280]{1,0:T(8,128)(2,1)} %param.11), kind=kOutput, calls=%fused_computation.63 | convolution fusion | flops 13424394240 | bytes 22282240 | tf_op jit(solution)/shard_map/dot_general | solution.py:51
  94.7 15.9 %reshape_reshape.3 = bf16[32,64,20,64]{1,0,3,2:T(8,128)(2,1)} reshape(bf16[2048,1280]{0,1:T(8,128)(2,1)} %convolution_convert_fusion.1) | data formatting | bytes 10485760 | tf_op jit(solution)/shard_map/reshape;reshape | solution.py:13
  110.6 20.5 %rev.20 = f32[2048,20,64]{0,2,1:T(8,128)} reverse(bf16[2048,20,64]{0,2,1:T(8,128)(2,1)} %bitcast.148), dimensions={0} | reverse | bytes 15728640 | tf_op jit(solution)/shard_map/rev | solution.py:60
  131.1 17.8 %reshape.138 = f32[32,64,20,64]{1,0,3,2:T(8,128)} reshape(f32[2048,20,64]{0,2,1:T(8,128)} %rev.20) | data formatting | bytes 20971520 | tf_op jit(solution)/shard_map/reshape | solution.py:13
  148.9 8.9 %fusion.13 = bf16[32,20,64,128]{3,2,1,0:T(8,128)(2,1)S(1)} fusion(bf16[32,64,128,1]{2,1,3,0:T(8,128)(2,1)} %bitcast.157, f32[32,64,20]{1,2,0:T(8,128)} %copy.63, bf16[32,64,20,64]{1,0,3,2:T(8,128)(2,1)} %reshape_reshape.3), kind=kOutput, calls=%fused_computation.15 | convolution fusion | flops 676331520 | bytes 16416768 | tf_op jit(solution)/shard_map/csh,cshp,csn->chpn/dot_general | solution.py:27
  157.9 3.9 copy-done.2
  161.8 5.8 fusion.29
  167.6 17.5 %fusion.11 = bf16[32,20,64,128]{3,2,1,0:T(8,128)(2,1)} fusion(bf16[32,64,128,1]{2,1,3,0:T(8,128)(2,1)S(1)} %bitcast.155, f32[32,64,20,64]{1,0,3,2:T(8,128)} %reshape.138, f32[32,64,20]{1,2,0:T(8,128)S(1)} %copy-done.6), kind=kOutput, calls=%fused_computation.13 | convolution fusion | flops 673710080 | bytes 21659648 | tf_op jit(solution)/shard_map/csh,cshp,csn->chpn/dot_general | solution.py:27
  185.1 9.9 %fusion.23 = f32[20,1,64,128]{3,1,2,0:T(1,128)S(1)} fusion(bf16[32,20,1,1]{0,2,3,1:T(2,128)(2,1)S(1)} %copy.97, bf16[32,20,64,128]{3,2,1,0:T(8,128)(2,1)} %fusion.11), kind=kOutput, calls=%fused_computation.25 | convolution fusion | flops 10485760 | bytes 11142400 | tf_op jit(solution)/shard_map/jh,jhpn->hpn/dot_general | solution.py:35
  214.9 11.0 %fusion.54 = bf16[32,20,64,128]{3,0,2,1:T(8,128)(2,1)S(1)} fusion(bf16[32,20,64,128]{3,2,1,0:T(8,128)(2,1)} %copy-done.2, f32[32,20]{0,1:T(8,128)S(1)} %copy.66, f32[32,20]{0,1:T(8,128)S(1)} %copy.65, pred[32,32]{1,0:T(8,128)(4,1)S(1)} %iota_compare_fusion.1), kind=kOutput, calls=%fused_computation.60 | convolution fusion | flops 335605760 | bytes 20977664 | tf_op jit(solution)/shard_map/cjh,jhpn->chpn/dot_general | solution.py:33
  225.9 15.2 %fusion.2 = f32[32,64,20,64]{1,3,2,0:T(8,128)} fusion(bf16[32,64,128,1]{2,1,3,0:T(8,128)(2,1)S(1)} %bitcast.154, bf16[32,20,64,128]{3,0,2,1:T(8,128)(2,1)S(1)} %fusion.54), kind=kOutput, calls=%fused_computation.4 | convolution fusion | flops 671088640 | bytes 21495808 | tf_op jit(solution)/shard_map/chpn,ctn->cthp/dot_general | solution.py:34
  241.2 15.6 %bitcast_add_fusion.1 = f32[32,64,20,64]{1,3,2,0:T(8,128)S(1)} fusion(f32[32,64,20,64]{1,3,2,0:T(8,128)} %fusion.2, f32[32,64,20]{1,2,0:T(8,128)} %copy.69, f32[32,64,20]{1,2,0:T(8,128)} %copy.60, f32[32,64,20]{1,2,0:T(8,128)} %copy.58, f32[32,64,64]{2,1,0:T(8,128)S(1)} %fusion.105, pred[64,64]{1,0:T(8,128)(4,1)S(1)} %iota_compare_fusion, ...), kind=kOutput, calls=%fused_computation.1 | convolution fusion | flops 353894400 | bytes 27234304 | tf_op jit(solution)/shard_map/ctsh,cshp->cthp/dot_general | solution.py:24
  256.8 14.6 %copy.71 = f32[32,64,20,64]{1,0,3,2:T(8,128)} copy(f32[32,64,20,64]{1,3,2,0:T(8,128)S(1)} %bitcast_add_fusion.1) | data formatting | bytes 20971520 | tf_op jit(solution)/shard_map/add | solution.py:37
  271.5 18.5 %reshape.133 = f32[2048,20,64]{0,2,1:T(8,128)} reshape(f32[32,64,20,64]{1,0,3,2:T(8,128)} %copy.71) | data formatting | bytes 20971520 | tf_op jit(solution)/shard_map/reshape | solution.py:37
  290.0 11.0 %fusion.57 = bf16[32,20,64,128]{3,0,2,1:T(8,128)(2,1)S(1)} fusion(bf16[32,20,64,128]{3,2,1,0:T(8,128)(2,1)} %fusion.11, f32[32,20]{0,1:T(8,128)S(1)} %copy.82, f32[32,20]{0,1:T(8,128)S(1)} %copy.81, pred[32,32]{1,0:T(8,128)(4,1)S(1)} %iota_compare_fusion.1), kind=kOutput, calls=%fused_computation.61 | convolution fusion | flops 335605760 | bytes 20977664 | tf_op jit(solution)/shard_map/cjh,jhpn->chpn/dot_general | solution.py:33
  301.4 15.4 %fusion = f32[32,64,20,64]{1,3,2,0:T(8,128)} fusion(bf16[32,64,128,1]{2,1,3,0:T(8,128)(2,1)S(1)} %bitcast.152, bf16[32,20,64,128]{3,0,2,1:T(8,128)(2,1)S(1)} %fusion.57), kind=kOutput, calls=%fused_computation.2 | convolution fusion | flops 671088640 | bytes 21495808 | tf_op jit(solution)/shard_map/chpn,ctn->cthp/dot_general | solution.py:34
  316.9 30.2 %bitcast_add_fusion = f32[32,64,20,64]{1,3,2,0:T(8,128)} fusion(f32[32,64,20,64]{1,3,2,0:T(8,128)} %fusion, f32[32,64,20]{1,2,0:T(8,128)} %copy.85, f32[32,64,20]{1,2,0:T(8,128)S(1)} %copy-done.10, f32[32,64,20]{1,2,0:T(8,128)} %copy.77, f32[32,64,64]{2,1,0:T(8,128)S(1)} %fusion.106, pred[64,64]{1,0:T(8,128)(4,1)S(1)} %iota_compare_fusion, ...), kind=kOutput, calls=%fused_computation | convolution fusion | flops 353894400 | bytes 32477184 | tf_op jit(solution)/shard_map/ctsh,cshp->cthp/dot_general | solution.py:24
  347.0 21.6 %copy.87 = f32[32,64,20,64]{1,0,3,2:T(8,128)} copy(f32[32,64,20,64]{1,3,2,0:T(8,128)} %bitcast_add_fusion) | data formatting | bytes 20971520 | tf_op jit(solution)/shard_map/add | solution.py:37
  368.6 18.5 %reshape.141 = f32[2048,20,64]{0,2,1:T(8,128)} reshape(f32[32,64,20,64]{1,0,3,2:T(8,128)} %copy.87) | data formatting | bytes 20971520 | tf_op jit(solution)/shard_map/reshape | solution.py:37
  390.5 9.5 %multiply_add_fusion.1 = f32[2048,20,64]{0,2,1:T(8,128)} fusion(f32[2048,20,64]{0,2,1:T(8,128)} %reshape.141, f32[2048,20]{0,1:T(8,128)S(1)} %exp.87, f32[20,64,128]{2,1,0:T(8,128)S(1)} %bitcast.162, bf16[2048,128]{1,0:T(8,128)(2,1)S(1)} %rev.22), kind=kOutput, calls=%fused_computation.42 | convolution fusion | flops 676331520 | bytes 22315008 | tf_op jit(solution)/shard_map/hpn,tn->thp/dot_general | solution.py:75
  400.0 22.9 %rev.23 = f32[2048,20,64]{0,2,1:T(8,128)} reverse(f32[2048,20,64]{0,2,1:T(8,128)} %multiply_add_fusion.1), dimensions={0} | reverse | bytes 20971520 | tf_op jit(solution)/shard_map/rev | solution.py:75
  424.0 14.0 %multiply_add_fusion = f32[2048,20,64]{0,2,1:T(8,128)} fusion(f32[2048,20,64]{0,2,1:T(8,128)} %rev.23, f32[2048,20,64]{0,2,1:T(8,128)} %reshape.133, f32[20]{0:T(128)S(1)} %broadcast_multiply_fusion.1, f32[2048,20]{0,1:T(8,128)S(1)} %copy-done.9, f32[20,64,128]{2,1,0:T(8,128)S(1)} %bitcast.163, bf16[2048,20,64]{0,2,1:T(8,128)(2,1)} %bitcast.149, ...), kind=kOutput, calls=%fused_computation.41 | convolution fusion | flops 686817280 | bytes 38076928 | tf_op jit(solution)/shard_map/hpn,tn->thp/dot_general | solution.py:74
  438.1 11.3 %copy.89 = f32[2048,1280]{1,0:T(8,128)} copy(f32[2048,1280]{0,1:T(8,128)} %bitcast.150) | data formatting | bytes 20971520 | tf_op jit(solution)/shard_map/reshape | solution.py:77
  449.3 41.3 %fusion.72 = f32[2048,2560]{1,0:T(8,128)} fusion(bf16[1280,2560]{1,0:T(8,128)(2,1)} %param.17, f32[2048,1280]{1,0:T(8,128)} %copy.89, bf16[2048,2560]{1,0:T(8,128)(2,1)} %param.9, bf16[2560,1280]{1,0:T(8,128)(2,1)} %param.10), kind=kOutput, calls=%fused_computation.73 | convolution fusion | flops 26864517120 | bytes 55050240 | tf_op jit(solution)/shard_map/dot_general | solution.py:78
  490.7 348.2 %reduce-scatter.2.cloned.1.call-done = f32[512,2560]{1,0:T(8,128)} async-done(((f32[2048,2560]{1,0:T(8,128)}), f32[512,2560]{1,0:T(8,128)}) %reduce-scatter.2.cloned.1.call-update) | async-done | bytes 5242896 | tf_op jit(solution)/shard_map/reduce_scatter | solution.py:79
  838.9 5.6 add_convert_fusion
  (90 shorter events, 54.2 us)
Async XLA Ops:
  6.5 53.5 %copy-start = (bf16[2560,256]{1,0:T(8,128)(2,1)S(1)}, bf16[2560,256]{1,0:T(8,128)(2,1)}, u32[]{:S(2)}) copy-start(bf16[2560,256]{1,0:T(8,128)(2,1)} %param.12) | copy-start | bytes 3932164
  6.5 380.6 %all-gather.4.cloned.1.call-start = ((), (), s32[]{:S(2)}) async-start(), calls=%async_computation.2 | async-start | bytes 3276800 | tf_op jit(solution)/shard_map/all_gather | solution.py:61
  66.9 1.1 copy-start.7
  74.6 93.1 %copy-start.3 = (bf16[2048,128]{1,0:T(8,128)(2,1)}, bf16[2048,128]{1,0:T(8,128)(2,1)S(1)}, u32[]{:S(2)}) copy-start(bf16[2048,128]{1,0:T(8,128)(2,1)S(1)} %rev.21) | copy-start | bytes 1572868
  157.9 3.9 copy-start.2
  161.8 5.8 copy-start.6
  185.1 12.9 %copy-start.5 = (f32[32,64,20]{1,0,2:T(8,128)S(1)}, f32[32,64,20]{1,0,2:T(8,128)}, u32[]{:S(2)}) copy-start(f32[32,64,20]{1,0,2:T(8,128)} %mul.107) | copy-start | bytes 491524
  185.1 17.0 %copy-start.12 = (pred[4]{0:T(512)(128)(4,1)S(1)}, pred[4]{0:T(512)(128)(4,1)}, u32[]{:S(2)}) copy-start(pred[4]{0:T(512)(128)(4,1)} %get-tuple-element.23) | copy-start | bytes 16
  196.0 642.9 %reduce-scatter.2.cloned.1.call-start = ((), (), s32[]{:S(2)}) async-start(), calls=%async_computation.1 | async-start | bytes 26214400 | tf_op jit(solution)/shard_map/reduce_scatter | solution.py:79
  290.0 11.1 %copy-start.4 = (bf16[2048,128]{1,0:T(8,128)(2,1)S(1)}, bf16[2048,128]{1,0:T(8,128)(2,1)}, u32[]{:S(2)}) copy-start(bf16[2048,128]{1,0:T(8,128)(2,1)} %copy-done.3) | copy-start | bytes 1572868
  301.4 15.4 %copy-start.10 = (f32[32,64,20]{1,2,0:T(8,128)S(1)}, f32[32,64,20]{1,2,0:T(8,128)}, u32[]{:S(2)}) copy-start(f32[32,64,20]{1,2,0:T(8,128)} %copy.79) | copy-start | bytes 491524
  368.6 18.5 %copy-start.13 = (f32[20]{0:T(128)S(1)}, f32[20]{0:T(128)}, u32[]{:S(2)}) copy-start(f32[20]{0:T(128)} %param.16) | copy-start | bytes 244
  400.0 22.9 %copy-start.11 = (bf16[4,20,1,1]{0,2,3,1:T(2,128)(2,1)S(1)}, bf16[4,20,1,1]{0,2,3,1:T(2,128)(2,1)}, u32[]{:S(2)}) copy-start(bf16[4,20,1,1]{0,2,3,1:T(2,128)(2,1)} %copy.99) | copy-start | bytes 484
  400.0 24.0 %copy-start.8 = (bf16[2048,256]{1,0:T(8,128)(2,1)S(1)}, bf16[2048,256]{1,0:T(8,128)(2,1)}, u32[]{:S(2)}) copy-start(bf16[2048,256]{1,0:T(8,128)(2,1)} %copy-done.7) | copy-start | bytes 3145732
  400.0 24.0 %copy-start.9 = (f32[2048,20]{0,1:T(8,128)S(1)}, f32[2048,20]{0,1:T(8,128)}, u32[]{:S(2)}) copy-start(f32[2048,20]{0,1:T(8,128)} %exp.78) | copy-start | bytes 491524
  490.7 353.8 %copy-start.1 = (bf16[2560,256]{1,0:T(8,128)(2,1)S(1)}, bf16[2560,256]{1,0:T(8,128)(2,1)}, u32[]{:S(2)}) copy-start(bf16[2560,256]{1,0:T(8,128)(2,1)} %param.12) | copy-start | bytes 3932164
Sparse Core Ops, SparseCore 0:
  196.2 26.9 all-gather.3
  490.8 348.0 reduce-scatter.1
where the time goes:
time: 864 us; the launch traced here: 852 us
  waiting for transfers between devices  348 us (40%)
  matrix products  244 us (28%)
  local copies, waits for them, and re-layouts  217 us (25%)
  other arithmetic  22.1 us (3%)
  between operations  14.1 us (2%)
    reduce_scatter x1, waiting for transfers between devices, device_fn(): lax.psum_scatter(partial_out, 'tp', scatter_dimension=0, tiled=True)  348 us
    dot_general x2, matrix products, local_ssd(): jnp.einsum('ctsh,cshp->cthp', weights, x_pc, preferred_element_type=jnp.f...  45.8 us
    dot_general x1, matrix products, device_fn(): partial_out = jnp.dot(gated, w_out, preferred_element_type=jnp.float32)  41.3 us
    reshape x2, local copies, waits for them, and re-layouts, local_ssd(): y_local = (y_intra + y_pass).reshape(tokens, heads, head_dim)  37 us
    add x2, local copies, waits for them, and re-layouts, local_ssd(): y_local = (y_intra + y_pass).reshape(tokens, heads, head_dim)  36.2 us
    dot_general x2, matrix products, local_ssd(): jnp.einsum('chpn,ctn->cthp', piece_in, c_pc, preferred_element_type=jnp.f...  30.7 us
    dot_general x2, matrix products, local_ssd(): jnp.einsum('csh,cshp,csn->chpn', to_end, x_pc, b_pc, preferred_element_ty...  26.4 us
    rev x1, local copies, waits for them, and re-layouts, device_fn(): (y_flip + jnp.exp(from_bwd)[:, :, None] * jnp.einsum('hpn,tn->thp', h_bwd...  22.9 us
  transfers between devices with their start and end apart: 2, of which 1 were waited for; matrix products, arithmetic and copies ran while one was open for 22% of the time, Pallas kernels for 0%

commit v1 on v0

v1 whole, which is shorter than its diff:
```python
import functools

import jax
import jax.numpy as jnp
from jax import lax
from jax.experimental import pallas as pl
from jax.experimental.pallas import tpu as pltpu
from jax.sharding import PartitionSpec as P


CHUNK = 128
LANES = 128
SLOT = 32
LOG2E = 1.4426950408889634
F32 = jnp.float32
BF16 = jnp.bfloat16


def prep_kernel(x_ref, wbc_ref, wdt_ref, par_ref, bc_ref, cols_ref, rows_ref, log_ref):
    x_val = x_ref[...]
    bc_ref[...] = jnp.dot(x_val, wbc_ref[...], preferred_element_type=F32).astype(BF16)
    raw = lax.dot_general(x_val, wdt_ref[...], (((1,), (1,)), ((), ())), preferred_element_type=F32) + par_ref[0:1, :]
    dt_val = jnp.maximum(raw, 0.0) + jnp.log1p(jnp.exp(-jnp.abs(raw)))
    la_val = jnp.maximum(dt_val * par_ref[1:2, :] * LOG2E, -1024.0)
    row = lax.broadcasted_iota(jnp.int32, (CHUNK, CHUNK), 0)
    lane = lax.broadcasted_iota(jnp.int32, (CHUNK, CHUNK), 1)
    tri = jnp.where(row >= lane, 1.0, 0.0).astype(F32)

    @pl.when(pl.program_id(0) == 0)
    def _():
        log_ref[...] = jnp.zeros_like(log_ref)

    for c in range(x_val.shape[0] // CHUNK):
        part = slice(c * CHUNK, (c + 1) * CHUNK)
        la_c = la_val[part, :]
        cum = jnp.dot(tri, la_c, preferred_element_type=F32, precision=lax.Precision.HIGHEST)
        col = jnp.where(lane < SLOT, cum, jnp.where(lane < 2 * SLOT, cum - la_c, dt_val[part, :]))
        cols_ref[part, :] = col
        rows_ref[:, part] = col.T
        log_ref[...] += col[CHUNK - 1:CHUNK, :]


def proj_kernel(n_tiles, x_ref, *refs):
    o_ref = refs[-1]
    x_val = x_ref[...]
    for i in range(n_tiles):
        o_ref[:, i * 256:(i + 1) * 256] = jnp.dot(x_val, refs[i][...], preferred_element_type=F32).astype(BF16)


def sum_kernel(n_tiles, n_pieces, acc_ref, *refs):
    o_ref = refs[-1]
    total = acc_ref[...].astype(F32)
    for i in range(n_pieces):
        g_ref, w_refs = refs[sum(n_tiles[:i]) + i], refs[sum(n_tiles[:i]) + i + 1:sum(n_tiles[:i + 1]) + i + 1]
        for t in range(n_tiles[i]):
            total = total + jnp.dot(g_ref[:, t * 256:(t + 1) * 256], w_refs[t][...], preferred_element_type=F32)
    o_ref[...] = total.astype(o_ref.dtype)


def pair_cols(cols, head, low):
    first = jnp.broadcast_to(cols[:, head:head + 1], (cols.shape[0], LANES))
    second = jnp.broadcast_to(cols[:, head + 1:head + 2], (cols.shape[0], LANES))
    return first, second, jnp.where(low, first, second)


def state_kernel(first_head, n_pairs, u_ref, bc_ref, cols_ref, after_ref, gloc_ref, suf_ref, sf_ref, sb_ref, g_acc, f_acc, suf_acc, v_buf):
    step = pl.program_id(0)
    width = n_pairs * LANES

    @pl.when(step == 0)
    def _():
        g_acc[...] = jnp.zeros_like(g_acc)
        f_acc[...] = jnp.zeros_like(f_acc)
        suf_acc[...] = jnp.zeros_like(suf_acc)

    cols = cols_ref[...]
    low = lax.broadcasted_iota(jnp.int32, (CHUNK, LANES), 1) < LANES // 2
    suffix = suf_acc[...]
    suf_ref[0] = suffix
    gloc_ref[0] = g_acc[...]
    totals = []
    for p in range(n_pairs):
        head = first_head + 2 * p
        part = slice(p * LANES, (p + 1) * LANES)
        cum = pair_cols(cols, head, low)[2]
        exc = pair_cols(cols, SLOT + head, low)[2]
        dt_val = pair_cols(cols, 2 * SLOT + head, low)[2]
        scaled = u_ref[:, part].astype(F32) * dt_val
        total = cum[CHUNK - 1:CHUNK, :]
        totals.append(total)
        v_buf[:, part] = (scaled * jnp.exp2(exc)).astype(BF16)
        v_buf[:, slice(width + p * LANES, width + (p + 1) * LANES)] = (scaled * jnp.exp2(total + suffix[0:1, part] - cum)).astype(BF16)
    total = jnp.concatenate(totals, axis=1)
    sums = lax.dot_general(bc_ref[:, :LANES], v_buf[...], (((0,), (0,)), ((), ())), preferred_element_type=F32)
    g_acc[...] = g_acc[...] * jnp.exp2(total) + sums[:, :width]
    f_acc[...] += sums[:, width:]
    suf_acc[...] = suffix + total

    @pl.when(step == pl.num_programs(0) - 1)
    def _():
        sf_ref[...] = f_acc[...].astype(BF16)
        sb_ref[...] = g_acc[...].astype(BF16)


def out_kernel(first_head, n_pairs, u_ref, z_ref, bc_ref, cols_ref, rows_ref, gloc_ref, suf_ref, r1_ref, r2_ref, r3_ref, mix_ref, after_ref, g_ref, f_acc, hb_acc, wide, v_buf):
    step = pl.program_id(0)

    @pl.when(step == 0)
    def _():
        for p in range(n_pairs):
            wide[:, p * LANES:(p + 1) * LANES] = pair_cols(mix_ref[...], first_head + 2 * p, lax.broadcasted_iota(jnp.int32, (8, LANES), 1) < LANES // 2)[2]
        got = [r[...].astype(F32) for r in (r1_ref, r2_ref, r3_ref)]
        f_acc[...] = sum(got[s] * wide[s:s + 1, :] for s in range(3))
        hb_acc[...] = sum(got[s] * wide[3 + s:4 + s, :] for s in range(3))

    cols = cols_ref[...]
    row = lax.broadcasted_iota(jnp.int32, (CHUNK, LANES), 0)
    lane = lax.broadcasted_iota(jnp.int32, (CHUNK, LANES), 1)
    low = lane < LANES // 2
    b_val = bc_ref[:, :LANES]
    c_val = bc_ref[:, LANES:]
    gram = lax.dot_general(c_val, b_val, (((1,), (1,)), ((), ())), preferred_element_type=F32)
    gram = jnp.where(row == lane, 2.0 * gram, gram)
    back = (gloc_ref[0] + hb_acc[...] * jnp.exp2(suf_ref[0, 0:1, :])).astype(BF16)
    y_fwd = jnp.dot(c_val, f_acc[...].astype(BF16), preferred_element_type=F32)
    y_bwd = jnp.dot(c_val, back, preferred_element_type=F32)
    totals = []
    for p in range(n_pairs):
        head = first_head + 2 * p
        part = slice(p * LANES, (p + 1) * LANES)
        cum0, cum1, cum = pair_cols(cols, head, low)
        exc0, exc1, exc = pair_cols(cols, SLOT + head, low)
        dt_val = pair_cols(cols, 2 * SLOT + head, low)[2]
        u_val = u_ref[:, part].astype(F32)
        scaled = u_val * dt_val
        m0 = jnp.exp2(jnp.minimum(cum0 - rows_ref[head:head + 1, :], rows_ref[SLOT + head:SLOT + head + 1, :] - exc0)) * gram
        m1 = jnp.exp2(jnp.minimum(cum1 - rows_ref[head + 1:head + 2, :], rows_ref[SLOT + head + 1:SLOT + head + 2, :] - exc1)) * gram
        mix = jnp.concatenate([m0.astype(BF16), m1.astype(BF16)], axis=1)
        rhs = jnp.concatenate([jnp.where(low, scaled, 0.0).astype(BF16), jnp.where(low, 0.0, scaled).astype(BF16)], axis=0)
        total = cum[CHUNK - 1:CHUNK, :]
        totals.append(total)
        y_val = jnp.dot(mix, rhs, preferred_element_type=F32)
        y_val = y_val + jnp.exp2(cum) * y_fwd[:, part] + jnp.exp2(total - exc) * y_bwd[:, part]
        y_val = y_val + wide[6:7, part] * u_val
        z_val = z_ref[:, part].astype(F32)
        g_ref[:, part] = (y_val * (z_val * jax.nn.sigmoid(z_val))).astype(BF16)
        v_buf[:, part] = (scaled * jnp.exp2(total - cum)).astype(BF16)
    total = jnp.concatenate(totals, axis=1)
    sums = lax.dot_general(b_val, v_buf[...], (((0,), (0,)), ((), ())), preferred_element_type=F32)
    f_acc[...] = f_acc[...] * jnp.exp2(total) + sums


def params():
    return pltpu.CompilerParams(dimension_semantics=("arbitrary",), vmem_limit_bytes=62 << 20)


def cost(flops, moved):
    return pl.CostEstimate(flops=int(flops), bytes_accessed=int(moved), transcendentals=0)


ANY = pl.BlockSpec(memory_space=pl.ANY)


def prep(x_blk, w_bc, w_dt_rows, par):
    tokens, d_model = x_blk.shape
    tile = min(512, tokens)
    whole = lambda a: pl.BlockSpec(a.shape, lambda i: (0, 0))
    return pl.pallas_call(
        prep_kernel,
        grid=(tokens // tile,),
        in_specs=[pl.BlockSpec((tile, d_model), lambda i: (i, 0)), whole(w_bc), whole(w_dt_rows), whole(par)],
        out_specs=[pl.BlockSpec((tile, 2 * LANES), lambda i: (i, 0)), pl.BlockSpec((tile, LANES), lambda i: (i, 0)), pl.BlockSpec((LANES, tile), lambda i: (0, i)), pl.BlockSpec((8, LANES), lambda i: (0, 0))],
        out_shape=[jax.ShapeDtypeStruct((tokens, 2 * LANES), BF16), jax.ShapeDtypeStruct((tokens, LANES), F32), jax.ShapeDtypeStruct((LANES, tokens), F32), jax.ShapeDtypeStruct((8, LANES), F32)],
        compiler_params=params(),
        cost_estimate=cost(2 * tokens * d_model * 512, 2 * tokens * d_model),
        name="prep",
    )(x_blk, w_bc, w_dt_rows, par)


def project(x_blk, w, first_tile, n_tiles, after):
    tokens, d_model = x_blk.shape
    tile = min(512, tokens)
    width = 256 * n_tiles
    w_specs = [pl.BlockSpec((d_model, 256), functools.partial(lambda t, i: (0, t), first_tile + t)) for t in range(n_tiles)]
    return pl.pallas_call(
        functools.partial(proj_kernel, n_tiles),
        grid=(tokens // tile,),
        in_specs=[pl.BlockSpec((tile, d_model), lambda i: (i, 0))] + w_specs + [ANY],
        out_specs=pl.BlockSpec((tile, width), lambda i: (i, 0)),
        out_shape=jax.ShapeDtypeStruct((tokens, width), BF16),
        compiler_params=params(),
        cost_estimate=cost(2 * tokens * d_model * width, 2 * tokens * d_model),
        name="project",
    )(x_blk, *([w] * n_tiles), after)


def add_products(acc, pieces, out_dtype):
    rows, d_model = acc.shape
    tile = min(512, d_model)
    n_tiles = [g.shape[1] // 256 for g, _, _ in pieces]
    specs, args = [pl.BlockSpec((rows, tile), lambda i: (0, i))], [acc]
    for (g, w, tile0), count in zip(pieces, n_tiles):
        specs.append(pl.BlockSpec(g.shape, lambda i: (0, 0)))
        specs += [pl.BlockSpec((256, tile), functools.partial(lambda t, i: (t, i), tile0 + t)) for t in range(count)]
        args += [g] + [w] * count
    return pl.pallas_call(
        functools.partial(sum_kernel, n_tiles, len(pieces)),
        grid=(d_model // tile,),
        in_specs=specs,
        out_specs=pl.BlockSpec((rows, tile), lambda i: (0, i)),
        out_shape=jax.ShapeDtypeStruct((rows, d_model), out_dtype),
        compiler_params=params(),
        cost_estimate=cost(2 * rows * d_model * 256 * sum(n_tiles), 2 * rows * d_model),
        name="add_products",
    )(*args)


def chunk_states(u, bc, cols, after, first_head, n_pairs):
    tokens, width = u.shape
    n_chunks = tokens // CHUNK
    last = n_chunks - 1
    tok = lambda w: pl.BlockSpec((CHUNK, w), lambda i: (last - i, 0))
    whole = pl.BlockSpec((LANES, width), lambda i: (0, 0))
    return pl.pallas_call(
        functools.partial(state_kernel, first_head, n_pairs),
        grid=(n_chunks,),
        in_specs=[tok(width), tok(2 * LANES), tok(LANES), ANY],
        out_specs=[pl.BlockSpec((1, LANES, width), lambda i: (last - i, 0, 0)), pl.BlockSpec((1, 8, width), lambda i: (last - i, 0, 0)), whole, whole],
        out_shape=[jax.ShapeDtypeStruct((n_chunks, LANES, width), F32), jax.ShapeDtypeStruct((n_chunks, 8, width), F32), jax.ShapeDtypeStruct((LANES, width), BF16), jax.ShapeDtypeStruct((LANES, width), BF16)],
        scratch_shapes=[pltpu.VMEM((LANES, width), F32), pltpu.VMEM((LANES, width), F32), pltpu.VMEM((8, width), F32), pltpu.VMEM((CHUNK, 2 * width), BF16)],
        compiler_params=params(),
        cost_estimate=cost(16 * tokens * width * 256, 8 * tokens * width),
        name="states",
    )(u, bc, cols, after)


def chunk_outputs(u, z, bc, cols, rows, gloc, suf, got, mix, after, first_head, n_pairs):
    tokens, width = u.shape
    n_chunks = tokens // CHUNK
    tok = lambda w: pl.BlockSpec((CHUNK, w), lambda i: (i, 0))
    state = pl.BlockSpec((LANES, width), lambda i: (0, 0))
    return pl.pallas_call(
        functools.partial(out_kernel, first_head, n_pairs),
        grid=(n_chunks,),
        in_specs=[tok(width), tok(width), tok(2 * LANES), tok(LANES), pl.BlockSpec((2 * SLOT, CHUNK), lambda i: (0, i)), pl.BlockSpec((1, LANES, width), lambda i: (i, 0, 0)), pl.BlockSpec((1, 8, width), lambda i: (i, 0, 0)), state, state, state, pl.BlockSpec((8, LANES), lambda i: (0, 0)), ANY],
        out_specs=tok(width),
        out_shape=jax.ShapeDtypeStruct((tokens, width), BF16),
        scratch_shapes=[pltpu.VMEM((LANES, width), F32), pltpu.VMEM((LANES, width), F32), pltpu.VMEM((8, width), F32), pltpu.VMEM((CHUNK, width), BF16)],
        compiler_params=params(),
        cost_estimate=cost(24 * tokens * width * 256, 8 * tokens * width),
        name="outputs",
    )(u, z, bc, cols, rows, gloc, suf, *got, mix, after)


def solution(mesh):
    n_tp, n_sp, n_dp = mesh.shape['tp'], mesh.shape['sp'], mesh.shape['dp']

    def swap(val, axis, slot):
        return lax.ppermute(val, axis, [(i, i ^ slot) for i in range(4)])

    def later(vals, after):
        return list(lax.optimization_barrier((*vals, after)))[:-1]

    def device_fn(x_blk, w_z, w_x, w_bc, w_dt, a_neg, dt_bias, d_skip, w_out):
        tokens, _ = x_blk.shape
        heads = a_neg.shape[0]
        head_dim = w_x.shape[1] // heads
        rows_out = tokens // n_tp
        tp_index = lax.axis_index('tp')
        sp_index = lax.axis_index('sp')

        piece_rows = w_out.shape[0] // (n_dp * n_sp)
        mine = lax.axis_index('dp') * n_sp + sp_index
        piece = lax.dynamic_slice_in_dim(w_out, mine * piece_rows, piece_rows, axis=0)
        right = lax.ppermute(piece, 'tp', [(0, 1), (1, 2), (2, 3)])
        left = lax.ppermute(piece, 'tp', [(1, 0), (2, 1), (3, 2)])

        w_dt_rows = jnp.pad(w_dt.T, ((0, SLOT - heads), (0, 0)))
        w_dt_rows = jnp.concatenate([w_dt_rows] * 3 + [jnp.zeros_like(w_dt_rows)], axis=0)
        spread = lambda v: jnp.concatenate([jnp.pad(v, (0, SLOT - heads))] * 4)[None, :]
        par = jnp.concatenate([spread(dt_bias), spread(a_neg), jnp.zeros((6, LANES), F32)], axis=0)
        bc, cols, rows, block_log = prep(x_blk, w_bc, w_dt_rows, par)

        logs = [swap(block_log, 'sp', s) for s in (1, 2, 3)]
        w_fwd, w_bwd = [], []
        for s in (1, 2, 3):
            peer = sp_index ^ s
            between = jnp.zeros((1, LANES), F32)
            for o in (1, 2, 3):
                other = sp_index ^ o
                inside = (other > jnp.minimum(peer, sp_index)) & (other < jnp.maximum(peer, sp_index))
                between = between + jnp.where(inside, logs[o - 1][:1], 0.0)
            decay = jnp.exp2(between)
            w_fwd.append(jnp.where(peer < sp_index, decay, 0.0))
            w_bwd.append(jnp.where(peer > sp_index, decay, 0.0))
        mix = jnp.concatenate(w_fwd + w_bwd + [spread(2.0 * d_skip), jnp.zeros((1, LANES), F32)], axis=0)

        n_tiles = w_x.shape[1] // 256
        first = n_tiles * 2 // 5
        (t_a, n_a), (t_b, n_b) = (0, first), (first, n_tiles - first)
        head_b = first * 256 // head_dim

        def exchange(s_fwd, s_bwd):
            return [swap(jnp.where(sp_index < (sp_index ^ s), s_fwd, s_bwd), 'sp', s) for s in (1, 2, 3)]

        def send(g):
            rows_of = lambda who: lax.dynamic_slice_in_dim(g, who * rows_out, rows_out, axis=0)
            return [rows_of(tp_index)] + [swap(rows_of(tp_index ^ s), 'tp', s) for s in (1, 2, 3)]

        plane = lambda v: lax.all_gather(v, ('dp', 'sp'), tiled=True)

        u_a = project(x_blk, w_x, t_a, n_a, block_log)
        gloc_a, suf_a, s_fwd, s_bwd = chunk_states(u_a, bc, cols, block_log, 0, 2 * n_a)
        got_a = exchange(s_fwd, s_bwd)
        right, left = later((right, left), s_fwd)
        one = jnp.where(tp_index % 2 == 1, right, left)
        right2 = lax.ppermute(right, 'tp', [(1, 2), (2, 3)])
        left2 = lax.ppermute(left, 'tp', [(1, 0), (2, 1)])
        w_one = plane(one)
        z_a = project(x_blk, w_z, t_a, n_a, one)
        u_b = project(x_blk, w_x, t_b, n_b, z_a)
        right2, left2 = later((right2, left2), u_b)
        two = jnp.where(tp_index >= 2, right2, left2)
        right3 = lax.ppermute(right2, 'tp', [(2, 3)])
        left3 = lax.ppermute(left2, 'tp', [(1, 0)])
        w_two = plane(two)
        g_a = chunk_outputs(u_a, z_a, bc, cols, rows, gloc_a, suf_a, got_a, mix, two, 0, 2 * n_a)
        got_g_a = send(g_a)
        gloc_b, suf_b, s_fwd, s_bwd = chunk_states(u_b, bc, cols, g_a, head_b, 2 * n_b)
        got_b = exchange(s_fwd, s_bwd)
        z_b = project(x_blk, w_z, t_b, n_b, s_fwd)
        right3, left3 = later((right3, left3), z_b)
        three = jnp.where(tp_index == 0, left3, jnp.where(tp_index == 1, left, jnp.where(tp_index == 2, right, right3)))
        w_three = plane(three)
        g_b = chunk_outputs(u_b, z_b, bc, cols, rows, gloc_b, suf_b, got_b, mix, three, head_b, 2 * n_b)
        got_g_b = send(g_b)

        own = lax.dynamic_slice_in_dim(x_blk, tp_index * rows_out, rows_out, axis=0)
        total = add_products(own, [(got_g_a[0], w_out, t_a), (got_g_b[0], w_out, t_b)], F32)
        total = add_products(total, [(got_g_a[1], w_one, t_a), (got_g_a[2], w_two, t_a)], F32)
        total = add_products(total, [(got_g_a[3], w_three, t_a), (got_g_b[1], w_one, t_b)], F32)
        return add_products(total, [(got_g_b[2], w_two, t_b), (got_g_b[3], w_three, t_b)], BF16)

    in_specs = (P(('dp', 'sp'), None), P(None, 'tp'), P(None, 'tp'), P(None, None), P(None, 'tp'), P('tp'), P('tp'), P('tp'), P('tp', None))
    out_specs = P(('dp', 'sp', 'tp'), None)
    return jax.shard_map(device_fn, mesh=mesh, in_specs=in_specs, out_specs=out_specs, check_vma=False)
```

time: 864 us -> 311 us (0.36)
  the two profiles are of different devices: /device:TPU:0 before, /device:TPU:17 now
where the time goes in v1:
time: 311 us; the launch traced here: 308 us
  Pallas kernels  171 us (55%)
  waiting for transfers between devices  72.3 us (23%)
  starting transfers between devices  29.1 us (9%)
  local copies, waits for them, and re-layouts  16.1 us (5%)
  between operations  13.4 us (4%)
  other arithmetic  6.2 us (2%)
    ppermute x15, waiting for transfers between devices, swap(): return lax.ppermute(val, axis, [(i, i ^ slot) for i in range(4)])  72.1 us
    pallas_call x4, Pallas kernels, project(): pl.pallas_call(functools.partial(proj_kernel, n_tiles), grid=(tokens // t...  45.5 us
    pallas_call x4, Pallas kernels, add_products(): pl.pallas_call(functools.partial(sum_kernel, n_tiles, len(pieces)), grid=...  40.2 us
    pallas_call x2, Pallas kernels, chunk_outputs(): pl.pallas_call(functools.partial(out_kernel, first_head, n_pairs), grid=(...  38.9 us
    pallas_call x2, Pallas kernels, chunk_states(): pl.pallas_call(functools.partial(state_kernel, first_head, n_pairs), grid...  35.5 us
    ppermute x15, starting transfers between devices, swap(): return lax.ppermute(val, axis, [(i, i ^ slot) for i in range(4)])  12.9 us
    pallas_call x1, Pallas kernels, prep(): pl.pallas_call(prep_kernel, grid=(tokens // tile,), in_specs=[pl.BlockSpe...  11.3 us
  transfers between devices with their start and end apart: 24, of which 8 were waited for; matrix products, arithmetic and copies ran while one was open for 6% of the time, Pallas kernels for 52%

profile of v1, /device:TPU:17, one launch (start us, length us, event | category | flops | bytes accessed | tf_op | source)
XLA Modules:
  0.0 308.4 jit_solution(14803056749169488288)
XLA Ops:
  6.5 2.1 constant_dynamic-slice_fusion.8
  8.6 3.2 %collective-permute-start = (bf16[160,2560]{1,0:T(8,128)(2,1)}, bf16[160,2560]{1,0:T(8,128)(2,1)S(1)}, u32[]{:S(2)}, u32[]{:S(2)}) collective-permute-start(bf16[160,2560]{1,0:T(8,128)(2,1)} %constant_dynamic-slice_fusion.8), channel_id=1, source_target_pairs={{0,4},{4,8},{8,12},{1,5},{5,9},{9,13},{2,6},{6,10},{10,14},{3,7},{... | collective-permute-start | bytes 2457608 | tf_op jit(solution)/shard_map/ppermute | solution.py:275
  11.8 2.1 collective-permute-start.1
  18.1 11.3 %prep.1 = (bf16[2048,256]{1,0:T(8,128)(2,1)}, f32[2048,128]{1,0:T(8,128)}, f32[128,2048]{1,0:T(8,128)}, f32[8,128]{1,0:T(8,128)}) custom-call(bf16[2048,2560]{1,0:T(8,128)(2,1)} %x_ref.9, bf16[2560,256]{1,0:T(8,128)(2,1)} %wbc_ref.1, bf16[128,2560]{1,0:T(8,128)(2,1)} %maximum_maximum_fusion.wdt_ref, f32[8,128]{1,0:T(8,128)} %maximum_maximum_fusion.1.par_ref), custom_call_target="tpu_custom_call" | custom-call | flops 5368709120 | bytes 10485760 | tf_op jit(solution)/shard_map/prep/pallas_call | solution.py:168
  29.4 9.9 %project.4.u_ref = bf16[2048,512]{1,0:T(8,128)(2,1)} custom-call(bf16[2048,2560]{1,0:T(8,128)(2,1)} %x_ref.9, bf16[2560,1280]{1,0:T(8,128)(2,1)} %refs_2_.3, bf16[2560,1280]{1,0:T(8,128)(2,1)} %refs_2_.3, f32[8,128]{1,0:T(8,128)} %get-tuple-element.23.refs_2_.after_ref), custom_call_target="tpu_custom_call" | custom-call | flops 5368709120 | bytes 10485760 | tf_op jit(solution)/shard_map/project/pallas_call | solution.py:185
  39.3 16.4 %states.2 = (f32[16,128,512]{2,1,0:T(8,128)}, f32[16,8,512]{2,1,0:T(8,128)}, bf16[128,512]{1,0:T(8,128)(2,1)}, bf16[128,512]{1,0:T(8,128)(2,1)}) custom-call(bf16[2048,512]{1,0:T(8,128)(2,1)} %project.4.u_ref, bf16[2048,256]{1,0:T(8,128)(2,1)} %get-tuple-element.24.bc_ref, f32[2048,128]{1,0:T(8,128)} %get-tuple-element.25.cols_ref, ...), custom_call_target="tpu_custom_call" | custom-call | flops 4294967296 | bytes 8388608 | tf_op jit(solution)/shard_map/states/pallas_call | solution.py:224
  56.8 3.2 %collective-permute-start.8 = (bf16[160,2560]{1,0:T(8,128)(2,1)S(1)}, bf16[160,2560]{1,0:T(8,128)(2,1)}, u32[]{:S(2)}, u32[]{:S(2)}) collective-permute-start(bf16[160,2560]{1,0:T(8,128)(2,1)S(1)} %collective-permute-done), channel_id=1, source_target_pairs={{4,8},{8,12},{5,9},{9,13},{6,10},{10,14},{7,11},{11,15},{20,24},{2... | collective-permute-start | bytes 2457608 | tf_op jit(solution)/shard_map/ppermute | solution.py:317
  60.1 3.8 %collective-permute-start.9 = (bf16[160,2560]{1,0:T(8,128)(2,1)S(1)}, bf16[160,2560]{1,0:T(8,128)(2,1)}, u32[]{:S(2)}, u32[]{:S(2)}) collective-permute-start(bf16[160,2560]{1,0:T(8,128)(2,1)S(1)} %collective-permute-done.1), channel_id=1, source_target_pairs={{4,0},{8,4},{5,1},{9,5},{6,2},{10,6},{7,3},{11,7},{20,16},{24,20},... | collective-permute-start | bytes 2457608 | tf_op jit(solution)/shard_map/ppermute | solution.py:318
  63.9 10.2 %project.5.refs_3_.z_ref = bf16[2048,512]{1,0:T(8,128)(2,1)} custom-call(bf16[2048,2560]{1,0:T(8,128)(2,1)} %x_ref.9, bf16[2560,1280]{1,0:T(8,128)(2,1)} %refs_2_.4, bf16[2560,1280]{1,0:T(8,128)(2,1)} %refs_2_.4, bf16[160,2560]{1,0:T(8,128)(2,1)} %broadcast_select_fusion.1.refs_2_), custom_call_target="tpu_custom_call" | custom-call | flops 5368709120 | bytes 10485760 | tf_op jit(solution)/shard_map/project/pallas_call | solution.py:185
  74.1 12.7 %project.6.u_ref = bf16[2048,768]{1,0:T(8,128)(2,1)} custom-call(bf16[2048,2560]{1,0:T(8,128)(2,1)} %x_ref.9, bf16[2560,1280]{1,0:T(8,128)(2,1)} %refs_2_.3, bf16[2560,1280]{1,0:T(8,128)(2,1)} %refs_2_.3, bf16[2560,1280]{1,0:T(8,128)(2,1)} %refs_2_.3, bf16[2048,512]{1,0:T(8,128)(2,1)} %project.5.refs_3_.z_ref), custom_call_target="tpu_custom_call" | custom-call | flops 8053063680 | bytes 10485760 | tf_op jit(solution)/shard_map/project/pallas_call | solution.py:185
  86.9 2.2 broadcast_select_fusion.after_ref
  89.2 2.5 collective-permute-start.5
  91.7 1.2 collective-permute-start.6
  97.3 2.2 collective-permute-start.13
  99.5 1.6 collective-permute-start.14
  101.9 6.4 %collective-permute-done.4.r3_ref = bf16[128,512]{1,0:T(8,128)(2,1)S(1)} collective-permute-done((bf16[128,512]{1,0:T(8,128)(2,1)S(1)}, bf16[128,512]{1,0:T(8,128)(2,1)S(1)}, u32[]{:S(2)}, u32[]{:S(2)}) %collective-permute-start.4) | collective-permute-done | bytes 131104 | tf_op jit(solution)/shard_map/ppermute | solution.py:259
  108.9 17.7 %outputs.2.after_ref = bf16[2048,512]{1,0:T(8,128)(2,1)} custom-call(bf16[2048,512]{1,0:T(8,128)(2,1)} %project.4.u_ref, bf16[2048,512]{1,0:T(8,128)(2,1)} %project.5.refs_3_.z_ref, bf16[2048,256]{1,0:T(8,128)(2,1)} %get-tuple-element.24.bc_ref, f32[2048,128]{1,0:T(8,128)} %get-tuple-element.25.cols_ref, f32[128,2048]{1,0:T(8,128)} %get-tuple-element.29.rows_ref, ...), custom_call_target="tpu_custom_call" | custom-call | flops 6442450944 | bytes 8388608 | tf_op jit(solution)/shard_map/outputs/pallas_call | solution.py:242
  126.6 19.1 %states.3 = (f32[16,128,768]{2,1,0:T(8,128)}, f32[16,8,768]{2,1,0:T(8,128)}, bf16[128,768]{1,0:T(8,128)(2,1)}, bf16[128,768]{1,0:T(8,128)(2,1)}) custom-call(bf16[2048,768]{1,0:T(8,128)(2,1)} %project.6.u_ref, bf16[2048,256]{1,0:T(8,128)(2,1)} %get-tuple-element.24.bc_ref, f32[2048,128]{1,0:T(8,128)} %get-tuple-element.25.cols_ref, ...), custom_call_target="tpu_custom_call" | custom-call | flops 6442450944 | bytes 12582912 | tf_op jit(solution)/shard_map/states/pallas_call | solution.py:224
  145.7 12.7 %project.7.z_ref = bf16[2048,768]{1,0:T(8,128)(2,1)} custom-call(bf16[2048,2560]{1,0:T(8,128)(2,1)} %x_ref.9, bf16[2560,1280]{1,0:T(8,128)(2,1)} %refs_2_.4, bf16[2560,1280]{1,0:T(8,128)(2,1)} %refs_2_.4, bf16[2560,1280]{1,0:T(8,128)(2,1)} %refs_2_.4, bf16[128,768]{1,0:T(8,128)(2,1)} %get-tuple-element.35.refs_3_), custom_call_target="tpu_custom_call" | custom-call | flops 8053063680 | bytes 10485760 | tf_op jit(solution)/shard_map/project/pallas_call | solution.py:185
  161.8 2.9 constant_dynamic-slice_fusion.3
  165.8 5.2 %collective-permute-done.12.r3_ref = bf16[128,768]{1,0:T(8,128)(2,1)S(1)} collective-permute-done((bf16[128,768]{1,0:T(8,128)(2,1)S(1)}, bf16[128,768]{1,0:T(8,128)(2,1)S(1)}, u32[]{:S(2)}, u32[]{:S(2)}) %collective-permute-start.12) | collective-permute-done | bytes 196640 | tf_op jit(solution)/shard_map/ppermute | solution.py:259
  171.7 21.1 %outputs.3 = bf16[2048,768]{1,0:T(8,128)(2,1)} custom-call(bf16[2048,768]{1,0:T(8,128)(2,1)} %project.6.u_ref, bf16[2048,768]{1,0:T(8,128)(2,1)} %project.7.z_ref, bf16[2048,256]{1,0:T(8,128)(2,1)} %get-tuple-element.24.bc_ref, f32[2048,128]{1,0:T(8,128)} %get-tuple-element.25.cols_ref, f32[128,2048]{1,0:T(8,128)} %get-tuple-element.29.rows_ref, ...), custom_call_target="tpu_custom_call" | custom-call | flops 9663676416 | bytes 12582912 | tf_op jit(solution)/shard_map/outputs/pallas_call | solution.py:242
  192.8 3.3 %constant_dynamic-slice_fusion = (bf16[512,768]{1,0:T(8,128)(2,1)S(1)}, bf16[512,768]{1,0:T(8,128)(2,1)S(1)}, bf16[512,768]{1,0:T(8,128)(2,1)}, bf16[512,768]{1,0:T(8,128)(2,1)}) fusion(bf16[2048,768]{1,0:T(8,128)(2,1)} %outputs.3, s32[]{:T(128)S(6)} %select_n.248, s32[]{:T(128)S(6)} %select_n.247, s32[]{:T(128)S(6)} %select_n.246, s32[]{:T(128)S(6)} %select_n.191), kind=kLoop, calls=%fused_computation.11 | loop fusion | bytes 6291472 | tf_op jit(solution)/shard_map/dynamic_slice | solution.py:307
  196.1 3.4 %constant_dynamic-slice_fusion.9.acc_ref = bf16[512,2560]{1,0:T(8,128)(2,1)} fusion(bf16[2048,2560]{1,0:T(8,128)(2,1)} %x_ref.9, s32[]{:T(128)S(6)} %select_n.191), kind=kLoop, calls=%fused_computation.20 | loop fusion | bytes 5242884 | tf_op jit(solution)/shard_map/dynamic_slice | solution.py:338
  199.5 3.5 %collective-permute-start.19 = (bf16[512,768]{1,0:T(8,128)(2,1)S(1)}, bf16[512,768]{1,0:T(8,128)(2,1)}, u32[]{:S(2)}, u32[]{:S(2)}) collective-permute-start(bf16[512,768]{1,0:T(8,128)(2,1)S(1)} %get-tuple-element.48), channel_id=1, source_target_pairs={{0,8},{4,12},{8,0},{12,4},{1,9},{5,13},{9,1},{13,5},{2,10},{6,14},... | collective-permute-start | bytes 2359304 | tf_op jit(solution)/shard_map/ppermute | solution.py:259
  203.1 9.6 %add_products.4.acc_ref = f32[512,2560]{1,0:T(8,128)} custom-call(bf16[512,2560]{1,0:T(8,128)(2,1)} %constant_dynamic-slice_fusion.9.acc_ref, bf16[512,512]{1,0:T(8,128)(2,1)} %get-tuple-element.54.refs_0_, bf16[1280,2560]{1,0:T(8,128)(2,1)} %refs_6_.1, bf16[1280,2560]{1,0:T(8,128)(2,1)} %refs_6_.1, bf16[512,768]{1,0:T(8,128)(2,1)} %get-tuple-element.50.refs_3_, ...), custom_call_target="tpu_custom_call" | custom-call | flops 3355443200 | bytes 2621440 | tf_op jit(solution)/shard_map/add_products/pallas_call | solution.py:206
  212.8 10.1 %add_products.5.acc_ref = f32[512,2560]{1,0:T(8,128)} custom-call(f32[512,2560]{1,0:T(8,128)} %add_products.4.acc_ref, bf16[512,512]{1,0:T(8,128)(2,1)} %collective-permute-done.15.refs_0_, bf16[1280,2560]{1,0:T(8,128)(2,1)} %all-gather.4.cloned.1.call-done.refs_1_.refs_2_.refs_4_.refs_5_.refs_6_, ...), custom_call_target="tpu_custom_call" | custom-call | flops 2684354560 | bytes 2621440 | tf_op jit(solution)/shard_map/add_products/pallas_call | solution.py:206
  222.9 3.2 %collective-permute-done.18.refs_3_ = bf16[512,768]{1,0:T(8,128)(2,1)} collective-permute-done((bf16[512,768]{1,0:T(8,128)(2,1)}, bf16[512,768]{1,0:T(8,128)(2,1)}, u32[]{:S(2)}, u32[]{:S(2)}) %collective-permute-start.18) | collective-permute-done | bytes 786464 | tf_op jit(solution)/shard_map/ppermute | solution.py:259
  226.1 10.5 %add_products.6.acc_ref = f32[512,2560]{1,0:T(8,128)} custom-call(f32[512,2560]{1,0:T(8,128)} %add_products.5.acc_ref, bf16[512,512]{1,0:T(8,128)(2,1)} %collective-permute-done.17.refs_0_, bf16[1280,2560]{1,0:T(8,128)(2,1)} %all-gather.8.cloned.1.call-done.refs_1_.refs_2_.refs_5_.refs_6_.refs_7_, ...), custom_call_target="tpu_custom_call" | custom-call | flops 3355443200 | bytes 2621440 | tf_op jit(solution)/shard_map/add_products/pallas_call | solution.py:206
  236.6 36.7 %collective-permute-done.19.refs_0_ = bf16[512,768]{1,0:T(8,128)(2,1)} collective-permute-done((bf16[512,768]{1,0:T(8,128)(2,1)S(1)}, bf16[512,768]{1,0:T(8,128)(2,1)}, u32[]{:S(2)}, u32[]{:S(2)}) %collective-permute-start.19) | collective-permute-done | bytes 786464 | tf_op jit(solution)/shard_map/ppermute | solution.py:259
  273.3 18.6 %collective-permute-done.20.refs_4_ = bf16[512,768]{1,0:T(8,128)(2,1)} collective-permute-done((bf16[512,768]{1,0:T(8,128)(2,1)S(1)}, bf16[512,768]{1,0:T(8,128)(2,1)}, u32[]{:S(2)}, u32[]{:S(2)}) %collective-permute-start.20) | collective-permute-done | bytes 786464 | tf_op jit(solution)/shard_map/ppermute | solution.py:259
  291.9 10.0 %add_products.7 = bf16[512,2560]{1,0:T(8,128)(2,1)} custom-call(f32[512,2560]{1,0:T(8,128)} %add_products.6.acc_ref, bf16[512,768]{1,0:T(8,128)(2,1)} %collective-permute-done.19.refs_0_, bf16[1280,2560]{1,0:T(8,128)(2,1)} %all-gather.6.cloned.1.call-done.refs_4_.refs_5_.refs_1_.refs_2_.refs_3_, ...), custom_call_target="tpu_custom_call" | custom-call | flops 4026531840 | bytes 2621440 | tf_op jit(solution)/shard_map/add_products/pallas_call | solution.py:206
  (85 shorter events, 16.1 us)
Async XLA Ops:
  6.5 206.2 %all-gather.4.cloned.1.call-start = ((), (), s32[]{:S(2)}) async-start(), calls=%async_computation | async-start | bytes 7372800 | tf_op jit(solution)/shard_map/all_gather | solution.py:310
  8.6 47.1 %collective-permute-start = (bf16[160,2560]{1,0:T(8,128)(2,1)}, bf16[160,2560]{1,0:T(8,128)(2,1)S(1)}, u32[]{:S(2)}, u32[]{:S(2)}) collective-permute-start(bf16[160,2560]{1,0:T(8,128)(2,1)} %constant_dynamic-slice_fusion.8), channel_id=1, source_target_pairs={{0,4},{4,8},{8,12},{1,5},{5,9},{9,13},{2,6},{6,10},{10,14},{3,7},{... | collective-permute-start | bytes 2457608 | tf_op jit(solution)/shard_map/ppermute | solution.py:275
  11.8 43.9 %collective-permute-start.1 = (bf16[160,2560]{1,0:T(8,128)(2,1)}, bf16[160,2560]{1,0:T(8,128)(2,1)S(1)}, u32[]{:S(2)}, u32[]{:S(2)}) collective-permute-start(bf16[160,2560]{1,0:T(8,128)(2,1)} %constant_dynamic-slice_fusion.8), channel_id=1, source_target_pairs={{4,0},{8,4},{12,8},{5,1},{9,5},{13,9},{6,2},{10,6},{14,10},{7,3},{... | collective-permute-start | bytes 2457608 | tf_op jit(solution)/shard_map/ppermute | solution.py:276
  56.8 156.0 %all-gather.6.cloned.1.call-start = ((), (), s32[]{:S(2)}) async-start(), calls=%async_computation.1 | async-start | bytes 7372800 | tf_op jit(solution)/shard_map/all_gather | solution.py:310
  56.8 30.0 %collective-permute-start.8 = (bf16[160,2560]{1,0:T(8,128)(2,1)S(1)}, bf16[160,2560]{1,0:T(8,128)(2,1)}, u32[]{:S(2)}, u32[]{:S(2)}) collective-permute-start(bf16[160,2560]{1,0:T(8,128)(2,1)S(1)} %collective-permute-done), channel_id=1, source_target_pairs={{4,8},{8,12},{5,9},{9,13},{6,10},{10,14},{7,11},{11,15},{20,24},{2... | collective-permute-start | bytes 2457608 | tf_op jit(solution)/shard_map/ppermute | solution.py:317
  60.1 26.8 %collective-permute-start.9 = (bf16[160,2560]{1,0:T(8,128)(2,1)S(1)}, bf16[160,2560]{1,0:T(8,128)(2,1)}, u32[]{:S(2)}, u32[]{:S(2)}) collective-permute-start(bf16[160,2560]{1,0:T(8,128)(2,1)S(1)} %collective-permute-done.1), channel_id=1, source_target_pairs={{4,0},{8,4},{5,1},{9,5},{6,2},{10,6},{7,3},{11,7},{20,16},{24,20},... | collective-permute-start | bytes 2457608 | tf_op jit(solution)/shard_map/ppermute | solution.py:318
  86.8 2.3 copy-start.4
  86.8 6.6 %copy-start.2 = (bf16[128,512]{1,0:T(8,128)(2,1)S(1)}, bf16[128,512]{1,0:T(8,128)(2,1)}, u32[]{:S(2)}) copy-start(bf16[128,512]{1,0:T(8,128)(2,1)} %get-tuple-element.26) | copy-start | bytes 393220
  86.8 6.6 %copy-start.3 = (bf16[128,512]{1,0:T(8,128)(2,1)S(1)}, bf16[128,512]{1,0:T(8,128)(2,1)}, u32[]{:S(2)}) copy-start(bf16[128,512]{1,0:T(8,128)(2,1)} %get-tuple-element.32) | copy-start | bytes 393220
  86.8 8.1 %copy-start.11 = (f32[20]{0:T(128)S(1)}, f32[20]{0:T(128)}, u32[]{:S(2)}) copy-start(f32[20]{0:T(128)} %param.16) | copy-start | bytes 244
  89.1 137.0 %all-gather.8.cloned.1.call-start = ((), (), s32[]{:S(2)}) async-start(), calls=%async_computation.2 | async-start | bytes 7372800 | tf_op jit(solution)/shard_map/all_gather | solution.py:310
  89.2 5.9 %collective-permute-start.5 = (f32[8,128]{1,0:T(8,128)S(1)}, f32[8,128]{1,0:T(8,128)S(1)}, u32[]{:S(2)}, u32[]{:S(2)}) collective-permute-start(f32[8,128]{1,0:T(8,128)S(1)} %copy-done.4), channel_id=1, source_target_pairs={{0,1},{1,0},{2,3},{3,2},{4,5},{5,4},{6,7},{7,6},{8,9},{9,8},{10,11... | collective-permute-start | bytes 12296 | tf_op jit(solution)/shard_map/ppermute | solution.py:259
  91.7 4.1 %collective-permute-start.6 = (f32[8,128]{1,0:T(8,128)S(1)}, f32[8,128]{1,0:T(8,128)S(1)}, u32[]{:S(2)}, u32[]{:S(2)}) collective-permute-start(f32[8,128]{1,0:T(8,128)S(1)} %copy-done.4), channel_id=1, source_target_pairs={{0,2},{1,3},{2,0},{3,1},{4,6},{5,7},{6,4},{7,5},{8,10},{9,11},{10,... | collective-permute-start | bytes 12296 | tf_op jit(solution)/shard_map/ppermute | solution.py:259
  92.9 3.7 %collective-permute-start.7 = (f32[8,128]{1,0:T(8,128)S(1)}, f32[8,128]{1,0:T(8,128)S(1)}, u32[]{:S(2)}, u32[]{:S(2)}) collective-permute-start(f32[8,128]{1,0:T(8,128)S(1)} %copy-done.4), channel_id=1, source_target_pairs={{0,3},{1,2},{2,1},{3,0},{4,7},{5,6},{6,5},{7,4},{8,11},{9,10},{10,... | collective-permute-start | bytes 12296 | tf_op jit(solution)/shard_map/ppermute | solution.py:259
  93.4 7.7 %collective-permute-start.2 = (bf16[128,512]{1,0:T(8,128)(2,1)S(1)}, bf16[128,512]{1,0:T(8,128)(2,1)S(1)}, u32[]{:S(2)}, u32[]{:S(2)}) collective-permute-start(bf16[128,512]{1,0:T(8,128)(2,1)S(1)} %get-tuple-element.60), channel_id=1, source_target_pairs={{0,1},{1,0},{2,3},{3,2},{4,5},{5,4},{6,7},{7,6},{8,9},{9,8},{10,11... | collective-permute-start | bytes 393224 | tf_op jit(solution)/shard_map/ppermute | solution.py:259
  93.7 8.2 %collective-permute-start.3 = (bf16[128,512]{1,0:T(8,128)(2,1)S(1)}, bf16[128,512]{1,0:T(8,128)(2,1)S(1)}, u32[]{:S(2)}, u32[]{:S(2)}) collective-permute-start(bf16[128,512]{1,0:T(8,128)(2,1)S(1)} %get-tuple-element.59), channel_id=1, source_target_pairs={{0,2},{1,3},{2,0},{3,1},{4,6},{5,7},{6,4},{7,5},{8,10},{9,11},{10,... | collective-permute-start | bytes 393224 | tf_op jit(solution)/shard_map/ppermute | solution.py:259
  95.0 13.2 %collective-permute-start.4 = (bf16[128,512]{1,0:T(8,128)(2,1)S(1)}, bf16[128,512]{1,0:T(8,128)(2,1)S(1)}, u32[]{:S(2)}, u32[]{:S(2)}) collective-permute-start(bf16[128,512]{1,0:T(8,128)(2,1)S(1)} %get-tuple-element.58), channel_id=1, source_target_pairs={{0,3},{1,2},{2,1},{3,0},{4,7},{5,6},{6,5},{7,4},{8,11},{9,10},{10,... | collective-permute-start | bytes 393224 | tf_op jit(solution)/shard_map/ppermute | solution.py:259
  97.3 61.1 %collective-permute-start.13 = (bf16[160,2560]{1,0:T(8,128)(2,1)}, bf16[160,2560]{1,0:T(8,128)(2,1)}, u32[]{:S(2)}, u32[]{:S(2)}) collective-permute-start(bf16[160,2560]{1,0:T(8,128)(2,1)} %collective-permute-done.8), channel_id=1, source_target_pairs={{8,12},{9,13},{10,14},{11,15},{24,28},{25,29},{26,30},{27,31}} | collective-permute-start | bytes 2457608 | tf_op jit(solution)/shard_map/ppermute | solution.py:324
  99.5 58.9 %collective-permute-start.14 = (bf16[160,2560]{1,0:T(8,128)(2,1)}, bf16[160,2560]{1,0:T(8,128)(2,1)}, u32[]{:S(2)}, u32[]{:S(2)}) collective-permute-start(bf16[160,2560]{1,0:T(8,128)(2,1)} %collective-permute-done.9), channel_id=1, source_target_pairs={{4,0},{5,1},{6,2},{7,3},{20,16},{21,17},{22,18},{23,19}} | collective-permute-start | bytes 2457608 | tf_op jit(solution)/shard_map/ppermute | solution.py:325
  101.1 7.2 %copy-start.8 = (bf16[128,512]{1,0:T(8,128)(2,1)}, bf16[128,512]{1,0:T(8,128)(2,1)S(1)}, u32[]{:S(2)}) copy-start(bf16[128,512]{1,0:T(8,128)(2,1)S(1)} %collective-permute-done.2.r1_ref) | copy-start | bytes 393220
  101.8 6.4 %copy-start.9 = (bf16[128,512]{1,0:T(8,128)(2,1)}, bf16[128,512]{1,0:T(8,128)(2,1)S(1)}, u32[]{:S(2)}) copy-start(bf16[128,512]{1,0:T(8,128)(2,1)S(1)} %collective-permute-done.3.r2_ref) | copy-start | bytes 393220
  159.6 5.7 %collective-permute-start.10 = (bf16[128,768]{1,0:T(8,128)(2,1)S(1)}, bf16[128,768]{1,0:T(8,128)(2,1)S(1)}, u32[]{:S(2)}, u32[]{:S(2)}) collective-permute-start(bf16[128,768]{1,0:T(8,128)(2,1)S(1)} %get-tuple-element.57), channel_id=1, source_target_pairs={{0,1},{1,0},{2,3},{3,2},{4,5},{5,4},{6,7},{7,6},{8,9},{9,8},{10,11... | collective-permute-start | bytes 589832 | tf_op jit(solution)/shard_map/ppermute | solution.py:259
  159.7 6.1 %collective-permute-start.11 = (bf16[128,768]{1,0:T(8,128)(2,1)S(1)}, bf16[128,768]{1,0:T(8,128)(2,1)S(1)}, u32[]{:S(2)}, u32[]{:S(2)}) collective-permute-start(bf16[128,768]{1,0:T(8,128)(2,1)S(1)} %get-tuple-element.56), channel_id=1, source_target_pairs={{0,2},{1,3},{2,0},{3,1},{4,6},{5,7},{6,4},{7,5},{8,10},{9,11},{10,... | collective-permute-start | bytes 589832 | tf_op jit(solution)/shard_map/ppermute | solution.py:259
  160.9 10.1 %collective-permute-start.12 = (bf16[128,768]{1,0:T(8,128)(2,1)S(1)}, bf16[128,768]{1,0:T(8,128)(2,1)S(1)}, u32[]{:S(2)}, u32[]{:S(2)}) collective-permute-start(bf16[128,768]{1,0:T(8,128)(2,1)S(1)} %get-tuple-element.55), channel_id=1, source_target_pairs={{0,3},{1,2},{2,1},{3,0},{4,7},{5,6},{6,5},{7,4},{8,11},{9,10},{10,... | collective-permute-start | bytes 589832 | tf_op jit(solution)/shard_map/ppermute | solution.py:259
  164.7 38.4 %collective-permute-start.15 = (bf16[512,512]{1,0:T(8,128)(2,1)}, bf16[512,512]{1,0:T(8,128)(2,1)}, u32[]{:S(2)}, u32[]{:S(2)}) collective-permute-start(bf16[512,512]{1,0:T(8,128)(2,1)} %get-tuple-element.53), channel_id=1, source_target_pairs={{0,4},{4,0},{8,12},{12,8},{1,5},{5,1},{9,13},{13,9},{2,6},{6,2},{1... | collective-permute-start | bytes 1572872 | tf_op jit(solution)/shard_map/ppermute | solution.py:259
  164.7 48.0 %collective-permute-start.16 = (bf16[512,512]{1,0:T(8,128)(2,1)}, bf16[512,512]{1,0:T(8,128)(2,1)}, u32[]{:S(2)}, u32[]{:S(2)}) collective-permute-start(bf16[512,512]{1,0:T(8,128)(2,1)} %get-tuple-element.52), channel_id=1, source_target_pairs={{0,8},{4,12},{8,0},{12,4},{1,9},{5,13},{9,1},{13,5},{2,10},{6,14},... | collective-permute-start | bytes 1572872 | tf_op jit(solution)/shard_map/ppermute | solution.py:259
  165.3 5.6 %copy-start.5 = (bf16[128,768]{1,0:T(8,128)(2,1)}, bf16[128,768]{1,0:T(8,128)(2,1)S(1)}, u32[]{:S(2)}) copy-start(bf16[128,768]{1,0:T(8,128)(2,1)S(1)} %collective-permute-done.10.r1_ref) | copy-start | bytes 589828
  165.8 5.2 %copy-start.6 = (bf16[128,768]{1,0:T(8,128)(2,1)}, bf16[128,768]{1,0:T(8,128)(2,1)S(1)}, u32[]{:S(2)}) copy-start(bf16[128,768]{1,0:T(8,128)(2,1)S(1)} %collective-permute-done.11.r2_ref) | copy-start | bytes 589828
  196.1 30.0 %collective-permute-start.18 = (bf16[512,768]{1,0:T(8,128)(2,1)}, bf16[512,768]{1,0:T(8,128)(2,1)}, u32[]{:S(2)}, u32[]{:S(2)}) collective-permute-start(bf16[512,768]{1,0:T(8,128)(2,1)} %get-tuple-element.49), channel_id=1, source_target_pairs={{0,4},{4,0},{8,12},{12,8},{1,5},{5,1},{9,13},{13,9},{2,6},{6,2},{1... | collective-permute-start | bytes 2359304 | tf_op jit(solution)/shard_map/ppermute | solution.py:259
  199.5 23.3 %collective-permute-start.17 = (bf16[512,512]{1,0:T(8,128)(2,1)}, bf16[512,512]{1,0:T(8,128)(2,1)}, u32[]{:S(2)}, u32[]{:S(2)}) collective-permute-start(bf16[512,512]{1,0:T(8,128)(2,1)} %get-tuple-element.51), channel_id=1, source_target_pairs={{0,12},{4,8},{8,4},{12,0},{1,13},{5,9},{9,5},{13,1},{2,14},{6,10},... | collective-permute-start | bytes 1572872 | tf_op jit(solution)/shard_map/ppermute | solution.py:259
  199.5 73.8 %collective-permute-start.19 = (bf16[512,768]{1,0:T(8,128)(2,1)S(1)}, bf16[512,768]{1,0:T(8,128)(2,1)}, u32[]{:S(2)}, u32[]{:S(2)}) collective-permute-start(bf16[512,768]{1,0:T(8,128)(2,1)S(1)} %get-tuple-element.48), channel_id=1, source_target_pairs={{0,8},{4,12},{8,0},{12,4},{1,9},{5,13},{9,1},{13,5},{2,10},{6,14},... | collective-permute-start | bytes 2359304 | tf_op jit(solution)/shard_map/ppermute | solution.py:259
  203.1 88.8 %collective-permute-start.20 = (bf16[512,768]{1,0:T(8,128)(2,1)S(1)}, bf16[512,768]{1,0:T(8,128)(2,1)}, u32[]{:S(2)}, u32[]{:S(2)}) collective-permute-start(bf16[512,768]{1,0:T(8,128)(2,1)S(1)} %get-tuple-element.47), channel_id=1, source_target_pairs={{0,12},{4,8},{8,4},{12,0},{1,13},{5,9},{9,5},{13,1},{2,14},{6,10},... | collective-permute-start | bytes 2359304 | tf_op jit(solution)/shard_map/ppermute | solution.py:259
  (4 other events, 3.5 us)
Sparse Core Ops, SparseCore 0:
  56.9 54.3 all-gather.3
  113.2 46.4 all-gather.5
  161.6 46.4 all-gather.7

commit v2 on v1

v2 whole, which is shorter than its diff:
```python
import functools

import jax
import jax.numpy as jnp
from jax import lax
from jax.experimental import pallas as pl
from jax.experimental.pallas import tpu as pltpu
from jax.sharding import PartitionSpec as P


CHUNK = 128
LANES = 128
SLOT = 32
STATE_CHUNKS = 4
OUT_CHUNKS = 2
OUT_AHEAD = 2
F32 = jnp.float32
BF16 = jnp.bfloat16


def split3(val, lane, last):
    first = val.astype(BF16).astype(F32)
    rest = val - first
    second = rest.astype(BF16).astype(F32)
    third = rest - second
    return jnp.where(lane < SLOT, first, jnp.where(lane < 2 * SLOT, second, jnp.where(lane < 3 * SLOT, third, last))).astype(BF16)


def prep_kernel(n_tiles, x_ref, wbc_ref, wdt_ref, bias_ref, a_ref, *refs):
    bc_ref, cum_ref, nexc_ref, dt_ref, tail1_ref, tail2_ref, log_ref, u_ref, w_buf, par, pick = refs[n_tiles:]
    heads = bias_ref.shape[1]
    row = lax.broadcasted_iota(jnp.int32, (CHUNK, LANES), 0)
    lane = lax.broadcasted_iota(jnp.int32, (CHUNK, LANES), 1)

    @pl.when(pl.program_id(0) == 0)
    def _():
        log_ref[...] = jnp.zeros_like(log_ref)
        w_buf[...] = jnp.zeros_like(w_buf)
        par[...] = jnp.zeros_like(par)
        for k in range(3):
            w_buf[k * SLOT:k * SLOT + heads, :] = wdt_ref[...]
            par[0:1, k * SLOT:k * SLOT + heads] = bias_ref[...]
            par[1:2, k * SLOT:k * SLOT + heads] = a_ref[...]
        out_row = lax.broadcasted_iota(jnp.int32, pick.shape, 0)
        term = lax.broadcasted_iota(jnp.int32, pick.shape, 1)
        head, which = out_row // 16, out_row % 16
        pick[...] = jnp.where((which < 3) & (term == which * SLOT + head), -1.0, 0.0).astype(BF16)

    x_val = x_ref[...]
    raw = lax.dot_general(x_val, w_buf[...], (((1,), (1,)), ((), ())), preferred_element_type=F32) + par[0:1, :]
    bc_ref[...] = jnp.dot(x_val, wbc_ref[...], preferred_element_type=F32).astype(BF16)
    dt_val = jnp.maximum(raw, 0.0) + jnp.log1p(jnp.exp(-jnp.abs(raw)))
    la_val = jnp.maximum(dt_val * par[1:2, :], -1000.0)
    tri = jnp.where(row >= lane, 1.0, 0.0).astype(BF16)
    for c in range(x_val.shape[0] // CHUNK):
        part = slice(c * CHUNK, (c + 1) * CHUNK)
        la_c = la_val[part, :]
        first = la_c.astype(BF16)
        rest = la_c - first.astype(F32)
        second = rest.astype(BF16)
        third = (rest - second.astype(F32)).astype(BF16)
        cum = sum(jnp.dot(tri, t, preferred_element_type=F32) for t in (first, second, third))
        one = jnp.where(lane < 3 * SLOT + 3, 1.0, 0.0)
        cum3 = split3(cum, lane, one)
        nexc3 = split3(la_c - cum, lane, one)
        cum_ref[part, :] = cum3
        nexc_ref[part, :] = nexc3
        dt_ref[part, :] = split3(dt_val[part, :], lane, 0.0)
        across = (((1,), (1,)), ((), ()))
        tail1_ref[:, part] = lax.dot_general(pick[...], cum3, across, preferred_element_type=F32).astype(BF16)
        tail2_ref[:, part] = lax.dot_general(pick[...], nexc3, across, preferred_element_type=F32).astype(BF16)
        log_ref[...] += cum[CHUNK - 1:CHUNK, :]
    for i in range(n_tiles):
        u_ref[:, i * 256:(i + 1) * 256] = jnp.dot(x_val, refs[i][...], preferred_element_type=F32).astype(BF16)


def proj_kernel(counts, x_ref, *refs):
    x_val = x_ref[...]
    o_refs = refs[sum(counts) + 1:]
    k = 0
    for o_ref, count in zip(o_refs, counts):
        for i in range(count):
            o_ref[:, i * 256:(i + 1) * 256] = jnp.dot(x_val, refs[k][...], preferred_element_type=F32).astype(BF16)
            k += 1


def sum_kernel(n_tiles, n_pieces, acc_ref, *refs):
    o_ref = refs[-1]
    total = acc_ref[...].astype(F32)
    for i in range(n_pieces):
        g_ref, w_refs = refs[sum(n_tiles[:i]) + i], refs[sum(n_tiles[:i]) + i + 1:sum(n_tiles[:i + 1]) + i + 1]
        for t in range(n_tiles[i]):
            total = total + jnp.dot(g_ref[:, t * 256:(t + 1) * 256], w_refs[t][...], preferred_element_type=F32)
    o_ref[...] = total.astype(o_ref.dtype)


def spread_matrix(shape, first_head, lanes_per_head):
    term = lax.broadcasted_iota(jnp.int32, shape, 0)
    lane = lax.broadcasted_iota(jnp.int32, shape, 1)
    return jnp.where((term % SLOT == first_head + lane // lanes_per_head) & (term < 3 * SLOT), 1.0, 0.0).astype(BF16)


def pair_cols(cols, head, low):
    return jnp.where(low, jnp.broadcast_to(cols[:, head:head + 1], low.shape), jnp.broadcast_to(cols[:, head + 1:head + 2], low.shape))


def state_kernel(first_head, n_pairs, u_ref, bc_ref, cum_ref, nexc_ref, dt_ref, gloc_ref, suf_ref, sf_ref, sb_ref, ut_ref, vf_ref, g_acc, f_acc, suf_acc, v_buf, spread):
    step = pl.program_id(0)
    width = n_pairs * LANES

    @pl.when(step == 0)
    def _():
        g_acc[...] = jnp.zeros_like(g_acc)
        f_acc[...] = jnp.zeros_like(f_acc)
        suf_acc[...] = jnp.zeros_like(suf_acc)
        spread[...] = spread_matrix(spread.shape, first_head, LANES // 2)

    def terms_of(c, p):
        rows = slice(c * CHUNK, (c + 1) * CHUNK)
        wide = slice(p * LANES, min(p + 2, n_pairs) * LANES)
        return [jnp.dot(r[rows, :], spread[:, wide], preferred_element_type=F32) for r in (cum_ref, nexc_ref, dt_ref)]

    def finish(c, total):
        rows = slice(c * CHUNK, (c + 1) * CHUNK)
        suffix = suf_acc[...]
        suf_ref[c, 0:1, :] = suffix[0:1, :]
        suf_ref[c, 1:2, :] = total
        sums = lax.dot_general(bc_ref[rows, :LANES], v_buf[rows, :], (((0,), (0,)), ((), ())), preferred_element_type=F32)
        back = g_acc[...]
        gloc_ref[c] = back
        g_acc[...] = back * jnp.exp(total) + sums[:, :width]
        f_acc[...] += sums[:, width:] * jnp.exp(suffix[0:1, :])
        suf_acc[...] = suffix + total

    order = [(c, p) for c in reversed(range(STATE_CHUNKS)) for p in range(0, n_pairs, 2)]
    ahead = terms_of(*order[0])
    for i, (c, p0) in enumerate(order):
        terms = ahead
        if i + 1 < len(order):
            ahead = terms_of(*order[i + 1])
        rows = slice(c * CHUNK, (c + 1) * CHUNK)
        if p0 == 0:
            totals = []
        for p in range(p0, min(p0 + 2, n_pairs)):
            part = slice(p * LANES, (p + 1) * LANES)
            half = slice((p - p0) * LANES, (p - p0 + 1) * LANES)
            cum, nexc, dt_val = [t[:, half] for t in terms]
            scaled = u_ref[rows, part].astype(F32) * dt_val
            total = cum[CHUNK - 1:CHUNK, :]
            totals.append(total)
            ut_ref[rows, part] = scaled.astype(BF16)
            v_buf[rows, part] = (scaled * jnp.exp(-nexc)).astype(BF16)
            end = (scaled * jnp.exp(total - cum)).astype(BF16)
            vf_ref[rows, part] = end
            v_buf[rows, slice(width + p * LANES, width + (p + 1) * LANES)] = end
        if p0 + 2 >= n_pairs:
            finish(c, jnp.concatenate(totals, axis=1))

    @pl.when(step == pl.num_programs(0) - 1)
    def _():
        sf_ref[...] = f_acc[...].astype(BF16)
        sb_ref[...] = g_acc[...].astype(BF16)


def peer_weights(sp_index, logs):
    fwd, bwd = [], []
    for s in (1, 2, 3):
        peer = sp_index ^ s
        between = jnp.zeros_like(logs[0])
        for o in (1, 2, 3):
            other = sp_index ^ o
            inside = (other > jnp.minimum(peer, sp_index)) & (other < jnp.maximum(peer, sp_index))
            between = between + jnp.where(inside, logs[o - 1], 0.0)
        decay = jnp.exp(between)
        fwd.append(jnp.where(peer < sp_index, decay, 0.0))
        bwd.append(jnp.where(peer > sp_index, decay, 0.0))
    return fwd, bwd


def out_kernel(first_head, n_pairs, who_ref, u_ref, z_ref, ut_ref, vf_ref, bc_ref, cum_ref, nexc_ref, tail1_ref, tail2_ref, gloc_ref, suf_ref, r1_ref, r2_ref, r3_ref, l1_ref, l2_ref, l3_ref, skip_ref, after_ref, o0_ref, o1_ref, o2_ref, o3_ref, f_acc, hb_acc, skip_buf, g_buf, spread, pick, fwd_buf, bwd_buf):
    step = pl.program_id(0)

    @pl.when(step == 0)
    def _():
        low8 = lax.broadcasted_iota(jnp.int32, (8, LANES), 1) < LANES // 2
        fwd, bwd = peer_weights(who_ref[1], [r[...] for r in (l1_ref, l2_ref, l3_ref)])
        got = (r1_ref, r2_ref, r3_ref)
        spread[...] = spread_matrix(spread.shape, first_head, LANES // 2)
        pick[...] = spread_matrix(pick.shape, first_head, LANES)
        for p in range(n_pairs):
            part = slice(p * LANES, (p + 1) * LANES)
            over = lambda v: pair_cols(v, first_head + 2 * p, low8)
            skip_buf[:, part] = 2.0 * over(jnp.broadcast_to(skip_ref[...], (8, skip_ref.shape[1])))
            f_acc[:, part] = sum(got[s][:, part].astype(F32) * over(fwd[s])[0:1, :] for s in range(3))
            hb_acc[:, part] = sum(got[s][:, part].astype(F32) * over(bwd[s])[0:1, :] for s in range(3))

    row = lax.broadcasted_iota(jnp.int32, (CHUNK, LANES), 0)
    lane = lax.broadcasted_iota(jnp.int32, (CHUNK, LANES), 1)
    low = lane < LANES // 2
    zeros = jnp.zeros((16, 2 * LANES), BF16)
    grams = []
    for c in range(OUT_CHUNKS):
        rows = slice(c * CHUNK, (c + 1) * CHUNK)
        b_val = bc_ref[rows, :LANES]
        gram = lax.dot_general(bc_ref[rows, LANES:], b_val, (((1,), (1,)), ((), ())), preferred_element_type=F32)
        grams.append(jnp.where(row == lane, 2.0 * gram, gram))
        sums = lax.dot_general(b_val, vf_ref[rows, :], (((0,), (0,)), ((), ())), preferred_element_type=F32)
        state = f_acc[...]
        fwd_buf[c] = state.astype(BF16)
        bwd_buf[c] = (gloc_ref[c] + hb_acc[...] * jnp.exp(suf_ref[c, 0:1, :])).astype(BF16)
        f_acc[...] = state * jnp.exp(suf_ref[c, 1:2, :]) + sums

    def weights(c, p):
        rows = slice(c * CHUNK, (c + 1) * CHUNK)
        head = first_head + 2 * p

        def differences(terms_ref, tail_ref):
            tails = jnp.concatenate([tail_ref[16 * h:16 * h + 16, rows] for h in (head, head + 1)], axis=1)
            chosen = pick[0:3 * SLOT, slice(2 * p * LANES, 2 * (p + 1) * LANES)]
            return jnp.dot(terms_ref[rows, :], jnp.concatenate([chosen, tails, zeros], axis=0), preferred_element_type=F32)

        decay = jnp.exp(jnp.minimum(differences(cum_ref, tail1_ref), differences(nexc_ref, tail2_ref)))
        return jnp.concatenate([(decay[:, :LANES] * grams[c]).astype(BF16), (decay[:, LANES:] * grams[c]).astype(BF16)], axis=1)

    def passed(c, p):
        rows = slice(c * CHUNK, (c + 1) * CHUNK)
        part = slice(p * LANES, (p + 1) * LANES)
        c_val = bc_ref[rows, LANES:]
        cum = jnp.dot(cum_ref[rows, :], spread[:, part], preferred_element_type=F32)
        nexc = jnp.dot(nexc_ref[rows, :], spread[:, part], preferred_element_type=F32)
        y_fwd = jnp.dot(c_val, fwd_buf[c, :, part], preferred_element_type=F32)
        y_bwd = jnp.dot(c_val, bwd_buf[c, :, part], preferred_element_type=F32)
        y_val = jnp.exp(cum) * y_fwd + jnp.exp(suf_ref[c, 1:2, part] + nexc) * y_bwd
        return y_val + skip_buf[0:1, part] * u_ref[rows, part].astype(F32)

    order = [(c, p) for c in range(OUT_CHUNKS) for p in range(n_pairs)]
    ahead = [weights(*order[i]) for i in range(OUT_AHEAD)]
    for i, (c, p) in enumerate(order):
        mix = ahead.pop(0)
        if i + OUT_AHEAD < len(order):
            ahead.append(weights(*order[i + OUT_AHEAD]))
        y_val = passed(c, p)
        rows = slice(c * CHUNK, (c + 1) * CHUNK)
        part = slice(p * LANES, (p + 1) * LANES)
        scaled = ut_ref[rows, part]
        none = jnp.zeros_like(scaled)
        rhs = jnp.concatenate([jnp.where(low, scaled, none), jnp.where(low, none, scaled)], axis=0)
        y_val = jnp.dot(mix, rhs, preferred_element_type=F32) + y_val
        z_val = z_ref[rows, part].astype(F32)
        g_buf[rows, part] = (y_val * (z_val * jax.nn.sigmoid(z_val))).astype(BF16)

    steps = pl.num_programs(0) // 4
    slot = (step // steps) ^ who_ref[0]
    length = OUT_CHUNKS * CHUNK
    for s, o_ref in enumerate((o0_ref, o1_ref, o2_ref, o3_ref)):
        @pl.when(slot == s)
        def _():
            o_ref[pl.ds(pl.multiple_of((step % steps) * length, length), length), :] = g_buf[...]


def params():
    return pltpu.CompilerParams(dimension_semantics=("arbitrary",), vmem_limit_bytes=62 << 20)


def cost(flops, moved):
    return pl.CostEstimate(flops=int(flops), bytes_accessed=int(moved), transcendentals=0)


ANY = pl.BlockSpec(memory_space=pl.ANY)


def w_specs(w, first_tile, n_tiles):
    return [pl.BlockSpec((w.shape[0], 256), functools.partial(lambda t, i: (0, t), first_tile + t), pipeline_mode=pl.Buffered(1)) for t in range(n_tiles)]


def prep(x_blk, w_bc, w_dt_rows, bias, a_neg, w_x, n_tiles):
    tokens, d_model = x_blk.shape
    tile = min(512, tokens)
    width = 256 * n_tiles
    whole = lambda a: pl.BlockSpec(a.shape, lambda i: (0, 0), pipeline_mode=pl.Buffered(1))
    tok = lambda w: pl.BlockSpec((tile, w), lambda i: (i, 0))
    heads = bias.shape[1]
    tail = pl.BlockSpec((16 * heads, tile), lambda i: (0, i))
    return pl.pallas_call(
        functools.partial(prep_kernel, n_tiles),
        grid=(tokens // tile,),
        in_specs=[tok(d_model), whole(w_bc), whole(w_dt_rows), whole(bias), whole(a_neg)] + w_specs(w_x, 0, n_tiles),
        out_specs=[tok(2 * LANES), tok(LANES), tok(LANES), tok(LANES), tail, tail, pl.BlockSpec((8, LANES), lambda i: (0, 0)), tok(width)],
        out_shape=[jax.ShapeDtypeStruct((tokens, 2 * LANES), BF16)] + [jax.ShapeDtypeStruct((tokens, LANES), BF16)] * 3 + [jax.ShapeDtypeStruct((16 * heads, tokens), BF16)] * 2 + [jax.ShapeDtypeStruct((8, LANES), F32), jax.ShapeDtypeStruct((tokens, width), BF16)],
        scratch_shapes=[pltpu.VMEM((LANES, d_model), BF16), pltpu.VMEM((8, LANES), F32), pltpu.VMEM((16 * heads, LANES), BF16)],
        compiler_params=params(),
        cost_estimate=cost(2 * tokens * d_model * (512 + width), 2 * tokens * d_model),
        name="prep",
    )(x_blk, w_bc, w_dt_rows, bias, a_neg, *([w_x] * n_tiles))


def project(x_blk, parts, after):
    tokens, d_model = x_blk.shape
    tile = min(512, tokens)
    counts = [n for _, _, n in parts]
    specs = [spec for w, t, n in parts for spec in w_specs(w, t, n)]
    return pl.pallas_call(
        functools.partial(proj_kernel, counts),
        grid=(tokens // tile,),
        in_specs=[pl.BlockSpec((tile, d_model), lambda i: (i, 0))] + specs + [ANY],
        out_specs=[pl.BlockSpec((tile, 256 * n), lambda i: (i, 0)) for n in counts],
        out_shape=[jax.ShapeDtypeStruct((tokens, 256 * n), BF16) for n in counts],
        compiler_params=params(),
        cost_estimate=cost(512 * tokens * d_model * sum(counts), 2 * tokens * d_model),
        name="project",
    )(x_blk, *[w for w, _, n in parts for _ in range(n)], after)


def add_products(acc, pieces, out_dtype):
    rows, d_model = acc.shape
    tile = min(512, d_model)
    n_tiles = [g.shape[1] // 256 for g, _, _ in pieces]
    specs, args = [pl.BlockSpec((rows, tile), lambda i: (0, i))], [acc]
    for (g, w, tile0), count in zip(pieces, n_tiles):
        specs.append(pl.BlockSpec(g.shape, lambda i: (0, 0)))
        specs += [pl.BlockSpec((256, tile), functools.partial(lambda t, i: (t, i), tile0 + t)) for t in range(count)]
        args += [g] + [w] * count
    return pl.pallas_call(
        functools.partial(sum_kernel, n_tiles, len(pieces)),
        grid=(d_model // tile,),
        in_specs=specs,
        out_specs=pl.BlockSpec((rows, tile), lambda i: (0, i)),
        out_shape=jax.ShapeDtypeStruct((rows, d_model), out_dtype),
        compiler_params=params(),
        cost_estimate=cost(2 * rows * d_model * 256 * sum(n_tiles), 2 * rows * d_model),
        name="add_products",
    )(*args)


def chunk_states(u, bc, sums, after, first_head, n_pairs):
    tokens, width = u.shape
    n_chunks = tokens // CHUNK
    last = n_chunks // STATE_CHUNKS - 1
    tok = lambda w: pl.BlockSpec((STATE_CHUNKS * CHUNK, w), lambda i: (last - i, 0))
    whole = pl.BlockSpec((LANES, width), lambda i: (0, 0))

    def body(u_ref, bc_ref, cum_ref, nexc_ref, dt_ref, after_ref, *refs):
        state_kernel(first_head, n_pairs, u_ref, bc_ref, cum_ref, nexc_ref, dt_ref, *refs)

    return pl.pallas_call(
        body,
        grid=(last + 1,),
        in_specs=[tok(width), tok(2 * LANES)] + [tok(LANES)] * 3 + [ANY],
        out_specs=[pl.BlockSpec((STATE_CHUNKS, LANES, width), lambda i: (last - i, 0, 0)), pl.BlockSpec((STATE_CHUNKS, 8, width), lambda i: (last - i, 0, 0)), whole, whole, tok(width), tok(width)],
        out_shape=[jax.ShapeDtypeStruct((n_chunks, LANES, width), F32), jax.ShapeDtypeStruct((n_chunks, 8, width), F32)] + [jax.ShapeDtypeStruct((LANES, width), BF16)] * 2 + [jax.ShapeDtypeStruct((tokens, width), BF16)] * 2,
        scratch_shapes=[pltpu.VMEM((LANES, width), F32), pltpu.VMEM((LANES, width), F32), pltpu.VMEM((8, width), F32), pltpu.VMEM((STATE_CHUNKS * CHUNK, 2 * width), BF16), pltpu.VMEM((LANES, width), BF16)],
        compiler_params=params(),
        cost_estimate=cost(16 * tokens * width * 256, 8 * tokens * width),
        name="states",
    )(u, bc, *sums, after)


def chunk_outputs(who, u, z, bc, sums, tails, local, got, logs, skip, after, first_head, n_pairs):
    tokens, width = u.shape
    n_steps = tokens // (OUT_CHUNKS * CHUNK)
    gloc, suf, scaled, ends = local
    tail = pl.BlockSpec((tails[0].shape[0], OUT_CHUNKS * CHUNK), lambda i, who: (0, i))
    tok = lambda w: pl.BlockSpec((OUT_CHUNKS * CHUNK, w), lambda i, who: (i, 0))
    state = pl.BlockSpec((LANES, width), lambda i, who: (0, 0))
    small = lambda a: pl.BlockSpec(a.shape, lambda i, who: (0, 0))
    rows_out = tokens // 4
    return pl.pallas_call(
        functools.partial(out_kernel, first_head, n_pairs),
        grid_spec=pltpu.PrefetchScalarGridSpec(
            num_scalar_prefetch=1,
            grid=(n_steps,),
            in_specs=[tok(width)] * 4 + [tok(2 * LANES), tok(LANES), tok(LANES), tail, tail, pl.BlockSpec((OUT_CHUNKS, LANES, width), lambda i, who: (i, 0, 0)), pl.BlockSpec((OUT_CHUNKS, 8, width), lambda i, who: (i, 0, 0)), state, state, state] + [small(v) for v in logs] + [small(skip), ANY],
            out_specs=[pl.BlockSpec((rows_out, width), lambda i, who: (0, 0))] * 4,
            scratch_shapes=[pltpu.VMEM((LANES, width), F32), pltpu.VMEM((LANES, width), F32), pltpu.VMEM((8, width), F32), pltpu.VMEM((OUT_CHUNKS * CHUNK, width), BF16), pltpu.VMEM((LANES, width), BF16), pltpu.VMEM((LANES, 2 * width), BF16)] + [pltpu.VMEM((OUT_CHUNKS, LANES, width), BF16)] * 2,
        ),
        out_shape=[jax.ShapeDtypeStruct((rows_out, width), BF16)] * 4,
        compiler_params=params(),
        cost_estimate=cost(24 * tokens * width * 256, 8 * tokens * width),
        name="outputs",
    )(who, u, z, scaled, ends, bc, sums[0], sums[1], *tails, gloc, suf, *got, *logs, skip, after)


def solution(mesh):
    n_tp, n_sp, n_dp = mesh.shape['tp'], mesh.shape['sp'], mesh.shape['dp']

    def swap(val, axis, slot):
        return lax.ppermute(val, axis, [(i, i ^ slot) for i in range(4)])

    def later(vals, after):
        return list(lax.optimization_barrier((*vals, after)))[:-1]

    def device_fn(x_blk, w_z, w_x, w_bc, w_dt, a_neg, dt_bias, d_skip, w_out):
        tokens, _ = x_blk.shape
        heads = a_neg.shape[0]
        head_dim = w_x.shape[1] // heads
        rows_out = tokens // n_tp
        tp_index = lax.axis_index('tp')
        sp_index = lax.axis_index('sp')

        piece_rows = w_out.shape[0] // (n_dp * n_sp)
        mine = lax.axis_index('dp') * n_sp + sp_index
        piece = lax.dynamic_slice_in_dim(w_out, mine * piece_rows, piece_rows, axis=0)
        one = swap(piece, 'tp', 1)
        two = swap(piece, 'tp', 2)
        three = swap(piece, 'tp', 3)
        plane = lambda v: lax.all_gather(v, ('dp', 'sp'), tiled=True)

        n_tiles = w_x.shape[1] // 256
        first = n_tiles * 2 // 5
        (t_a, n_a), (t_b, n_b) = (0, first), (first, n_tiles - first)
        head_b = first * 256 // head_dim
        who = jnp.stack([tp_index, sp_index])
        skip = d_skip[None, :]

        def exchange(s_fwd, s_bwd):
            return [swap(jnp.where(sp_index < (sp_index ^ s), s_fwd, s_bwd), 'sp', s) for s in (1, 2, 3)]

        def send(pieces):
            return [pieces[0]] + [swap(pieces[s], 'tp', s) for s in (1, 2, 3)]

        bc, cum3, nexc3, dt3, tail1, tail2, block_log, u_a = prep(x_blk, w_bc, w_dt.T, dt_bias[None, :], a_neg[None, :], w_x, n_a)
        logs = [swap(block_log, 'sp', s) for s in (1, 2, 3)]
        one, = later((one,), block_log)
        w_one = plane(one)
        gloc_a, suf_a, s_fwd, s_bwd, ut_a, vf_a = chunk_states(u_a, bc, (cum3, nexc3, dt3), one, 0, 2 * n_a)
        got_a = exchange(s_fwd, s_bwd)
        z_a, u_b = project(x_blk, [(w_z, t_a, n_a), (w_x, t_b, n_b)], s_fwd)
        two, = later((two,), z_a)
        w_two = plane(two)
        g_a = chunk_outputs(who, u_a, z_a, bc, (cum3, nexc3), (tail1, tail2), (gloc_a, suf_a, ut_a, vf_a), got_a, logs, skip, two, 0, 2 * n_a)
        got_g_a = send(g_a)
        three, = later((three,), g_a[0])
        w_three = plane(three)
        gloc_b, suf_b, s_fwd, s_bwd, ut_b, vf_b = chunk_states(u_b, bc, (cum3, nexc3, dt3), three, head_b, 2 * n_b)
        got_b = exchange(s_fwd, s_bwd)
        z_b, = project(x_blk, [(w_z, t_b, n_b)], s_fwd)
        g_b = chunk_outputs(who, u_b, z_b, bc, (cum3, nexc3), (tail1, tail2), (gloc_b, suf_b, ut_b, vf_b), got_b, logs, skip, z_b, head_b, 2 * n_b)
        got_g_b = send(g_b)

        own = lax.dynamic_slice_in_dim(x_blk, tp_index * rows_out, rows_out, axis=0)
        total = add_products(own, [(got_g_a[0], w_out, t_a), (got_g_b[0], w_out, t_b)], F32)
        total = add_products(total, [(got_g_a[1], w_one, t_a), (got_g_a[2], w_two, t_a)], F32)
        total = add_products(total, [(got_g_a[3], w_three, t_a), (got_g_b[1], w_one, t_b)], F32)
        return add_products(total, [(got_g_b[2], w_two, t_b), (got_g_b[3], w_three, t_b)], BF16)

    in_specs = (P(('dp', 'sp'), None), P(None, 'tp'), P(None, 'tp'), P(None, None), P(None, 'tp'), P('tp'), P('tp'), P('tp'), P('tp', None))
    out_specs = P(('dp', 'sp', 'tp'), None)
    return jax.shard_map(device_fn, mesh=mesh, in_specs=in_specs, out_specs=out_specs, check_vma=False)
```

time: 311 us -> 276 us (0.89)
  the two profiles are of different devices: /device:TPU:17 before, /device:TPU:10 now
where the time goes in v2:
time: 276 us; the launch traced here: 275 us
  Pallas kernels  145 us (53%)
  waiting for transfers between devices  86 us (31%)
  starting transfers between devices  19.6 us (7%)
  between operations  13.3 us (5%)
  local copies, waits for them, and re-layouts  9.77 us (4%)
    ppermute x18, waiting for transfers between devices, swap(): return lax.ppermute(val, axis, [(i, i ^ slot) for i in range(4)])  59.8 us
    pallas_call x4, Pallas kernels, add_products(): pl.pallas_call(functools.partial(sum_kernel, n_tiles, len(pieces)), grid=...  40.4 us
    pallas_call x2, Pallas kernels, chunk_outputs(): pl.pallas_call(functools.partial(out_kernel, first_head, n_pairs), grid_s...  33.1 us
    pallas_call x2, Pallas kernels, project(): pl.pallas_call(functools.partial(proj_kernel, counts), grid=(tokens // ti...  31.7 us
    all_gather x3, waiting for transfers between devices, device_fn(): plane = lambda v: lax.all_gather(v, ('dp', 'sp'), tiled=True)  25.5 us
    pallas_call x2, Pallas kernels, chunk_states(): pl.pallas_call(body, grid=(last + 1,), in_specs=[tok(width), tok(2 * LANE...  19.9 us
    pallas_call x1, Pallas kernels, prep(): pl.pallas_call(functools.partial(prep_kernel, n_tiles), grid=(tokens // t...  19.6 us
    ppermute x18, starting transfers between devices, swap(): return lax.ppermute(val, axis, [(i, i ^ slot) for i in range(4)])  19.4 us
  transfers between devices with their start and end apart: 21, of which 9 were waited for; matrix products, arithmetic and copies ran while one was open for 2% of the time, Pallas kernels for 49%

profile of v2, /device:TPU:10, one launch (start us, length us, event | category | flops | bytes accessed | tf_op | source)
XLA Modules:
  0.0 275.1 jit_solution(4502431697440334207)
XLA Ops:
  6.5 2.1 constant_dynamic-slice_fusion
  9.1 2.6 collective-permute-start.7
  11.7 19.6 %prep.1 = (bf16[2048,256]{1,0:T(8,128)(2,1)}, bf16[2048,128]{1,0:T(8,128)(2,1)}, bf16[2048,128]{1,0:T(8,128)(2,1)}, bf16[2048,128]{1,0:T(8,128)(2,1)}, bf16[320,...) custom-call(bf16[2048,2560]{1,0:T(8,128)(2,1)} %x_ref.5, ...), custom_call_target="tpu_custom_call" | custom-call | flops 10737418240 | bytes 10485760 | tf_op jit(solution)/shard_map/prep/pallas_call | solution.py:284
  31.3 13.1 %collective-permute-done.after_ref = bf16[160,2560]{1,0:T(8,128)(2,1)S(1)} collective-permute-done((bf16[160,2560]{1,0:T(8,128)(2,1)}, bf16[160,2560]{1,0:T(8,128)(2,1)S(1)}, u32[]{:S(2)}, u32[]{:S(2)}) %collective-permute-start) | collective-permute-done | bytes 819232 | tf_op jit(solution)/shard_map/ppermute | solution.py:387
  44.4 0.9 copy-done
  45.3 8.9 %states.2 = (f32[16,128,512]{2,1,0:T(8,128)}, f32[16,8,512]{2,1,0:T(8,128)}, bf16[128,512]{1,0:T(8,128)(2,1)}, bf16[128,512]{1,0:T(8,128)(2,1)}, bf16[2048,512]{1,0:T(8,128)(2,1)}, /*index=5*/bf16[2048,512]{1,0:T(8,128)(2,1)}) custom-call(bf16[2048,512]{1,0:T(8,128)(2,1)} %get-tuple-element.38.u_ref, bf16[2048,256]{1,0:T(8,128)(2,1)} %get-tuple-element.39.bc_ref, ...), custom_call_target="tpu_custom_call" | custom-call | flops 4294967296 | bytes 8388608 | tf_op jit(solution)/shard_map/states/pallas_call | solution.py:345
  54.2 19.0 %project.2 = (bf16[2048,512]{1,0:T(8,128)(2,1)}, bf16[2048,768]{1,0:T(8,128)(2,1)}) custom-call(bf16[2048,2560]{1,0:T(8,128)(2,1)} %x_ref.5, bf16[2560,1280]{1,0:T(8,128)(2,1)} %refs_2_.4, bf16[2560,1280]{1,0:T(8,128)(2,1)} %refs_2_.4, bf16[2560,1280]{1,0:T(8,128)(2,1)} %refs_4_.2, bf16[2560,1280]{1,0:T(8,128)(2,1)} %refs_4_.2, bf16[2560,1280]{1,0:T(8,128)(2,1)} %refs_4_.2, ...), custom_call_target="tpu_custom_call" | custom-call | flops 13421772800 | bytes 10485760 | tf_op jit(solution)/shard_map/project/pallas_call | solution.py:302
  73.2 0.9 copy-done.1
  75.1 1.7 collective-permute-start.8
  76.9 1.6 collective-permute-start.2
  79.9 1.5 collective-permute-start.5
  81.4 4.2 %collective-permute-done.5.l2_ref = f32[8,128]{1,0:T(8,128)S(1)} collective-permute-done((f32[8,128]{1,0:T(8,128)S(1)}, f32[8,128]{1,0:T(8,128)S(1)}, u32[]{:S(2)}, u32[]{:S(2)}) %collective-permute-start.5) | collective-permute-done | bytes 4128 | tf_op jit(solution)/shard_map/ppermute | solution.py:387
  87.0 1.9 collective-permute-done.6.l3_ref
  89.7 14.6 %outputs.2 = (bf16[512,512]{1,0:T(8,128)(2,1)}, bf16[512,512]{1,0:T(8,128)(2,1)}, bf16[512,512]{1,0:T(8,128)(2,1)}, bf16[512,512]{1,0:T(8,128)(2,1)}) custom-call(s32[2]{0:T(128)} %pad_add_fusion.who_ref, bf16[2048,512]{1,0:T(8,128)(2,1)} %get-tuple-element.38.u_ref, bf16[2048,512]{1,0:T(8,128)(2,1)} %get-tuple-element.46.z_ref, ...), custom_call_target="tpu_custom_call" | custom-call | flops 6442450944 | bytes 8388608 | tf_op jit(solution)/shard_map/outputs/pallas_call | solution.py:367
  104.3 7.8 %collective-permute-done.8.after_ref = bf16[160,2560]{1,0:T(8,128)(2,1)S(1)} collective-permute-done((bf16[160,2560]{1,0:T(8,128)(2,1)}, bf16[160,2560]{1,0:T(8,128)(2,1)S(1)}, u32[]{:S(2)}, u32[]{:S(2)}) %collective-permute-start.8) | collective-permute-done | bytes 819232 | tf_op jit(solution)/shard_map/ppermute | solution.py:387
  112.0 0.9 copy-done.2
  113.0 11.1 %states.3 = (f32[16,128,768]{2,1,0:T(8,128)}, f32[16,8,768]{2,1,0:T(8,128)}, bf16[128,768]{1,0:T(8,128)(2,1)}, bf16[128,768]{1,0:T(8,128)(2,1)}, bf16[2048,768]{1,0:T(8,128)(2,1)}, /*index=5*/bf16[2048,768]{1,0:T(8,128)(2,1)}) custom-call(bf16[2048,768]{1,0:T(8,128)(2,1)} %get-tuple-element.56.u_ref, bf16[2048,256]{1,0:T(8,128)(2,1)} %get-tuple-element.39.bc_ref, ...), custom_call_target="tpu_custom_call" | custom-call | flops 6442450944 | bytes 12582912 | tf_op jit(solution)/shard_map/states/pallas_call | solution.py:345
  124.0 1.1 broadcast_select_fusion
  125.1 1.5 collective-permute-start.10
  127.3 12.7 %project.3.z_ref.after_ref = bf16[2048,768]{1,0:T(8,128)(2,1)} custom-call(bf16[2048,2560]{1,0:T(8,128)(2,1)} %x_ref.5, bf16[2560,1280]{1,0:T(8,128)(2,1)} %refs_2_.4, bf16[2560,1280]{1,0:T(8,128)(2,1)} %refs_2_.4, bf16[2560,1280]{1,0:T(8,128)(2,1)} %refs_2_.4, bf16[128,768]{1,0:T(8,128)(2,1)} %get-tuple-element.58.refs_3_), custom_call_target="tpu_custom_call" | custom-call | flops 8053063680 | bytes 10485760 | tf_op jit(solution)/shard_map/project/pallas_call | solution.py:302
  140.0 3.1 %collective-permute-start.13 = (bf16[512,512]{1,0:T(8,128)(2,1)}, bf16[512,512]{1,0:T(8,128)(2,1)}, u32[]{:S(2)}, u32[]{:S(2)}) collective-permute-start(bf16[512,512]{1,0:T(8,128)(2,1)} %get-tuple-element.66), channel_id=1, source_target_pairs={{0,8},{4,12},{8,0},{12,4},{1,9},{5,13},{9,1},{13,5},{2,10},{6,14},... | collective-permute-start | bytes 1572872 | tf_op jit(solution)/shard_map/ppermute | solution.py:387
  143.9 18.5 %outputs.3 = (bf16[512,768]{1,0:T(8,128)(2,1)}, bf16[512,768]{1,0:T(8,128)(2,1)}, bf16[512,768]{1,0:T(8,128)(2,1)}, bf16[512,768]{1,0:T(8,128)(2,1)}) custom-call(s32[2]{0:T(128)} %pad_add_fusion.who_ref, bf16[2048,768]{1,0:T(8,128)(2,1)} %get-tuple-element.56.u_ref, bf16[2048,768]{1,0:T(8,128)(2,1)} %project.3.z_ref.after_ref, ...), custom_call_target="tpu_custom_call" | custom-call | flops 9663676416 | bytes 12582912 | tf_op jit(solution)/shard_map/outputs/pallas_call | solution.py:367
  163.0 3.4 %constant_dynamic-slice_fusion.1.acc_ref = bf16[512,2560]{1,0:T(8,128)(2,1)} fusion(bf16[2048,2560]{1,0:T(8,128)(2,1)} %x_ref.5, s32[]{:T(128)S(6)} %select_n.46), kind=kLoop, calls=%fused_computation.8 | loop fusion | bytes 5242884 | tf_op jit(solution)/shard_map/dynamic_slice | solution.py:440
  166.8 3.5 %collective-permute-start.16 = (bf16[512,768]{1,0:T(8,128)(2,1)}, bf16[512,768]{1,0:T(8,128)(2,1)S(1)}, u32[]{:S(2)}, u32[]{:S(2)}) collective-permute-start(bf16[512,768]{1,0:T(8,128)(2,1)} %get-tuple-element.69), channel_id=1, source_target_pairs={{0,8},{4,12},{8,0},{12,4},{1,9},{5,13},{9,1},{13,5},{2,10},{6,14},... | collective-permute-start | bytes 2359304 | tf_op jit(solution)/shard_map/ppermute | solution.py:387
  170.7 9.5 %add_products.4.acc_ref = f32[512,2560]{1,0:T(8,128)} custom-call(bf16[512,2560]{1,0:T(8,128)(2,1)} %constant_dynamic-slice_fusion.1.acc_ref, bf16[512,512]{1,0:T(8,128)(2,1)} %get-tuple-element.55.refs_0_, bf16[1280,2560]{1,0:T(8,128)(2,1)} %refs_6_.1, bf16[1280,2560]{1,0:T(8,128)(2,1)} %refs_6_.1, bf16[512,768]{1,0:T(8,128)(2,1)} %get-tuple-element.64.refs_3_, ...), custom_call_target="tpu_custom_call" | custom-call | flops 3355443200 | bytes 2621440 | tf_op jit(solution)/shard_map/add_products/pallas_call | solution.py:323
  180.2 10.5 %add_products.5.acc_ref = f32[512,2560]{1,0:T(8,128)} custom-call(f32[512,2560]{1,0:T(8,128)} %add_products.4.acc_ref, bf16[512,512]{1,0:T(8,128)(2,1)} %collective-permute-done.12.refs_0_, bf16[1280,2560]{1,0:T(8,128)(2,1)} %all-gather.4.cloned.1.call-done.refs_1_.refs_2_.refs_4_.refs_5_.refs_6_, ...), custom_call_target="tpu_custom_call" | custom-call | flops 2684354560 | bytes 2621440 | tf_op jit(solution)/shard_map/add_products/pallas_call | solution.py:323
  190.7 3.9 %collective-permute-done.15.refs_3_ = bf16[512,768]{1,0:T(8,128)(2,1)S(1)} collective-permute-done((bf16[512,768]{1,0:T(8,128)(2,1)}, bf16[512,768]{1,0:T(8,128)(2,1)S(1)}, u32[]{:S(2)}, u32[]{:S(2)}) %collective-permute-start.15) | collective-permute-done | bytes 786464 | tf_op jit(solution)/shard_map/ppermute | solution.py:387
  194.6 25.4 %all-gather.8.cloned.1.call-done.refs_1_.refs_2_.refs_5_.refs_6_.refs_7_ = bf16[1280,2560]{1,0:T(8,128)(2,1)} async-done(((bf16[160,2560]{1,0:T(8,128)(2,1)}), bf16[1280,2560]{1,0:T(8,128)(2,1)}) %all-gather.8.cloned.1.call-update) | async-done | bytes 6553616 | tf_op jit(solution)/shard_map/all_gather | solution.py:406
  220.1 10.5 %add_products.6.acc_ref = f32[512,2560]{1,0:T(8,128)} custom-call(f32[512,2560]{1,0:T(8,128)} %add_products.5.acc_ref, bf16[512,512]{1,0:T(8,128)(2,1)} %collective-permute-done.14.refs_0_, bf16[1280,2560]{1,0:T(8,128)(2,1)} %all-gather.8.cloned.1.call-done.refs_1_.refs_2_.refs_5_.refs_6_.refs_7_, ...), custom_call_target="tpu_custom_call" | custom-call | flops 3355443200 | bytes 2621440 | tf_op jit(solution)/shard_map/add_products/pallas_call | solution.py:323
  230.6 10.7 %collective-permute-done.16.refs_0_ = bf16[512,768]{1,0:T(8,128)(2,1)S(1)} collective-permute-done((bf16[512,768]{1,0:T(8,128)(2,1)}, bf16[512,768]{1,0:T(8,128)(2,1)S(1)}, u32[]{:S(2)}, u32[]{:S(2)}) %collective-permute-start.16) | collective-permute-done | bytes 786464 | tf_op jit(solution)/shard_map/ppermute | solution.py:387
  241.3 17.3 %collective-permute-done.17.refs_4_ = bf16[512,768]{1,0:T(8,128)(2,1)} collective-permute-done((bf16[512,768]{1,0:T(8,128)(2,1)}, bf16[512,768]{1,0:T(8,128)(2,1)}, u32[]{:S(2)}, u32[]{:S(2)}) %collective-permute-start.17) | collective-permute-done | bytes 786464 | tf_op jit(solution)/shard_map/ppermute | solution.py:387
  258.6 10.0 %add_products.7 = bf16[512,2560]{1,0:T(8,128)(2,1)} custom-call(f32[512,2560]{1,0:T(8,128)} %add_products.6.acc_ref, bf16[512,768]{1,0:T(8,128)(2,1)} %copy-done.3, bf16[1280,2560]{1,0:T(8,128)(2,1)} %all-gather.6.cloned.1.call-done.refs_4_.refs_5_.refs_1_.refs_2_.refs_3_, ...), custom_call_target="tpu_custom_call" | custom-call | flops 4026531840 | bytes 2621440 | tf_op jit(solution)/shard_map/add_products/pallas_call | solution.py:323
  (63 shorter events, 8.1 us)
Async XLA Ops:
  6.5 173.6 %all-gather.6.cloned.1.call-start = ((), (), s32[]{:S(2)}) async-start(), calls=%async_computation.1 | async-start | bytes 7372800 | tf_op jit(solution)/shard_map/all_gather | solution.py:406
  8.7 35.7 %collective-permute-start = (bf16[160,2560]{1,0:T(8,128)(2,1)}, bf16[160,2560]{1,0:T(8,128)(2,1)S(1)}, u32[]{:S(2)}, u32[]{:S(2)}) collective-permute-start(bf16[160,2560]{1,0:T(8,128)(2,1)} %constant_dynamic-slice_fusion), channel_id=1, source_target_pairs={{0,4},{4,0},{8,12},{12,8},{1,5},{5,1},{9,13},{13,9},{2,6},{6,2},{1... | collective-permute-start | bytes 2457608 | tf_op jit(solution)/shard_map/ppermute | solution.py:387
  9.1 64.1 %collective-permute-start.7 = (bf16[160,2560]{1,0:T(8,128)(2,1)}, bf16[160,2560]{1,0:T(8,128)(2,1)S(1)}, u32[]{:S(2)}, u32[]{:S(2)}) collective-permute-start(bf16[160,2560]{1,0:T(8,128)(2,1)} %constant_dynamic-slice_fusion), channel_id=1, source_target_pairs={{0,8},{4,12},{8,0},{12,4},{1,9},{5,13},{9,1},{13,5},{2,10},{6,14},... | collective-permute-start | bytes 2457608 | tf_op jit(solution)/shard_map/ppermute | solution.py:387
  44.4 0.9 copy-start
  54.2 22.6 %copy-start.5 = (bf16[128,512]{1,0:T(8,128)(2,1)S(1)}, bf16[128,512]{1,0:T(8,128)(2,1)}, u32[]{:S(2)}) copy-start(bf16[128,512]{1,0:T(8,128)(2,1)} %get-tuple-element.45.refs_5_) | copy-start | bytes 393220
  54.2 22.6 %copy-start.6 = (bf16[128,512]{1,0:T(8,128)(2,1)S(1)}, bf16[128,512]{1,0:T(8,128)(2,1)}, u32[]{:S(2)}) copy-start(bf16[128,512]{1,0:T(8,128)(2,1)} %get-tuple-element.53) | copy-start | bytes 393220
  54.2 24.5 %copy-start.16 = (f32[8,128]{1,0:T(8,128)S(1)}, f32[8,128]{1,0:T(8,128)}, u32[]{:S(2)}) copy-start(f32[8,128]{1,0:T(8,128)} %get-tuple-element.43) | copy-start | bytes 12292
  73.2 0.9 copy-start.1
  74.1 106.1 %all-gather.4.cloned.1.call-start = ((), (), s32[]{:S(2)}) async-start(), calls=%async_computation | async-start | bytes 7372800 | tf_op jit(solution)/shard_map/all_gather | solution.py:406
  74.9 145.2 %all-gather.8.cloned.1.call-start = ((), (), s32[]{:S(2)}) async-start(), calls=%async_computation.2 | async-start | bytes 7372800 | tf_op jit(solution)/shard_map/all_gather | solution.py:406
  75.1 37.0 %collective-permute-start.8 = (bf16[160,2560]{1,0:T(8,128)(2,1)}, bf16[160,2560]{1,0:T(8,128)(2,1)S(1)}, u32[]{:S(2)}, u32[]{:S(2)}) collective-permute-start(bf16[160,2560]{1,0:T(8,128)(2,1)} %constant_dynamic-slice_fusion), channel_id=1, source_target_pairs={{0,12},{4,8},{8,4},{12,0},{1,13},{5,9},{9,5},{13,1},{2,14},{6,10},... | collective-permute-start | bytes 2457608 | tf_op jit(solution)/shard_map/ppermute | solution.py:387
  76.8 12.1 %collective-permute-start.1 = (bf16[128,512]{1,0:T(8,128)(2,1)S(1)}, bf16[128,512]{1,0:T(8,128)(2,1)S(1)}, u32[]{:S(2)}, u32[]{:S(2)}) collective-permute-start(bf16[128,512]{1,0:T(8,128)(2,1)S(1)} %get-tuple-element.76), channel_id=1, source_target_pairs={{0,1},{1,0},{2,3},{3,2},{4,5},{5,4},{6,7},{7,6},{8,9},{9,8},{10,11... | collective-permute-start | bytes 393224 | tf_op jit(solution)/shard_map/ppermute | solution.py:387
  76.9 12.0 %collective-permute-start.2 = (bf16[128,512]{1,0:T(8,128)(2,1)S(1)}, bf16[128,512]{1,0:T(8,128)(2,1)S(1)}, u32[]{:S(2)}, u32[]{:S(2)}) collective-permute-start(bf16[128,512]{1,0:T(8,128)(2,1)S(1)} %get-tuple-element.75), channel_id=1, source_target_pairs={{0,2},{1,3},{2,0},{3,1},{4,6},{5,7},{6,4},{7,5},{8,10},{9,11},{10,... | collective-permute-start | bytes 393224 | tf_op jit(solution)/shard_map/ppermute | solution.py:387
  78.4 10.5 %collective-permute-start.3 = (bf16[128,512]{1,0:T(8,128)(2,1)S(1)}, bf16[128,512]{1,0:T(8,128)(2,1)S(1)}, u32[]{:S(2)}, u32[]{:S(2)}) collective-permute-start(bf16[128,512]{1,0:T(8,128)(2,1)S(1)} %get-tuple-element.74), channel_id=1, source_target_pairs={{0,3},{1,2},{2,1},{3,0},{4,7},{5,6},{6,5},{7,4},{8,11},{9,10},{10,... | collective-permute-start | bytes 393224 | tf_op jit(solution)/shard_map/ppermute | solution.py:387
  78.7 1.2 collective-permute-start.4
  79.9 9.0 %copy-start.13 = (f32[8,128]{1,0:T(8,128)}, f32[8,128]{1,0:T(8,128)S(1)}, u32[]{:S(2)}) copy-start(f32[8,128]{1,0:T(8,128)S(1)} %collective-permute-done.4.l1_ref) | copy-start | bytes 12292
  79.9 5.8 %collective-permute-start.5 = (f32[8,128]{1,0:T(8,128)S(1)}, f32[8,128]{1,0:T(8,128)S(1)}, u32[]{:S(2)}, u32[]{:S(2)}) collective-permute-start(f32[8,128]{1,0:T(8,128)S(1)} %copy-done.16), channel_id=1, source_target_pairs={{0,2},{1,3},{2,0},{3,1},{4,6},{5,7},{6,4},{7,5},{8,10},{9,11},{10,... | collective-permute-start | bytes 12296 | tf_op jit(solution)/shard_map/ppermute | solution.py:387
  85.7 3.3 %copy-start.14 = (f32[8,128]{1,0:T(8,128)}, f32[8,128]{1,0:T(8,128)S(1)}, u32[]{:S(2)}) copy-start(f32[8,128]{1,0:T(8,128)S(1)} %collective-permute-done.5.l2_ref) | copy-start | bytes 12292
  85.7 3.2 %collective-permute-start.6 = (f32[8,128]{1,0:T(8,128)S(1)}, f32[8,128]{1,0:T(8,128)S(1)}, u32[]{:S(2)}, u32[]{:S(2)}) collective-permute-start(f32[8,128]{1,0:T(8,128)S(1)} %copy-done.16), channel_id=1, source_target_pairs={{0,3},{1,2},{2,1},{3,0},{4,7},{5,6},{6,5},{7,4},{8,11},{9,10},{10,... | collective-permute-start | bytes 12296 | tf_op jit(solution)/shard_map/ppermute | solution.py:387
  112.0 0.9 copy-start.2
  125.1 18.0 %collective-permute-start.10 = (bf16[128,768]{1,0:T(8,128)(2,1)S(1)}, bf16[128,768]{1,0:T(8,128)(2,1)S(1)}, u32[]{:S(2)}, u32[]{:S(2)}) collective-permute-start(bf16[128,768]{1,0:T(8,128)(2,1)S(1)} %get-tuple-element.72), channel_id=1, source_target_pairs={{0,2},{1,3},{2,0},{3,1},{4,6},{5,7},{6,4},{7,5},{8,10},{9,11},{10,... | collective-permute-start | bytes 589832 | tf_op jit(solution)/shard_map/ppermute | solution.py:387
  126.6 16.5 %collective-permute-start.11 = (bf16[128,768]{1,0:T(8,128)(2,1)S(1)}, bf16[128,768]{1,0:T(8,128)(2,1)S(1)}, u32[]{:S(2)}, u32[]{:S(2)}) collective-permute-start(bf16[128,768]{1,0:T(8,128)(2,1)S(1)} %get-tuple-element.71), channel_id=1, source_target_pairs={{0,3},{1,2},{2,1},{3,0},{4,7},{5,6},{6,5},{7,4},{8,11},{9,10},{10,... | collective-permute-start | bytes 589832 | tf_op jit(solution)/shard_map/ppermute | solution.py:387
  126.6 16.5 %collective-permute-start.9 = (bf16[128,768]{1,0:T(8,128)(2,1)S(1)}, bf16[128,768]{1,0:T(8,128)(2,1)S(1)}, u32[]{:S(2)}, u32[]{:S(2)}) collective-permute-start(bf16[128,768]{1,0:T(8,128)(2,1)S(1)} %get-tuple-element.73), channel_id=1, source_target_pairs={{0,1},{1,0},{2,3},{3,2},{4,5},{5,4},{6,7},{7,6},{8,9},{9,8},{10,11... | collective-permute-start | bytes 589832 | tf_op jit(solution)/shard_map/ppermute | solution.py:387
  140.0 30.3 %collective-permute-start.12 = (bf16[512,512]{1,0:T(8,128)(2,1)}, bf16[512,512]{1,0:T(8,128)(2,1)}, u32[]{:S(2)}, u32[]{:S(2)}) collective-permute-start(bf16[512,512]{1,0:T(8,128)(2,1)} %get-tuple-element.65), channel_id=1, source_target_pairs={{0,4},{4,0},{8,12},{12,8},{1,5},{5,1},{9,13},{13,9},{2,6},{6,2},{1... | collective-permute-start | bytes 1572872 | tf_op jit(solution)/shard_map/ppermute | solution.py:387
  140.0 40.2 %collective-permute-start.13 = (bf16[512,512]{1,0:T(8,128)(2,1)}, bf16[512,512]{1,0:T(8,128)(2,1)}, u32[]{:S(2)}, u32[]{:S(2)}) collective-permute-start(bf16[512,512]{1,0:T(8,128)(2,1)} %get-tuple-element.66), channel_id=1, source_target_pairs={{0,8},{4,12},{8,0},{12,4},{1,9},{5,13},{9,1},{13,5},{2,10},{6,14},... | collective-permute-start | bytes 1572872 | tf_op jit(solution)/shard_map/ppermute | solution.py:387
  143.1 0.8 copy-start.9
  162.4 32.2 %collective-permute-start.15 = (bf16[512,768]{1,0:T(8,128)(2,1)}, bf16[512,768]{1,0:T(8,128)(2,1)S(1)}, u32[]{:S(2)}, u32[]{:S(2)}) collective-permute-start(bf16[512,768]{1,0:T(8,128)(2,1)} %get-tuple-element.68), channel_id=1, source_target_pairs={{0,4},{4,0},{8,12},{12,8},{1,5},{5,1},{9,13},{13,9},{2,6},{6,2},{1... | collective-permute-start | bytes 2359304 | tf_op jit(solution)/shard_map/ppermute | solution.py:387
  166.4 24.4 %collective-permute-start.14 = (bf16[512,512]{1,0:T(8,128)(2,1)}, bf16[512,512]{1,0:T(8,128)(2,1)}, u32[]{:S(2)}, u32[]{:S(2)}) collective-permute-start(bf16[512,512]{1,0:T(8,128)(2,1)} %get-tuple-element.67), channel_id=1, source_target_pairs={{0,12},{4,8},{8,4},{12,0},{1,13},{5,9},{9,5},{13,1},{2,14},{6,10},... | collective-permute-start | bytes 1572872 | tf_op jit(solution)/shard_map/ppermute | solution.py:387
  166.8 74.5 %collective-permute-start.16 = (bf16[512,768]{1,0:T(8,128)(2,1)}, bf16[512,768]{1,0:T(8,128)(2,1)S(1)}, u32[]{:S(2)}, u32[]{:S(2)}) collective-permute-start(bf16[512,768]{1,0:T(8,128)(2,1)} %get-tuple-element.69), channel_id=1, source_target_pairs={{0,8},{4,12},{8,0},{12,4},{1,9},{5,13},{9,1},{13,5},{2,10},{6,14},... | collective-permute-start | bytes 2359304 | tf_op jit(solution)/shard_map/ppermute | solution.py:387
  170.3 88.3 %collective-permute-start.17 = (bf16[512,768]{1,0:T(8,128)(2,1)}, bf16[512,768]{1,0:T(8,128)(2,1)}, u32[]{:S(2)}, u32[]{:S(2)}) collective-permute-start(bf16[512,768]{1,0:T(8,128)(2,1)} %get-tuple-element.70), channel_id=1, source_target_pairs={{0,12},{4,8},{8,4},{12,0},{1,13},{5,9},{9,5},{13,1},{2,14},{6,10},... | collective-permute-start | bytes 2359304 | tf_op jit(solution)/shard_map/ppermute | solution.py:387
  194.6 25.4 %copy-start.4 = (bf16[512,768]{1,0:T(8,128)(2,1)}, bf16[512,768]{1,0:T(8,128)(2,1)S(1)}, u32[]{:S(2)}) copy-start(bf16[512,768]{1,0:T(8,128)(2,1)S(1)} %collective-permute-done.15.refs_3_) | copy-start | bytes 2359300
  241.3 17.3 %copy-start.3 = (bf16[512,768]{1,0:T(8,128)(2,1)}, bf16[512,768]{1,0:T(8,128)(2,1)S(1)}, u32[]{:S(2)}) copy-start(bf16[512,768]{1,0:T(8,128)(2,1)S(1)} %collective-permute-done.16.refs_0_) | copy-start | bytes 2359300
  (6 other events, 4.1 us)
Sparse Core Ops, SparseCore 0:
  74.2 48.9 all-gather.5
  125.1 46.4 all-gather.3
  173.5 46.4 all-gather.7

commit v3 on v2

--- a/solution.py
+++ b/solution.py
@@ -14,6 +14,7 @@
 STATE_CHUNKS = 4
 OUT_CHUNKS = 2
 OUT_AHEAD = 2
+SUM_MIB = 24
 F32 = jnp.float32
 BF16 = jnp.bfloat16
 
@@ -48,30 +49,35 @@
 
     x_val = x_ref[...]
     raw = lax.dot_general(x_val, w_buf[...], (((1,), (1,)), ((), ())), preferred_element_type=F32) + par[0:1, :]
-    bc_ref[...] = jnp.dot(x_val, wbc_ref[...], preferred_element_type=F32).astype(BF16)
+
+    def u_tile(i):
+        u_ref[:, i * 256:(i + 1) * 256] = jnp.dot(x_val, refs[i][...], preferred_element_type=F32).astype(BF16)
+
+    u_tile(0)
     dt_val = jnp.maximum(raw, 0.0) + jnp.log1p(jnp.exp(-jnp.abs(raw)))
     la_val = jnp.maximum(dt_val * par[1:2, :], -1000.0)
     tri = jnp.where(row >= lane, 1.0, 0.0).astype(BF16)
-    for c in range(x_val.shape[0] // CHUNK):
-        part = slice(c * CHUNK, (c + 1) * CHUNK)
+    parts = [slice(c * CHUNK, (c + 1) * CHUNK) for c in range(x_val.shape[0] // CHUNK)]
+    sums = []
+    for part in parts:
         la_c = la_val[part, :]
         first = la_c.astype(BF16)
         rest = la_c - first.astype(F32)
         second = rest.astype(BF16)
         third = (rest - second.astype(F32)).astype(BF16)
-        cum = sum(jnp.dot(tri, t, preferred_element_type=F32) for t in (first, second, third))
-        one = jnp.where(lane < 3 * SLOT + 3, 1.0, 0.0)
-        cum3 = split3(cum, lane, one)
-        nexc3 = split3(la_c - cum, lane, one)
-        cum_ref[part, :] = cum3
-        nexc_ref[part, :] = nexc3
+        sums.append(sum(jnp.dot(tri, t, preferred_element_type=F32) for t in (first, second, third)))
+    for i in range(1, n_tiles):
+        u_tile(i)
+    one = jnp.where(lane < 3 * SLOT + 3, 1.0, 0.0)
+    for part, cum in zip(parts, sums):
+        cum_ref[part, :] = split3(cum, lane, one)
+        nexc_ref[part, :] = split3(la_val[part, :] - cum, lane, one)
         dt_ref[part, :] = split3(dt_val[part, :], lane, 0.0)
-        across = (((1,), (1,)), ((), ()))
-        tail1_ref[:, part] = lax.dot_general(pick[...], cum3, across, preferred_element_type=F32).astype(BF16)
-        tail2_ref[:, part] = lax.dot_general(pick[...], nexc3, across, preferred_element_type=F32).astype(BF16)
         log_ref[...] += cum[CHUNK - 1:CHUNK, :]
-    for i in range(n_tiles):
-        u_ref[:, i * 256:(i + 1) * 256] = jnp.dot(x_val, refs[i][...], preferred_element_type=F32).astype(BF16)
+    bc_ref[...] = jnp.dot(x_val, wbc_ref[...], preferred_element_type=F32).astype(BF16)
+    across = (((1,), (1,)), ((), ()))
+    tail1_ref[...] = lax.dot_general(pick[...], cum_ref[...], across, preferred_element_type=F32).astype(BF16)
+    tail2_ref[...] = lax.dot_general(pick[...], nexc_ref[...], across, preferred_element_type=F32).astype(BF16)
 
 
 def proj_kernel(counts, x_ref, *refs):
@@ -258,8 +264,8 @@
             o_ref[pl.ds(pl.multiple_of((step % steps) * length, length), length), :] = g_buf[...]
 
 
-def params():
-    return pltpu.CompilerParams(dimension_semantics=("arbitrary",), vmem_limit_bytes=62 << 20)
+def params(mib=62):
+    return pltpu.CompilerParams(dimension_semantics=("arbitrary",), vmem_limit_bytes=mib << 20)
 
 
 def cost(flops, moved):
@@ -311,25 +317,28 @@
     )(x_blk, *[w for w, _, n in parts for _ in range(n)], after)
 
 
-def add_products(acc, pieces, out_dtype):
-    rows, d_model = acc.shape
+def add_products(who, acc, pieces, out_dtype):
+    rows, d_model = pieces[0][0].shape[0], acc.shape[1]
     tile = min(512, d_model)
     n_tiles = [g.shape[1] // 256 for g, _, _ in pieces]
-    specs, args = [pl.BlockSpec((rows, tile), lambda i: (0, i))], [acc]
+    mine = acc.shape[0] > rows
+    specs, args = [pl.BlockSpec((rows, tile), lambda i, who: (who[0] if mine else 0, i))], [acc]
     for (g, w, tile0), count in zip(pieces, n_tiles):
-        specs.append(pl.BlockSpec(g.shape, lambda i: (0, 0)))
-        specs += [pl.BlockSpec((256, tile), functools.partial(lambda t, i: (t, i), tile0 + t)) for t in range(count)]
+        specs.append(pl.BlockSpec(g.shape, lambda i, who: (0, 0)))
+        specs += [pl.BlockSpec((256, tile), functools.partial(lambda t, i, who: (t, i), tile0 + t)) for t in range(count)]
         args += [g] + [w] * count
+
+    def body(who_ref, *refs):
+        sum_kernel(n_tiles, len(pieces), *refs)
+
     return pl.pallas_call(
-        functools.partial(sum_kernel, n_tiles, len(pieces)),
-        grid=(d_model // tile,),
-        in_specs=specs,
-        out_specs=pl.BlockSpec((rows, tile), lambda i: (0, i)),
+        body,
+        grid_spec=pltpu.PrefetchScalarGridSpec(num_scalar_prefetch=1, grid=(d_model // tile,), in_specs=specs, out_specs=pl.BlockSpec((rows, tile), lambda i, who: (0, i))),
         out_shape=jax.ShapeDtypeStruct((rows, d_model), out_dtype),
-        compiler_params=params(),
+        compiler_params=params(SUM_MIB),
         cost_estimate=cost(2 * rows * d_model * 256 * sum(n_tiles), 2 * rows * d_model),
         name="add_products",
-    )(*args)
+    )(who, *args)
 
 
 def chunk_states(u, bc, sums, after, first_head, n_pairs):
@@ -381,7 +390,7 @@
 
 
 def solution(mesh):
-    n_tp, n_sp, n_dp = mesh.shape['tp'], mesh.shape['sp'], mesh.shape['dp']
+    n_sp, n_dp = mesh.shape['sp'], mesh.shape['dp']
 
     def swap(val, axis, slot):
         return lax.ppermute(val, axis, [(i, i ^ slot) for i in range(4)])
@@ -390,20 +399,24 @@
         return list(lax.optimization_barrier((*vals, after)))[:-1]
 
     def device_fn(x_blk, w_z, w_x, w_bc, w_dt, a_neg, dt_bias, d_skip, w_out):
-        tokens, _ = x_blk.shape
         heads = a_neg.shape[0]
         head_dim = w_x.shape[1] // heads
-        rows_out = tokens // n_tp
         tp_index = lax.axis_index('tp')
         sp_index = lax.axis_index('sp')
 
         piece_rows = w_out.shape[0] // (n_dp * n_sp)
-        mine = lax.axis_index('dp') * n_sp + sp_index
+        mine = (sp_index % 2) * (n_dp * n_sp // 2) + lax.axis_index('dp') * (n_sp // 2) + sp_index // 2
         piece = lax.dynamic_slice_in_dim(w_out, mine * piece_rows, piece_rows, axis=0)
         one = swap(piece, 'tp', 1)
         two = swap(piece, 'tp', 2)
-        three = swap(piece, 'tp', 3)
-        plane = lambda v: lax.all_gather(v, ('dp', 'sp'), tiled=True)
+        core = sp_index % 2
+
+        def plane(v):
+            return lax.all_gather(v, ('dp', 'sp'), tiled=True, axis_index_groups=[[0, 2, 4, 6], [1, 3, 5, 7]])
+
+        def whole(half):
+            other = swap(half, 'sp', 1)
+            return jnp.where(core == 0, jnp.concatenate([half, other]), jnp.concatenate([other, half]))
 
         n_tiles = w_x.shape[1] // 256
         first = n_tiles * 2 // 5
@@ -424,24 +437,24 @@
         w_one = plane(one)
         gloc_a, suf_a, s_fwd, s_bwd, ut_a, vf_a = chunk_states(u_a, bc, (cum3, nexc3, dt3), one, 0, 2 * n_a)
         got_a = exchange(s_fwd, s_bwd)
-        z_a, u_b = project(x_blk, [(w_z, t_a, n_a), (w_x, t_b, n_b)], s_fwd)
-        two, = later((two,), z_a)
+        two, = later((two,), s_fwd)
+        three = swap(two, 'tp', 1)
         w_two = plane(two)
-        g_a = chunk_outputs(who, u_a, z_a, bc, (cum3, nexc3), (tail1, tail2), (gloc_a, suf_a, ut_a, vf_a), got_a, logs, skip, two, 0, 2 * n_a)
+        z_a, u_b = project(x_blk, [(w_z, t_a, n_a), (w_x, t_b, n_b)], two)
+        g_a = chunk_outputs(who, u_a, z_a, bc, (cum3, nexc3), (tail1, tail2), (gloc_a, suf_a, ut_a, vf_a), got_a, logs, skip, three, 0, 2 * n_a)
         got_g_a = send(g_a)
-        three, = later((three,), g_a[0])
         w_three = plane(three)
-        gloc_b, suf_b, s_fwd, s_bwd, ut_b, vf_b = chunk_states(u_b, bc, (cum3, nexc3, dt3), three, head_b, 2 * n_b)
+        gloc_b, suf_b, s_fwd, s_bwd, ut_b, vf_b = chunk_states(u_b, bc, (cum3, nexc3, dt3), g_a[0], head_b, 2 * n_b)
         got_b = exchange(s_fwd, s_bwd)
         z_b, = project(x_blk, [(w_z, t_b, n_b)], s_fwd)
         g_b = chunk_outputs(who, u_b, z_b, bc, (cum3, nexc3), (tail1, tail2), (gloc_b, suf_b, ut_b, vf_b), got_b, logs, skip, z_b, head_b, 2 * n_b)
         got_g_b = send(g_b)
 
-        own = lax.dynamic_slice_in_dim(x_blk, tp_index * rows_out, rows_out, axis=0)
-        total = add_products(own, [(got_g_a[0], w_out, t_a), (got_g_b[0], w_out, t_b)], F32)
-        total = add_products(total, [(got_g_a[1], w_one, t_a), (got_g_a[2], w_two, t_a)], F32)
-        total = add_products(total, [(got_g_a[3], w_three, t_a), (got_g_b[1], w_one, t_b)], F32)
-        return add_products(total, [(got_g_b[2], w_two, t_b), (got_g_b[3], w_three, t_b)], BF16)
+        w_one, w_two, w_three = [whole(half) for half in later((w_one, w_two, w_three), g_b[0])]
+        total = add_products(who, x_blk, [(got_g_a[0], w_out, t_a), (got_g_b[0], w_out, t_b)], F32)
+        total = add_products(who, total, [(got_g_a[1], w_one, t_a), (got_g_a[2], w_two, t_a), (got_g_a[3], w_three, t_a)], F32)
+        total = add_products(who, total, [(got_g_b[1], w_one, t_b), (got_g_b[2], w_two, t_b)], F32)
+        return add_products(who, total, [(got_g_b[3], w_three, t_b)], BF16)
 
     in_specs = (P(('dp', 'sp'), None), P(None, 'tp'), P(None, 'tp'), P(None, None), P(None, 'tp'), P('tp'), P('tp'), P('tp'), P('tp', None))
     out_specs = P(('dp', 'sp', 'tp'), None)

time: 276 us -> 336 us (1.22)
  the two profiles are of different devices: /device:TPU:10 before, /device:TPU:9 now
where the time goes in v3:
time: 336 us; the launch traced here: 335 us
  waiting for transfers between devices  142 us (42%)
  Pallas kernels  128 us (38%)
  starting transfers between devices  19.7 us (6%)
  other arithmetic  18.5 us (6%)
  local copies, waits for them, and re-layouts  13.4 us (4%)
  between operations  13.4 us (4%)
    ppermute x21, waiting for transfers between devices, swap(): return lax.ppermute(val, axis, [(i, i ^ slot) for i in range(4)])  99.5 us
    all_gather x3, waiting for transfers between devices, plane(): lax.all_gather(v, ('dp', 'sp'), tiled=True, axis_index_groups=[[0, 2, 4,...  41.8 us
    pallas_call x2, Pallas kernels, chunk_outputs(): pl.pallas_call(functools.partial(out_kernel, first_head, n_pairs), grid_s...  32.8 us
    pallas_call x2, Pallas kernels, project(): pl.pallas_call(functools.partial(proj_kernel, counts), grid=(tokens // ti...  31.6 us
    pallas_call x4, Pallas kernels, add_products(): pl.pallas_call(body, grid_spec=pltpu.PrefetchScalarGridSpec(num_scalar_pr...  25.5 us
    pallas_call x2, Pallas kernels, chunk_states(): pl.pallas_call(body, grid=(last + 1,), in_specs=[tok(width), tok(2 * LANE...  19.8 us
    ppermute x21, starting transfers between devices, swap(): return lax.ppermute(val, axis, [(i, i ^ slot) for i in range(4)])  19.7 us
    pallas_call x1, Pallas kernels, prep(): pl.pallas_call(functools.partial(prep_kernel, n_tiles), grid=(tokens // t...  17.9 us
  transfers between devices with their start and end apart: 24, of which 8 were waited for; matrix products, arithmetic and copies ran while one was open for 6% of the time, Pallas kernels for 37%

profile of v3, /device:TPU:9, one launch (start us, length us, event | category | flops | bytes accessed | tf_op | source)
XLA Modules:
  0.0 334.7 jit_solution(18066421220509284053)
XLA Ops:
  6.5 2.1 constant_dynamic-slice_fusion
  8.6 2.5 collective-permute-start
  11.1 17.9 %prep.1 = (bf16[2048,256]{1,0:T(8,128)(2,1)}, bf16[2048,128]{1,0:T(8,128)(2,1)}, bf16[2048,128]{1,0:T(8,128)(2,1)}, bf16[2048,128]{1,0:T(8,128)(2,1)}, bf16[320,...) custom-call(bf16[2048,2560]{1,0:T(8,128)(2,1)} %refs_0_.7, ...), custom_call_target="tpu_custom_call" | custom-call | flops 10737418240 | bytes 10485760 | tf_op jit(solution)/shard_map/prep/pallas_call | solution.py:290
  29.1 14.5 %collective-permute-done.1.after_ref = bf16[160,2560]{1,0:T(8,128)(2,1)S(1)} collective-permute-done((bf16[160,2560]{1,0:T(8,128)(2,1)}, bf16[160,2560]{1,0:T(8,128)(2,1)S(1)}, u32[]{:S(2)}, u32[]{:S(2)}) %collective-permute-start.1) | collective-permute-done | bytes 819232 | tf_op jit(solution)/shard_map/ppermute | solution.py:396
  44.5 8.8 %states.2 = (f32[16,128,512]{2,1,0:T(8,128)}, f32[16,8,512]{2,1,0:T(8,128)}, bf16[128,512]{1,0:T(8,128)(2,1)}, bf16[128,512]{1,0:T(8,128)(2,1)}, bf16[2048,512]{1,0:T(8,128)(2,1)}, /*index=5*/bf16[2048,512]{1,0:T(8,128)(2,1)}) custom-call(bf16[2048,512]{1,0:T(8,128)(2,1)} %get-tuple-element.40.u_ref, bf16[2048,256]{1,0:T(8,128)(2,1)} %get-tuple-element.41.bc_ref, ...), custom_call_target="tpu_custom_call" | custom-call | flops 4294967296 | bytes 8388608 | tf_op jit(solution)/shard_map/states/pallas_call | solution.py:354
  54.1 2.3 collective-permute-start.8
  56.4 17.8 %collective-permute-done.8.after_ref = bf16[160,2560]{1,0:T(8,128)(2,1)S(1)} collective-permute-done((bf16[160,2560]{1,0:T(8,128)(2,1)}, bf16[160,2560]{1,0:T(8,128)(2,1)S(1)}, u32[]{:S(2)}, u32[]{:S(2)}) %collective-permute-start.8) | collective-permute-done | bytes 819232 | tf_op jit(solution)/shard_map/ppermute | solution.py:396
  75.1 1.7 collective-permute-start.5
  82.3 18.9 %project.2 = (bf16[2048,512]{1,0:T(8,128)(2,1)}, bf16[2048,768]{1,0:T(8,128)(2,1)}) custom-call(bf16[2048,2560]{1,0:T(8,128)(2,1)} %refs_0_.7, bf16[2560,1280]{1,0:T(8,128)(2,1)} %refs_2_.4, bf16[2560,1280]{1,0:T(8,128)(2,1)} %refs_2_.4, bf16[2560,1280]{1,0:T(8,128)(2,1)} %refs_4_.1, bf16[2560,1280]{1,0:T(8,128)(2,1)} %refs_4_.1, ...), custom_call_target="tpu_custom_call" | custom-call | flops 13421772800 | bytes 10485760 | tf_op jit(solution)/shard_map/project/pallas_call | solution.py:308
  102.0 14.6 %outputs.2 = (bf16[512,512]{1,0:T(8,128)(2,1)}, bf16[512,512]{1,0:T(8,128)(2,1)}, bf16[512,512]{1,0:T(8,128)(2,1)}, bf16[512,512]{1,0:T(8,128)(2,1)}) custom-call(s32[2]{0:T(128)} %pad_add_fusion.who_ref, bf16[2048,512]{1,0:T(8,128)(2,1)} %get-tuple-element.40.u_ref, bf16[2048,512]{1,0:T(8,128)(2,1)} %get-tuple-element.49.z_ref, ...), custom_call_target="tpu_custom_call" | custom-call | flops 6442450944 | bytes 8388608 | tf_op jit(solution)/shard_map/outputs/pallas_call | solution.py:376
  116.6 11.0 %states.3 = (f32[16,128,768]{2,1,0:T(8,128)}, f32[16,8,768]{2,1,0:T(8,128)}, bf16[128,768]{1,0:T(8,128)(2,1)}, bf16[128,768]{1,0:T(8,128)(2,1)}, bf16[2048,768]{1,0:T(8,128)(2,1)}, /*index=5*/bf16[2048,768]{1,0:T(8,128)(2,1)}) custom-call(bf16[2048,768]{1,0:T(8,128)(2,1)} %get-tuple-element.58.u_ref, bf16[2048,256]{1,0:T(8,128)(2,1)} %get-tuple-element.41.bc_ref, ...), custom_call_target="tpu_custom_call" | custom-call | flops 6442450944 | bytes 12582912 | tf_op jit(solution)/shard_map/states/pallas_call | solution.py:354
  128.7 1.2 collective-permute-start.10
  130.6 12.7 %project.3.z_ref.after_ref = bf16[2048,768]{1,0:T(8,128)(2,1)} custom-call(bf16[2048,2560]{1,0:T(8,128)(2,1)} %refs_0_.7, bf16[2560,1280]{1,0:T(8,128)(2,1)} %refs_2_.4, bf16[2560,1280]{1,0:T(8,128)(2,1)} %refs_2_.4, bf16[2560,1280]{1,0:T(8,128)(2,1)} %refs_2_.4, bf16[128,768]{1,0:T(8,128)(2,1)} %get-tuple-element.59.refs_3_), custom_call_target="tpu_custom_call" | custom-call | flops 8053063680 | bytes 10485760 | tf_op jit(solution)/shard_map/project/pallas_call | solution.py:308
  143.3 1.2 collective-permute-done.11.r3_ref
  145.3 18.2 %outputs.3 = (bf16[512,768]{1,0:T(8,128)(2,1)}, bf16[512,768]{1,0:T(8,128)(2,1)}, bf16[512,768]{1,0:T(8,128)(2,1)}, bf16[512,768]{1,0:T(8,128)(2,1)}) custom-call(s32[2]{0:T(128)} %pad_add_fusion.who_ref, bf16[2048,768]{1,0:T(8,128)(2,1)} %get-tuple-element.58.u_ref, bf16[2048,768]{1,0:T(8,128)(2,1)} %project.3.z_ref.after_ref, ...), custom_call_target="tpu_custom_call" | custom-call | flops 9663676416 | bytes 12582912 | tf_op jit(solution)/shard_map/outputs/pallas_call | solution.py:376
  163.6 41.8 %all-gather.8.cloned.1.call-done = bf16[640,2560]{1,0:T(8,128)(2,1)} async-done(((bf16[160,2560]{1,0:T(8,128)(2,1)}), bf16[640,2560]{1,0:T(8,128)(2,1)}) %all-gather.8.cloned.1.call-update) | async-done | bytes 3276816 | tf_op jit(solution)/shard_map/all_gather | solution.py:415
  207.0 2.1 collective-permute-start.14
  209.1 2.9 copy-done
  212.0 4.0 %copy-done.1 = bf16[2048,2560]{1,0:T(8,128)(2,1)S(1)} copy-done((bf16[2048,2560]{1,0:T(8,128)(2,1)S(1)}, bf16[2048,2560]{1,0:T(8,128)(2,1)}, u32[]{:S(2)}) %copy-start.1) | copy-done | bytes 10485784
  217.1 5.8 %add_products.4.refs_0_ = f32[512,2560]{1,0:T(8,128)S(1)} custom-call(s32[2]{0:T(128)S(1)} %copy-done.4, bf16[2048,2560]{1,0:T(8,128)(2,1)S(1)} %copy-done.1, bf16[512,512]{1,0:T(8,128)(2,1)S(1)} %copy-done.3, bf16[1280,2560]{1,0:T(8,128)(2,1)S(1)} %copy-done, bf16[1280,2560]{1,0:T(8,128)(2,1)S(1)} %copy-done, bf16[512,768]{1,0:T(8,128)(2,1)S(1)} %copy-done.2, ...), custom_call_target="tpu_custom_call" | custom-call | flops 3355443200 | bytes 2621440 | tf_op jit(solution)/shard_map/add_products/pallas_call | solution.py:334
  223.3 6.9 %maximum_select_fusion.2.refs_8_.refs_9_.refs_2_.refs_3_.refs_4_ = bf16[1280,2560]{1,0:T(8,128)(2,1)} fusion(bf16[640,2560]{1,0:T(8,128)(2,1)} %collective-permute-done.17, bf16[640,2560]{1,0:T(8,128)(2,1)S(1)} %copy-done.7, pred[]{:T(512)S(6)} %eq.8), kind=kLoop, calls=%fused_computation.2 | loop fusion | flops 29491200 | bytes 13107201 | tf_op jit(solution)/shard_map/jit(_where)/select_n | solution.py:419
  230.2 1.2 collective-permute-start.18
  231.4 4.6 %maximum_select_fusion.1.refs_5_.refs_6_.refs_7_.refs_8_ = bf16[1280,2560]{1,0:T(8,128)(2,1)S(1)} fusion(bf16[640,2560]{1,0:T(8,128)(2,1)} %collective-permute-done.15, bf16[640,2560]{1,0:T(8,128)(2,1)S(1)} %copy-done.6, pred[]{:T(512)S(6)} %eq.8), kind=kLoop, calls=%fused_computation.1 | loop fusion | flops 29491200 | bytes 13107201 | tf_op jit(solution)/shard_map/jit(_where)/select_n | solution.py:419
  236.0 2.0 collective-permute-start.19
  238.1 4.4 %maximum_select_fusion.refs_2_.refs_3_.refs_4_ = bf16[1280,2560]{1,0:T(8,128)(2,1)S(1)} fusion(bf16[640,2560]{1,0:T(8,128)(2,1)} %collective-permute-done.13, bf16[640,2560]{1,0:T(8,128)(2,1)S(1)} %copy-done.5, pred[]{:T(512)S(6)} %eq.8), kind=kLoop, calls=%fused_computation | loop fusion | flops 29491200 | bytes 13107201 | tf_op jit(solution)/shard_map/jit(_where)/select_n | solution.py:419
  242.5 13.1 %collective-permute-done.16.refs_7_ = bf16[512,512]{1,0:T(8,128)(2,1)S(1)} collective-permute-done((bf16[512,512]{1,0:T(8,128)(2,1)S(1)}, bf16[512,512]{1,0:T(8,128)(2,1)S(1)}, u32[]{:S(2)}, u32[]{:S(2)}) %collective-permute-start.16) | collective-permute-done | bytes 524320 | tf_op jit(solution)/shard_map/ppermute | solution.py:396
  255.6 7.9 %add_products.5.refs_0_ = f32[512,2560]{1,0:T(8,128)S(1)} custom-call(s32[2]{0:T(128)S(1)} %copy-done.4, f32[512,2560]{1,0:T(8,128)S(1)} %add_products.4.refs_0_, bf16[512,512]{1,0:T(8,128)(2,1)S(1)} %collective-permute-done.12.refs_1_, bf16[1280,2560]{1,0:T(8,128)(2,1)S(1)} %maximum_select_fusion.refs_2_.refs_3_.refs_4_, ...), custom_call_target="tpu_custom_call" | custom-call | flops 4026531840 | bytes 2621440 | tf_op jit(solution)/shard_map/add_products/pallas_call | solution.py:334
  263.5 1.8 collective-permute-done.18.refs_1_
  265.3 39.4 %collective-permute-done.19.refs_5_ = bf16[512,768]{1,0:T(8,128)(2,1)S(1)} collective-permute-done((bf16[512,768]{1,0:T(8,128)(2,1)S(1)}, bf16[512,768]{1,0:T(8,128)(2,1)S(1)}, u32[]{:S(2)}, u32[]{:S(2)}) %collective-permute-start.19) | collective-permute-done | bytes 786464 | tf_op jit(solution)/shard_map/ppermute | solution.py:396
  304.7 6.7 %add_products.6.refs_0_ = f32[512,2560]{1,0:T(8,128)S(1)} custom-call(s32[2]{0:T(128)S(1)} %copy-done.4, f32[512,2560]{1,0:T(8,128)S(1)} %add_products.5.refs_0_, bf16[512,768]{1,0:T(8,128)(2,1)S(1)} %collective-permute-done.18.refs_1_, bf16[1280,2560]{1,0:T(8,128)(2,1)S(1)} %maximum_select_fusion.refs_2_.refs_3_.refs_4_, ...), custom_call_target="tpu_custom_call" | custom-call | flops 4026531840 | bytes 2621440 | tf_op jit(solution)/shard_map/add_products/pallas_call | solution.py:334
  311.5 11.6 %collective-permute-done.20.refs_1_ = bf16[512,768]{1,0:T(8,128)(2,1)S(1)} collective-permute-done((bf16[512,768]{1,0:T(8,128)(2,1)S(1)}, bf16[512,768]{1,0:T(8,128)(2,1)S(1)}, u32[]{:S(2)}, u32[]{:S(2)}) %collective-permute-start.20) | collective-permute-done | bytes 786464 | tf_op jit(solution)/shard_map/ppermute | solution.py:396
  323.1 5.0 %add_products.7 = bf16[512,2560]{1,0:T(8,128)(2,1)} custom-call(s32[2]{0:T(128)S(1)} %copy-done.4, f32[512,2560]{1,0:T(8,128)S(1)} %add_products.6.refs_0_, bf16[512,768]{1,0:T(8,128)(2,1)S(1)} %collective-permute-done.20.refs_1_, bf16[1280,2560]{1,0:T(8,128)(2,1)S(1)} %bitcast.7, bf16[1280,2560]{1,0:T(8,128)(2,1)S(1)} %bitcast.7, bf16[1280,2560]{1,0:T(8,128)(2,1)S(1)} %bitcast.7), custom_call_target="tpu_custom_call" | custom-call | flops 2013265920 | bytes 2621440 | tf_op jit(solution)/shard_map/add_products/pallas_call | solution.py:334
  (88 shorter events, 14.7 us)
Async XLA Ops:
  6.5 157.0 %all-gather.6.cloned.1.call-start = ((), (), s32[]{:S(2)}) async-start(), calls=%async_computation.1 | async-start | bytes 4096000 | tf_op jit(solution)/shard_map/all_gather | solution.py:415
  8.6 35.0 %collective-permute-start.1 = (bf16[160,2560]{1,0:T(8,128)(2,1)}, bf16[160,2560]{1,0:T(8,128)(2,1)S(1)}, u32[]{:S(2)}, u32[]{:S(2)}) collective-permute-start(bf16[160,2560]{1,0:T(8,128)(2,1)} %constant_dynamic-slice_fusion), channel_id=1, source_target_pairs={{0,4},{4,0},{8,12},{12,8},{1,5},{5,1},{9,13},{13,9},{2,6},{6,2},{1... | collective-permute-start | bytes 2457608 | tf_op jit(solution)/shard_map/ppermute | solution.py:396
  8.6 44.6 %collective-permute-start = (bf16[160,2560]{1,0:T(8,128)(2,1)}, bf16[160,2560]{1,0:T(8,128)(2,1)}, u32[]{:S(2)}, u32[]{:S(2)}) collective-permute-start(bf16[160,2560]{1,0:T(8,128)(2,1)} %constant_dynamic-slice_fusion), channel_id=1, source_target_pairs={{0,8},{4,12},{8,0},{12,4},{1,9},{5,13},{9,1},{13,5},{2,10},{6,14},... | collective-permute-start | bytes 2457608 | tf_op jit(solution)/shard_map/ppermute | solution.py:396
  44.5 30.6 %copy-start.22 = (f32[8,128]{1,0:T(8,128)S(1)}, f32[8,128]{1,0:T(8,128)}, u32[]{:S(2)}) copy-start(f32[8,128]{1,0:T(8,128)} %get-tuple-element.45) | copy-start | bytes 12292
  53.3 110.3 %all-gather.4.cloned.1.call-start = ((), (), s32[]{:S(2)}) async-start(), calls=%async_computation | async-start | bytes 4096000 | tf_op jit(solution)/shard_map/all_gather | solution.py:415
  54.1 151.3 %all-gather.8.cloned.1.call-start = ((), (), s32[]{:S(2)}) async-start(), calls=%async_computation.2 | async-start | bytes 4096000 | tf_op jit(solution)/shard_map/all_gather | solution.py:415
  54.1 20.1 %collective-permute-start.8 = (bf16[160,2560]{1,0:T(8,128)(2,1)}, bf16[160,2560]{1,0:T(8,128)(2,1)S(1)}, u32[]{:S(2)}, u32[]{:S(2)}) collective-permute-start(bf16[160,2560]{1,0:T(8,128)(2,1)} %collective-permute-done.refs_5_), channel_id=1, source_target_pairs={{0,4},{4,0},{8,12},{12,8},{1,5},{5,1},{9,13},{13,9},{2,6},{6,2},{1... | collective-permute-start | bytes 2457608 | tf_op jit(solution)/shard_map/ppermute | solution.py:396
  75.1 6.3 %collective-permute-start.5 = (f32[8,128]{1,0:T(8,128)S(1)}, f32[8,128]{1,0:T(8,128)S(1)}, u32[]{:S(2)}, u32[]{:S(2)}) collective-permute-start(f32[8,128]{1,0:T(8,128)S(1)} %copy-done.22), channel_id=1, source_target_pairs={{0,1},{1,0},{2,3},{3,2},{4,5},{5,4},{6,7},{7,6},{8,9},{9,8},{10,11... | collective-permute-start | bytes 12296 | tf_op jit(solution)/shard_map/ppermute | solution.py:396
  76.8 24.4 %collective-permute-start.6 = (f32[8,128]{1,0:T(8,128)S(1)}, f32[8,128]{1,0:T(8,128)S(1)}, u32[]{:S(2)}, u32[]{:S(2)}) collective-permute-start(f32[8,128]{1,0:T(8,128)S(1)} %copy-done.22), channel_id=1, source_target_pairs={{0,2},{1,3},{2,0},{3,1},{4,6},{5,7},{6,4},{7,5},{8,10},{9,11},{10,... | collective-permute-start | bytes 12296 | tf_op jit(solution)/shard_map/ppermute | solution.py:396
  77.9 23.3 %collective-permute-start.7 = (f32[8,128]{1,0:T(8,128)S(1)}, f32[8,128]{1,0:T(8,128)S(1)}, u32[]{:S(2)}, u32[]{:S(2)}) collective-permute-start(f32[8,128]{1,0:T(8,128)S(1)} %copy-done.22), channel_id=1, source_target_pairs={{0,3},{1,2},{2,1},{3,0},{4,7},{5,6},{6,5},{7,4},{8,11},{9,10},{10,... | collective-permute-start | bytes 12296 | tf_op jit(solution)/shard_map/ppermute | solution.py:396
  80.1 21.2 %collective-permute-start.2 = (bf16[128,512]{1,0:T(8,128)(2,1)S(1)}, bf16[128,512]{1,0:T(8,128)(2,1)S(1)}, u32[]{:S(2)}, u32[]{:S(2)}) collective-permute-start(bf16[128,512]{1,0:T(8,128)(2,1)S(1)} %get-tuple-element.80), channel_id=1, source_target_pairs={{0,1},{1,0},{2,3},{3,2},{4,5},{5,4},{6,7},{7,6},{8,9},{9,8},{10,11... | collective-permute-start | bytes 393224 | tf_op jit(solution)/shard_map/ppermute | solution.py:396
  80.3 21.0 %collective-permute-start.3 = (bf16[128,512]{1,0:T(8,128)(2,1)S(1)}, bf16[128,512]{1,0:T(8,128)(2,1)S(1)}, u32[]{:S(2)}, u32[]{:S(2)}) collective-permute-start(bf16[128,512]{1,0:T(8,128)(2,1)S(1)} %get-tuple-element.79), channel_id=1, source_target_pairs={{0,2},{1,3},{2,0},{3,1},{4,6},{5,7},{6,4},{7,5},{8,10},{9,11},{10,... | collective-permute-start | bytes 393224 | tf_op jit(solution)/shard_map/ppermute | solution.py:396
  81.5 19.8 %copy-start.19 = (f32[8,128]{1,0:T(8,128)}, f32[8,128]{1,0:T(8,128)S(1)}, u32[]{:S(2)}) copy-start(f32[8,128]{1,0:T(8,128)S(1)} %collective-permute-done.5.l1_ref) | copy-start | bytes 12292
  81.5 19.8 %collective-permute-start.4 = (bf16[128,512]{1,0:T(8,128)(2,1)S(1)}, bf16[128,512]{1,0:T(8,128)(2,1)S(1)}, u32[]{:S(2)}, u32[]{:S(2)}) collective-permute-start(bf16[128,512]{1,0:T(8,128)(2,1)S(1)} %get-tuple-element.78), channel_id=1, source_target_pairs={{0,3},{1,2},{2,1},{3,0},{4,7},{5,6},{6,5},{7,4},{8,11},{9,10},{10,... | collective-permute-start | bytes 393224 | tf_op jit(solution)/shard_map/ppermute | solution.py:396
  128.7 14.6 %collective-permute-start.10 = (bf16[128,768]{1,0:T(8,128)(2,1)S(1)}, bf16[128,768]{1,0:T(8,128)(2,1)S(1)}, u32[]{:S(2)}, u32[]{:S(2)}) collective-permute-start(bf16[128,768]{1,0:T(8,128)(2,1)S(1)} %get-tuple-element.76), channel_id=1, source_target_pairs={{0,2},{1,3},{2,0},{3,1},{4,6},{5,7},{6,4},{7,5},{8,10},{9,11},{10,... | collective-permute-start | bytes 589832 | tf_op jit(solution)/shard_map/ppermute | solution.py:396
  129.9 14.6 %collective-permute-start.11 = (bf16[128,768]{1,0:T(8,128)(2,1)S(1)}, bf16[128,768]{1,0:T(8,128)(2,1)S(1)}, u32[]{:S(2)}, u32[]{:S(2)}) collective-permute-start(bf16[128,768]{1,0:T(8,128)(2,1)S(1)} %get-tuple-element.75), channel_id=1, source_target_pairs={{0,3},{1,2},{2,1},{3,0},{4,7},{5,6},{6,5},{7,4},{8,11},{9,10},{10,... | collective-permute-start | bytes 589832 | tf_op jit(solution)/shard_map/ppermute | solution.py:396
  130.6 13.9 %collective-permute-start.9 = (bf16[128,768]{1,0:T(8,128)(2,1)S(1)}, bf16[128,768]{1,0:T(8,128)(2,1)S(1)}, u32[]{:S(2)}, u32[]{:S(2)}) collective-permute-start(bf16[128,768]{1,0:T(8,128)(2,1)S(1)} %get-tuple-element.77), channel_id=1, source_target_pairs={{0,1},{1,0},{2,3},{3,2},{4,5},{5,4},{6,7},{7,6},{8,9},{9,8},{10,11... | collective-permute-start | bytes 589832 | tf_op jit(solution)/shard_map/ppermute | solution.py:396
  145.3 63.8 %copy-start.3 = (bf16[512,512]{1,0:T(8,128)(2,1)S(1)}, bf16[512,512]{1,0:T(8,128)(2,1)}, u32[]{:S(2)}) copy-start(bf16[512,512]{1,0:T(8,128)(2,1)} %get-tuple-element.57.after_ref.refs_1_) | copy-start | bytes 1572868
  145.3 63.8 %copy-start.4 = (s32[2]{0:T(128)S(1)}, s32[2]{0:T(128)}, u32[]{:S(2)}) copy-start(s32[2]{0:T(128)} %pad_add_fusion.who_ref) | copy-start | bytes 28
  205.4 17.6 %collective-permute-start.17 = (bf16[640,2560]{1,0:T(8,128)(2,1)}, bf16[640,2560]{1,0:T(8,128)(2,1)}, u32[]{:S(2)}, u32[]{:S(2)}) collective-permute-start(bf16[640,2560]{1,0:T(8,128)(2,1)} %all-gather.8.cloned.1.call-done), channel_id=1, source_target_pairs={{0,1},{1,0},{2,3},{3,2},{4,5},{5,4},{6,7},{7,6},{8,9},{9,8},{10,11... | collective-permute-start | bytes 9830408 | tf_op jit(solution)/shard_map/ppermute | solution.py:396
  206.2 23.9 %collective-permute-start.15 = (bf16[640,2560]{1,0:T(8,128)(2,1)}, bf16[640,2560]{1,0:T(8,128)(2,1)}, u32[]{:S(2)}, u32[]{:S(2)}) collective-permute-start(bf16[640,2560]{1,0:T(8,128)(2,1)} %all-gather.6.cloned.1.call-done), channel_id=1, source_target_pairs={{0,1},{1,0},{2,3},{3,2},{4,5},{5,4},{6,7},{7,6},{8,9},{9,8},{10,11... | collective-permute-start | bytes 9830408 | tf_op jit(solution)/shard_map/ppermute | solution.py:396
  206.2 31.8 %collective-permute-start.13 = (bf16[640,2560]{1,0:T(8,128)(2,1)}, bf16[640,2560]{1,0:T(8,128)(2,1)}, u32[]{:S(2)}, u32[]{:S(2)}) collective-permute-start(bf16[640,2560]{1,0:T(8,128)(2,1)} %all-gather.4.cloned.1.call-done), channel_id=1, source_target_pairs={{0,1},{1,0},{2,3},{3,2},{4,5},{5,4},{6,7},{7,6},{8,9},{9,8},{10,11... | collective-permute-start | bytes 9830408 | tf_op jit(solution)/shard_map/ppermute | solution.py:396
  206.7 29.2 %collective-permute-start.12 = (bf16[512,512]{1,0:T(8,128)(2,1)}, bf16[512,512]{1,0:T(8,128)(2,1)S(1)}, u32[]{:S(2)}, u32[]{:S(2)}) collective-permute-start(bf16[512,512]{1,0:T(8,128)(2,1)} %get-tuple-element.66), channel_id=1, source_target_pairs={{0,4},{4,0},{8,12},{12,8},{1,5},{5,1},{9,13},{13,9},{2,6},{6,2},{1... | collective-permute-start | bytes 1572872 | tf_op jit(solution)/shard_map/ppermute | solution.py:396
  207.0 35.5 %collective-permute-start.14 = (bf16[512,512]{1,0:T(8,128)(2,1)}, bf16[512,512]{1,0:T(8,128)(2,1)S(1)}, u32[]{:S(2)}, u32[]{:S(2)}) collective-permute-start(bf16[512,512]{1,0:T(8,128)(2,1)} %get-tuple-element.68), channel_id=1, source_target_pairs={{0,8},{4,12},{8,0},{12,4},{1,9},{5,13},{9,1},{13,5},{2,10},{6,14},... | collective-permute-start | bytes 1572872 | tf_op jit(solution)/shard_map/ppermute | solution.py:396
  222.9 8.4 %copy-start.6 = (bf16[640,2560]{1,0:T(8,128)(2,1)S(1)}, bf16[640,2560]{1,0:T(8,128)(2,1)}, u32[]{:S(2)}) copy-start(bf16[640,2560]{1,0:T(8,128)(2,1)} %all-gather.6.cloned.1.call-done) | copy-start | bytes 9830404
  223.0 32.7 %collective-permute-start.16 = (bf16[512,512]{1,0:T(8,128)(2,1)S(1)}, bf16[512,512]{1,0:T(8,128)(2,1)S(1)}, u32[]{:S(2)}, u32[]{:S(2)}) collective-permute-start(bf16[512,512]{1,0:T(8,128)(2,1)S(1)} %copy-done.12), channel_id=1, source_target_pairs={{0,12},{4,8},{8,4},{12,0},{1,13},{5,9},{9,5},{13,1},{2,14},{6,10},... | collective-permute-start | bytes 1572872 | tf_op jit(solution)/shard_map/ppermute | solution.py:396
  230.2 7.9 %copy-start.5 = (bf16[640,2560]{1,0:T(8,128)(2,1)S(1)}, bf16[640,2560]{1,0:T(8,128)(2,1)}, u32[]{:S(2)}) copy-start(bf16[640,2560]{1,0:T(8,128)(2,1)} %all-gather.4.cloned.1.call-done) | copy-start | bytes 9830404
  230.2 35.2 %collective-permute-start.18 = (bf16[512,768]{1,0:T(8,128)(2,1)}, bf16[512,768]{1,0:T(8,128)(2,1)S(1)}, u32[]{:S(2)}, u32[]{:S(2)}) collective-permute-start(bf16[512,768]{1,0:T(8,128)(2,1)} %get-tuple-element.72), channel_id=1, source_target_pairs={{0,4},{4,0},{8,12},{12,8},{1,5},{5,1},{9,13},{13,9},{2,6},{6,2},{1... | collective-permute-start | bytes 2359304 | tf_op jit(solution)/shard_map/ppermute | solution.py:396
  236.0 68.7 %collective-permute-start.19 = (bf16[512,768]{1,0:T(8,128)(2,1)S(1)}, bf16[512,768]{1,0:T(8,128)(2,1)S(1)}, u32[]{:S(2)}, u32[]{:S(2)}) collective-permute-start(bf16[512,768]{1,0:T(8,128)(2,1)S(1)} %copy-done.11), channel_id=1, source_target_pairs={{0,8},{4,12},{8,0},{12,4},{1,9},{5,13},{9,1},{13,5},{2,10},{6,14},... | collective-permute-start | bytes 2359304 | tf_op jit(solution)/shard_map/ppermute | solution.py:396
  238.0 85.1 %collective-permute-start.20 = (bf16[512,768]{1,0:T(8,128)(2,1)S(1)}, bf16[512,768]{1,0:T(8,128)(2,1)S(1)}, u32[]{:S(2)}, u32[]{:S(2)}) collective-permute-start(bf16[512,768]{1,0:T(8,128)(2,1)S(1)} %copy-done.10), channel_id=1, source_target_pairs={{0,12},{4,8},{8,4},{12,0},{1,13},{5,9},{9,5},{13,1},{2,14},{6,10},... | collective-permute-start | bytes 2359304 | tf_op jit(solution)/shard_map/ppermute | solution.py:396
  255.6 67.5 %slice-start = ((s8[6553600]{0:T(1024)(128)(4,1)}), s8[4194304]{0:T(1024)(128)(4,1)S(1)}, s32[]{:S(2)}) async-start(s8[6553600]{0:T(1024)(128)(4,1)} %bitcast.6), calls=%async_computation.3 | async-start | bytes 8388608
  263.5 59.6 %slice-start.1 = ((s8[6553600]{0:T(1024)(128)(4,1)}), s8[2359296]{0:T(1024)(128)(4,1)S(1)}, s32[]{:S(2)}) async-start(s8[6553600]{0:T(1024)(128)(4,1)} %bitcast.6), calls=%async_computation.4 | async-start | bytes 4718592
  (17 other events, 41.4 us)
Sparse Core Ops, SparseCore 0:
  53.4 52.8 all-gather.5
  108.2 49.3 all-gather.3
  159.5 45.8 all-gather.7

commit v4 on v3

--- a/solution.py
+++ b/solution.py
@@ -28,7 +28,8 @@
 
 
 def prep_kernel(n_tiles, x_ref, wbc_ref, wdt_ref, bias_ref, a_ref, *refs):
-    bc_ref, cum_ref, nexc_ref, dt_ref, tail1_ref, tail2_ref, log_ref, u_ref, w_buf, par, pick = refs[n_tiles:]
+    bc_ref, cum_ref, nexc_ref, dt_ref, tail1_ref, tail2_ref, log_ref, u_ref = refs[n_tiles:n_tiles + 8]
+    w_buf, par, pick = refs[-8:-5]
     heads = bias_ref.shape[1]
     row = lax.broadcasted_iota(jnp.int32, (CHUNK, LANES), 0)
     lane = lax.broadcasted_iota(jnp.int32, (CHUNK, LANES), 1)
@@ -80,14 +81,21 @@
     tail2_ref[...] = lax.dot_general(pick[...], nexc_ref[...], across, preferred_element_type=F32).astype(BF16)
 
 
-def proj_kernel(counts, x_ref, *refs):
-    x_val = x_ref[...]
-    o_refs = refs[sum(counts) + 1:]
-    k = 0
-    for o_ref, count in zip(o_refs, counts):
-        for i in range(count):
-            o_ref[:, i * 256:(i + 1) * 256] = jnp.dot(x_val, refs[k][...], preferred_element_type=F32).astype(BF16)
-            k += 1
+def first_kernel(n_tiles, *refs):
+    prep_kernel(n_tiles, *refs)
+    bc_ref, cum_ref, nexc_ref, dt_ref, _, _, _, u_ref = refs[5 + n_tiles:13 + n_tiles]
+    state_kernel(0, 2 * n_tiles, u_ref, bc_ref, cum_ref, nexc_ref, dt_ref, *refs[13 + n_tiles:-8], *refs[-5:])
+
+
+def next_kernel(first_head, n_tiles, x_ref, bc_ref, cum_ref, nexc_ref, dt_ref, *refs):
+    u_ref = refs[n_tiles + 1]
+    project_into(u_ref, x_ref[...], refs[:n_tiles])
+    state_kernel(first_head, 2 * n_tiles, u_ref, bc_ref, cum_ref, nexc_ref, dt_ref, *refs[n_tiles + 2:])
+
+
+def project_into(o_ref, x_val, w_refs):
+    for i, w_ref in enumerate(w_refs):
+        o_ref[:, i * 256:(i + 1) * 256] = jnp.dot(x_val, w_ref[...], preferred_element_type=F32).astype(BF16)
 
 
 def sum_kernel(n_tiles, n_pieces, acc_ref, *refs):
@@ -183,8 +191,10 @@
     return fwd, bwd
 
 
-def out_kernel(first_head, n_pairs, who_ref, u_ref, z_ref, ut_ref, vf_ref, bc_ref, cum_ref, nexc_ref, tail1_ref, tail2_ref, gloc_ref, suf_ref, r1_ref, r2_ref, r3_ref, l1_ref, l2_ref, l3_ref, skip_ref, after_ref, o0_ref, o1_ref, o2_ref, o3_ref, f_acc, hb_acc, skip_buf, g_buf, spread, pick, fwd_buf, bwd_buf):
+def out_kernel(first_head, n_pairs, who_ref, u_ref, x_ref, ut_ref, vf_ref, bc_ref, cum_ref, nexc_ref, tail1_ref, tail2_ref, gloc_ref, suf_ref, r1_ref, r2_ref, r3_ref, l1_ref, l2_ref, l3_ref, skip_ref, after_ref, *refs):
+    w_refs, (o0_ref, o1_ref, o2_ref, o3_ref, f_acc, hb_acc, skip_buf, g_buf, spread, pick, fwd_buf, bwd_buf, z_ref) = refs[:n_pairs // 2], refs[n_pairs // 2:]
     step = pl.program_id(0)
+    project_into(z_ref, x_ref[...], w_refs)
 
     @pl.when(step == 0)
     def _():
@@ -279,42 +289,55 @@
     return [pl.BlockSpec((w.shape[0], 256), functools.partial(lambda t, i: (0, t), first_tile + t), pipeline_mode=pl.Buffered(1)) for t in range(n_tiles)]
 
 
-def prep(x_blk, w_bc, w_dt_rows, bias, a_neg, w_x, n_tiles):
+def state_parts(tokens, width, tok, at):
+    n_chunks = tokens // CHUNK
+    whole = pl.BlockSpec((LANES, width), lambda i: (0, 0))
+    specs = [tok(width), pl.BlockSpec((STATE_CHUNKS, LANES, width), lambda i: (at(i), 0, 0)), pl.BlockSpec((STATE_CHUNKS, 8, width), lambda i: (at(i), 0, 0)), whole, whole, tok(width), tok(width)]
+    shapes = [jax.ShapeDtypeStruct((tokens, width), BF16), jax.ShapeDtypeStruct((n_chunks, LANES, width), F32), jax.ShapeDtypeStruct((n_chunks, 8, width), F32)] + [jax.ShapeDtypeStruct((LANES, width), BF16)] * 2 + [jax.ShapeDtypeStruct((tokens, width), BF16)] * 2
+    scratch = [pltpu.VMEM((LANES, width), F32), pltpu.VMEM((LANES, width), F32), pltpu.VMEM((8, width), F32), pltpu.VMEM((STATE_CHUNKS * CHUNK, 2 * width), BF16), pltpu.VMEM((LANES, width), BF16)]
+    return specs, shapes, scratch
+
+
+def first_group(x_blk, w_bc, w_dt_rows, bias, a_neg, w_x, n_tiles):
     tokens, d_model = x_blk.shape
-    tile = min(512, tokens)
+    tile = STATE_CHUNKS * CHUNK
     width = 256 * n_tiles
+    at = lambda i: tokens // tile - 1 - i
     whole = lambda a: pl.BlockSpec(a.shape, lambda i: (0, 0), pipeline_mode=pl.Buffered(1))
-    tok = lambda w: pl.BlockSpec((tile, w), lambda i: (i, 0))
+    tok = lambda w: pl.BlockSpec((tile, w), lambda i: (at(i), 0))
     heads = bias.shape[1]
-    tail = pl.BlockSpec((16 * heads, tile), lambda i: (0, i))
+    tail = pl.BlockSpec((16 * heads, tile), lambda i: (0, at(i)))
+    specs, shapes, scratch = state_parts(tokens, width, tok, at)
     return pl.pallas_call(
-        functools.partial(prep_kernel, n_tiles),
+        functools.partial(first_kernel, n_tiles),
         grid=(tokens // tile,),
         in_specs=[tok(d_model), whole(w_bc), whole(w_dt_rows), whole(bias), whole(a_neg)] + w_specs(w_x, 0, n_tiles),
-        out_specs=[tok(2 * LANES), tok(LANES), tok(LANES), tok(LANES), tail, tail, pl.BlockSpec((8, LANES), lambda i: (0, 0)), tok(width)],
-        out_shape=[jax.ShapeDtypeStruct((tokens, 2 * LANES), BF16)] + [jax.ShapeDtypeStruct((tokens, LANES), BF16)] * 3 + [jax.ShapeDtypeStruct((16 * heads, tokens), BF16)] * 2 + [jax.ShapeDtypeStruct((8, LANES), F32), jax.ShapeDtypeStruct((tokens, width), BF16)],
-        scratch_shapes=[pltpu.VMEM((LANES, d_model), BF16), pltpu.VMEM((8, LANES), F32), pltpu.VMEM((16 * heads, LANES), BF16)],
+        out_specs=[tok(2 * LANES), tok(LANES), tok(LANES), tok(LANES), tail, tail, pl.BlockSpec((8, LANES), lambda i: (0, 0))] + specs,
+        out_shape=[jax.ShapeDtypeStruct((tokens, 2 * LANES), BF16)] + [jax.ShapeDtypeStruct((tokens, LANES), BF16)] * 3 + [jax.ShapeDtypeStruct((16 * heads, tokens), BF16)] * 2 + [jax.ShapeDtypeStruct((8, LANES), F32)] + shapes,
+        scratch_shapes=[pltpu.VMEM((LANES, d_model), BF16), pltpu.VMEM((8, LANES), F32), pltpu.VMEM((16 * heads, LANES), BF16)] + scratch,
         compiler_params=params(),
-        cost_estimate=cost(2 * tokens * d_model * (512 + width), 2 * tokens * d_model),
-        name="prep",
+        cost_estimate=cost(2 * tokens * d_model * (1024 + width), 2 * tokens * d_model),
+        name="first_group",
     )(x_blk, w_bc, w_dt_rows, bias, a_neg, *([w_x] * n_tiles))
 
 
-def project(x_blk, parts, after):
+def next_group(x_blk, w_x, first_tile, n_tiles, bc, sums, after, first_head):
     tokens, d_model = x_blk.shape
-    tile = min(512, tokens)
-    counts = [n for _, _, n in parts]
-    specs = [spec for w, t, n in parts for spec in w_specs(w, t, n)]
+    tile = STATE_CHUNKS * CHUNK
+    at = lambda i: tokens // tile - 1 - i
+    tok = lambda w: pl.BlockSpec((tile, w), lambda i: (at(i), 0))
+    specs, shapes, scratch = state_parts(tokens, 256 * n_tiles, tok, at)
     return pl.pallas_call(
-        functools.partial(proj_kernel, counts),
+        functools.partial(next_kernel, first_head, n_tiles),
         grid=(tokens // tile,),
-        in_specs=[pl.BlockSpec((tile, d_model), lambda i: (i, 0))] + specs + [ANY],
-        out_specs=[pl.BlockSpec((tile, 256 * n), lambda i: (i, 0)) for n in counts],
-        out_shape=[jax.ShapeDtypeStruct((tokens, 256 * n), BF16) for n in counts],
+        in_specs=[tok(d_model), tok(2 * LANES), tok(LANES), tok(LANES), tok(LANES)] + w_specs(w_x, first_tile, n_tiles) + [ANY],
+        out_specs=specs,
+        out_shape=shapes,
+        scratch_shapes=scratch,
         compiler_params=params(),
-        cost_estimate=cost(512 * tokens * d_model * sum(counts), 2 * tokens * d_model),
-        name="project",
-    )(x_blk, *[w for w, _, n in parts for _ in range(n)], after)
+        cost_estimate=cost(2 * tokens * d_model * (512 + 256 * n_tiles), 2 * tokens * d_model),
+        name="next_group",
+    )(x_blk, bc, *sums, *([w_x] * n_tiles), after)
 
 
 def add_products(who, acc, pieces, out_dtype):
@@ -341,30 +364,7 @@
     )(who, *args)
 
 
-def chunk_states(u, bc, sums, after, first_head, n_pairs):
-    tokens, width = u.shape
-    n_chunks = tokens // CHUNK
-    last = n_chunks // STATE_CHUNKS - 1
-    tok = lambda w: pl.BlockSpec((STATE_CHUNKS * CHUNK, w), lambda i: (last - i, 0))
-    whole = pl.BlockSpec((LANES, width), lambda i: (0, 0))
-
-    def body(u_ref, bc_ref, cum_ref, nexc_ref, dt_ref, after_ref, *refs):
-        state_kernel(first_head, n_pairs, u_ref, bc_ref, cum_ref, nexc_ref, dt_ref, *refs)
-
-    return pl.pallas_call(
-        body,
-        grid=(last + 1,),
-        in_specs=[tok(width), tok(2 * LANES)] + [tok(LANES)] * 3 + [ANY],
-        out_specs=[pl.BlockSpec((STATE_CHUNKS, LANES, width), lambda i: (last - i, 0, 0)), pl.BlockSpec((STATE_CHUNKS, 8, width), lambda i: (last - i, 0, 0)), whole, whole, tok(width), tok(width)],
-        out_shape=[jax.ShapeDtypeStruct((n_chunks, LANES, width), F32), jax.ShapeDtypeStruct((n_chunks, 8, width), F32)] + [jax.ShapeDtypeStruct((LANES, width), BF16)] * 2 + [jax.ShapeDtypeStruct((tokens, width), BF16)] * 2,
-        scratch_shapes=[pltpu.VMEM((LANES, width), F32), pltpu.VMEM((LANES, width), F32), pltpu.VMEM((8, width), F32), pltpu.VMEM((STATE_CHUNKS * CHUNK, 2 * width), BF16), pltpu.VMEM((LANES, width), BF16)],
-        compiler_params=params(),
-        cost_estimate=cost(16 * tokens * width * 256, 8 * tokens * width),
-        name="states",
-    )(u, bc, *sums, after)
-
-
-def chunk_outputs(who, u, z, bc, sums, tails, local, got, logs, skip, after, first_head, n_pairs):
+def chunk_outputs(who, u, x_blk, w_z, first_tile, bc, sums, tails, local, got, logs, skip, after, first_head, n_pairs):
     tokens, width = u.shape
     n_steps = tokens // (OUT_CHUNKS * CHUNK)
     gloc, suf, scaled, ends = local
@@ -378,15 +378,15 @@
         grid_spec=pltpu.PrefetchScalarGridSpec(
             num_scalar_prefetch=1,
             grid=(n_steps,),
-            in_specs=[tok(width)] * 4 + [tok(2 * LANES), tok(LANES), tok(LANES), tail, tail, pl.BlockSpec((OUT_CHUNKS, LANES, width), lambda i, who: (i, 0, 0)), pl.BlockSpec((OUT_CHUNKS, 8, width), lambda i, who: (i, 0, 0)), state, state, state] + [small(v) for v in logs] + [small(skip), ANY],
+            in_specs=[tok(width), tok(x_blk.shape[1]), tok(width), tok(width)] + [tok(2 * LANES), tok(LANES), tok(LANES), tail, tail, pl.BlockSpec((OUT_CHUNKS, LANES, width), lambda i, who: (i, 0, 0)), pl.BlockSpec((OUT_CHUNKS, 8, width), lambda i, who: (i, 0, 0)), state, state, state] + [small(v) for v in logs] + [small(skip), ANY] + [pl.BlockSpec((w_z.shape[0], 256), functools.partial(lambda t, i, who: (0, t), first_tile + t), pipeline_mode=pl.Buffered(1)) for t in range(n_pairs // 2)],
             out_specs=[pl.BlockSpec((rows_out, width), lambda i, who: (0, 0))] * 4,
-            scratch_shapes=[pltpu.VMEM((LANES, width), F32), pltpu.VMEM((LANES, width), F32), pltpu.VMEM((8, width), F32), pltpu.VMEM((OUT_CHUNKS * CHUNK, width), BF16), pltpu.VMEM((LANES, width), BF16), pltpu.VMEM((LANES, 2 * width), BF16)] + [pltpu.VMEM((OUT_CHUNKS, LANES, width), BF16)] * 2,
+            scratch_shapes=[pltpu.VMEM((LANES, width), F32), pltpu.VMEM((LANES, width), F32), pltpu.VMEM((8, width), F32), pltpu.VMEM((OUT_CHUNKS * CHUNK, width), BF16), pltpu.VMEM((LANES, width), BF16), pltpu.VMEM((LANES, 2 * width), BF16)] + [pltpu.VMEM((OUT_CHUNKS, LANES, width), BF16)] * 2 + [pltpu.VMEM((OUT_CHUNKS * CHUNK, width), BF16)],
         ),
         out_shape=[jax.ShapeDtypeStruct((rows_out, width), BF16)] * 4,
         compiler_params=params(),
         cost_estimate=cost(24 * tokens * width * 256, 8 * tokens * width),
         name="outputs",
-    )(who, u, z, scaled, ends, bc, sums[0], sums[1], *tails, gloc, suf, *got, *logs, skip, after)
+    )(who, u, x_blk, scaled, ends, bc, sums[0], sums[1], *tails, gloc, suf, *got, *logs, skip, after, *([w_z] * (n_pairs // 2)))
 
 
 def solution(mesh):
@@ -405,18 +405,11 @@
         sp_index = lax.axis_index('sp')
 
         piece_rows = w_out.shape[0] // (n_dp * n_sp)
-        mine = (sp_index % 2) * (n_dp * n_sp // 2) + lax.axis_index('dp') * (n_sp // 2) + sp_index // 2
+        mine = lax.axis_index('dp') * n_sp + sp_index
         piece = lax.dynamic_slice_in_dim(w_out, mine * piece_rows, piece_rows, axis=0)
         one = swap(piece, 'tp', 1)
         two = swap(piece, 'tp', 2)
-        core = sp_index % 2
-
-        def plane(v):
-            return lax.all_gather(v, ('dp', 'sp'), tiled=True, axis_index_groups=[[0, 2, 4, 6], [1, 3, 5, 7]])
-
-        def whole(half):
-            other = swap(half, 'sp', 1)
-            return jnp.where(core == 0, jnp.concatenate([half, other]), jnp.concatenate([other, half]))
+        plane = lambda v: lax.all_gather(v, ('dp', 'sp'), tiled=True)
 
         n_tiles = w_x.shape[1] // 256
         first = n_tiles * 2 // 5
@@ -431,30 +424,28 @@
         def send(pieces):
             return [pieces[0]] + [swap(pieces[s], 'tp', s) for s in (1, 2, 3)]
 
-        bc, cum3, nexc3, dt3, tail1, tail2, block_log, u_a = prep(x_blk, w_bc, w_dt.T, dt_bias[None, :], a_neg[None, :], w_x, n_a)
+        bc, cum3, nexc3, dt3, tail1, tail2, block_log, u_a, gloc, suf, s_fwd, s_bwd, ut, vf = first_group(x_blk, w_bc, w_dt.T, dt_bias[None, :], a_neg[None, :], w_x, n_a)
+        local_a = (gloc, suf, ut, vf)
         logs = [swap(block_log, 'sp', s) for s in (1, 2, 3)]
+        got_a = exchange(s_fwd, s_bwd)
         one, = later((one,), block_log)
         w_one = plane(one)
-        gloc_a, suf_a, s_fwd, s_bwd, ut_a, vf_a = chunk_states(u_a, bc, (cum3, nexc3, dt3), one, 0, 2 * n_a)
-        got_a = exchange(s_fwd, s_bwd)
-        two, = later((two,), s_fwd)
+        u_b, gloc, suf, s_fwd, s_bwd, ut, vf = next_group(x_blk, w_x, t_b, n_b, bc, (cum3, nexc3, dt3), one, head_b)
+        local_b = (gloc, suf, ut, vf)
+        got_b = exchange(s_fwd, s_bwd)
+        g_a = chunk_outputs(who, u_a, x_blk, w_z, t_a, bc, (cum3, nexc3), (tail1, tail2), local_a, got_a, logs, skip, u_b, 0, 2 * n_a)
+        got_g_a = send(g_a)
+        two, = later((two,), g_a[0])
         three = swap(two, 'tp', 1)
         w_two = plane(two)
-        z_a, u_b = project(x_blk, [(w_z, t_a, n_a), (w_x, t_b, n_b)], two)
-        g_a = chunk_outputs(who, u_a, z_a, bc, (cum3, nexc3), (tail1, tail2), (gloc_a, suf_a, ut_a, vf_a), got_a, logs, skip, three, 0, 2 * n_a)
-        got_g_a = send(g_a)
+        g_b = chunk_outputs(who, u_b, x_blk, w_z, t_b, bc, (cum3, nexc3), (tail1, tail2), local_b, got_b, logs, skip, two, head_b, 2 * n_b)
+        got_g_b = send(g_b)
         w_three = plane(three)
-        gloc_b, suf_b, s_fwd, s_bwd, ut_b, vf_b = chunk_states(u_b, bc, (cum3, nexc3, dt3), g_a[0], head_b, 2 * n_b)
-        got_b = exchange(s_fwd, s_bwd)
-        z_b, = project(x_blk, [(w_z, t_b, n_b)], s_fwd)
-        g_b = chunk_outputs(who, u_b, z_b, bc, (cum3, nexc3), (tail1, tail2), (gloc_b, suf_b, ut_b, vf_b), got_b, logs, skip, z_b, head_b, 2 * n_b)
-        got_g_b = send(g_b)
-
-        w_one, w_two, w_three = [whole(half) for half in later((w_one, w_two, w_three), g_b[0])]
+
         total = add_products(who, x_blk, [(got_g_a[0], w_out, t_a), (got_g_b[0], w_out, t_b)], F32)
-        total = add_products(who, total, [(got_g_a[1], w_one, t_a), (got_g_a[2], w_two, t_a), (got_g_a[3], w_three, t_a)], F32)
-        total = add_products(who, total, [(got_g_b[1], w_one, t_b), (got_g_b[2], w_two, t_b)], F32)
-        return add_products(who, total, [(got_g_b[3], w_three, t_b)], BF16)
+        total = add_products(who, total, [(got_g_a[1], w_one, t_a), (got_g_b[1], w_one, t_b)], F32)
+        total = add_products(who, total, [(got_g_a[2], w_two, t_a), (got_g_b[2], w_two, t_b)], F32)
+        return add_products(who, total, [(got_g_a[3], w_three, t_a), (got_g_b[3], w_three, t_b)], BF16)
 
     in_specs = (P(('dp', 'sp'), None), P(None, 'tp'), P(None, 'tp'), P(None, None), P(None, 'tp'), P('tp'), P('tp'), P('tp'), P('tp', None))
     out_specs = P(('dp', 'sp', 'tp'), None)

time: 336 us -> 306 us (0.911)
  the two profiles are of different devices: /device:TPU:9 before, /device:TPU:12 now
where the time goes in v4:
time: 306 us; the launch traced here: 305 us
  Pallas kernels  131 us (43%)
  waiting for transfers between devices  105 us (34%)
  local copies, waits for them, and re-layouts  38.3 us (13%)
  starting transfers between devices  15.9 us (5%)
  between operations  13.4 us (4%)
    ppermute x18, waiting for transfers between devices, swap(): return lax.ppermute(val, axis, [(i, i ^ slot) for i in range(4)])  105 us
    pallas_call x2, Pallas kernels, chunk_outputs(): pl.pallas_call(functools.partial(out_kernel, first_head, n_pairs), grid_s...  56.2 us
    unnamed x62, local copies, waits for them, and re-layouts  37.1 us
    pallas_call x1, Pallas kernels, next_group(): pl.pallas_call(functools.partial(next_kernel, first_head, n_tiles), grid=...  26.4 us
    pallas_call x1, Pallas kernels, first_group(): pl.pallas_call(functools.partial(first_kernel, n_tiles), grid=(tokens //...  24.4 us
    pallas_call x4, Pallas kernels, add_products(): pl.pallas_call(body, grid_spec=pltpu.PrefetchScalarGridSpec(num_scalar_pr...  24.2 us
    ppermute x18, starting transfers between devices, swap(): return lax.ppermute(val, axis, [(i, i ^ slot) for i in range(4)])  15.6 us
  transfers between devices with their start and end apart: 21, of which 6 were waited for; matrix products, arithmetic and copies ran while one was open for 1% of the time, Pallas kernels for 41%

profile of v4, /device:TPU:12, one launch (start us, length us, event | category | flops | bytes accessed | tf_op | source)
XLA Modules:
  0.0 305.1 jit_solution(13528266499837124930)
XLA Ops:
  8.3 24.4 %first_group.1 = (bf16[2048,256]{1,0:T(8,128)(2,1)}, bf16[2048,128]{1,0:T(8,128)(2,1)}, bf16[2048,128]{1,0:T(8,128)(2,1)}, bf16[2048,128]{1,0:T(8,128)(2,1)}, bf...) custom-call(bf16[2048,2560]{1,0:T(8,128)(2,1)} %refs_0_.9, ...), custom_call_target="tpu_custom_call" | custom-call | flops 16106127360 | bytes 10485760 | tf_op jit(solution)/shard_map/first_group/pallas_call | solution.py:311
  34.1 1.5 collective-permute-start.5
  35.6 2.6 collective-permute-start.10
  40.4 1.3 collective-permute-start.2
  41.7 26.4 %next_group.1 = (bf16[2048,768]{1,0:T(8,128)(2,1)}, f32[16,128,768]{2,1,0:T(8,128)}, f32[16,8,768]{2,1,0:T(8,128)}, bf16[128,768]{1,0:T(8,128)(2,1)}, bf16[128,7...) custom-call(bf16[2048,2560]{1,0:T(8,128)(2,1)} %refs_0_.9, ...), custom_call_target="tpu_custom_call" | custom-call | flops 13421772800 | bytes 10485760 | tf_op jit(solution)/shard_map/next_group/pallas_call | solution.py:330
  68.9 21.9 %outputs.2 = (bf16[512,512]{1,0:T(8,128)(2,1)}, bf16[512,512]{1,0:T(8,128)(2,1)}, bf16[512,512]{1,0:T(8,128)(2,1)}, bf16[512,512]{1,0:T(8,128)(2,1)}) custom-call(s32[2]{0:T(128)} %pad_add_fusion.who_ref, bf16[2048,512]{1,0:T(8,128)(2,1)} %get-tuple-element.36.u_ref, bf16[2048,2560]{1,0:T(8,128)(2,1)} %refs_0_.9, ...), custom_call_target="tpu_custom_call" | custom-call | flops 6442450944 | bytes 8388608 | tf_op jit(solution)/shard_map/outputs/pallas_call | solution.py:376
  91.9 1.4 collective-permute-start.16
  93.3 19.4 %collective-permute-done.16 = bf16[160,2560]{1,0:T(8,128)(2,1)S(1)} collective-permute-done((bf16[160,2560]{1,0:T(8,128)(2,1)}, bf16[160,2560]{1,0:T(8,128)(2,1)S(1)}, u32[]{:S(2)}, u32[]{:S(2)}) %collective-permute-start.16) | collective-permute-done | bytes 819232 | tf_op jit(solution)/shard_map/ppermute | solution.py:396
  114.3 1.3 collective-permute-start.9
  115.6 10.0 %collective-permute-done.8.r2_ref = bf16[128,768]{1,0:T(8,128)(2,1)S(1)} collective-permute-done((bf16[128,768]{1,0:T(8,128)(2,1)S(1)}, bf16[128,768]{1,0:T(8,128)(2,1)S(1)}, u32[]{:S(2)}, u32[]{:S(2)}) %collective-permute-start.8) | collective-permute-done | bytes 196640 | tf_op jit(solution)/shard_map/ppermute | solution.py:396
  125.6 7.2 %collective-permute-done.9.r3_ref = bf16[128,768]{1,0:T(8,128)(2,1)S(1)} collective-permute-done((bf16[128,768]{1,0:T(8,128)(2,1)S(1)}, bf16[128,768]{1,0:T(8,128)(2,1)S(1)}, u32[]{:S(2)}, u32[]{:S(2)}) %collective-permute-start.9) | collective-permute-done | bytes 196640 | tf_op jit(solution)/shard_map/ppermute | solution.py:396
  133.5 34.3 %outputs.3 = (bf16[512,768]{1,0:T(8,128)(2,1)}, bf16[512,768]{1,0:T(8,128)(2,1)}, bf16[512,768]{1,0:T(8,128)(2,1)}, bf16[512,768]{1,0:T(8,128)(2,1)}) custom-call(s32[2]{0:T(128)} %pad_add_fusion.who_ref, bf16[2048,768]{1,0:T(8,128)(2,1)} %get-tuple-element.51.after_ref.u_ref, bf16[2048,2560]{1,0:T(8,128)(2,1)} %refs_0_.9, ...), custom_call_target="tpu_custom_call" | custom-call | flops 9663676416 | bytes 12582912 | tf_op jit(solution)/shard_map/outputs/pallas_call | solution.py:376
  167.8 1.9 collective-permute-start.12
  169.9 2.9 collective-permute-start.13
  173.2 2.9 copy-done
  176.1 4.1 %copy-done.4 = bf16[2048,2560]{1,0:T(8,128)(2,1)S(1)} copy-done((bf16[2048,2560]{1,0:T(8,128)(2,1)S(1)}, bf16[2048,2560]{1,0:T(8,128)(2,1)}, u32[]{:S(2)}) %copy-start.4) | copy-done | bytes 10485784
  181.3 5.8 %add_products.4.refs_0_ = f32[512,2560]{1,0:T(8,128)S(1)} custom-call(s32[2]{0:T(128)S(1)} %copy-done.15, bf16[2048,2560]{1,0:T(8,128)(2,1)S(1)} %copy-done.4, bf16[512,512]{1,0:T(8,128)(2,1)S(1)} %copy-done.12, bf16[1280,2560]{1,0:T(8,128)(2,1)S(1)} %copy-done, bf16[1280,2560]{1,0:T(8,128)(2,1)S(1)} %copy-done, bf16[512,768]{1,0:T(8,128)(2,1)S(1)} %copy-done.11, ...), custom_call_target="tpu_custom_call" | custom-call | flops 3355443200 | bytes 2621440 | tf_op jit(solution)/shard_map/add_products/pallas_call | solution.py:357
  187.1 2.3 copy-done.5
  189.5 33.6 %collective-permute-done.11.refs_1_ = bf16[512,512]{1,0:T(8,128)(2,1)S(1)} collective-permute-done((bf16[512,512]{1,0:T(8,128)(2,1)}, bf16[512,512]{1,0:T(8,128)(2,1)S(1)}, u32[]{:S(2)}, u32[]{:S(2)}) %collective-permute-start.11) | collective-permute-done | bytes 524320 | tf_op jit(solution)/shard_map/ppermute | solution.py:396
  223.9 2.9 copy-done.1
  226.8 2.5 copy-done.6
  230.3 6.0 %add_products.5.refs_0_ = f32[512,2560]{1,0:T(8,128)S(1)} custom-call(s32[2]{0:T(128)S(1)} %copy-done.15, f32[512,2560]{1,0:T(8,128)S(1)} %copy-done.6, bf16[512,512]{1,0:T(8,128)(2,1)S(1)} %copy-done.14, bf16[1280,2560]{1,0:T(8,128)(2,1)S(1)} %copy-done.1, bf16[1280,2560]{1,0:T(8,128)(2,1)S(1)} %copy-done.1, ...), custom_call_target="tpu_custom_call" | custom-call | flops 3355443200 | bytes 2621440 | tf_op jit(solution)/shard_map/add_products/pallas_call | solution.py:357
  236.3 2.3 copy-done.7
  238.6 16.9 %collective-permute-done.13.refs_1_ = bf16[512,512]{1,0:T(8,128)(2,1)S(1)} collective-permute-done((bf16[512,512]{1,0:T(8,128)(2,1)}, bf16[512,512]{1,0:T(8,128)(2,1)S(1)}, u32[]{:S(2)}, u32[]{:S(2)}) %collective-permute-start.13) | collective-permute-done | bytes 524320 | tf_op jit(solution)/shard_map/ppermute | solution.py:396
  255.5 2.9 copy-done.3
  258.4 2.5 copy-done.8
  260.9 6.0 %add_products.6.refs_0_ = f32[512,2560]{1,0:T(8,128)S(1)} custom-call(s32[2]{0:T(128)S(1)} %copy-done.15, f32[512,2560]{1,0:T(8,128)S(1)} %copy-done.8, bf16[512,512]{1,0:T(8,128)(2,1)S(1)} %collective-permute-done.13.refs_1_, bf16[1280,2560]{1,0:T(8,128)(2,1)S(1)} %copy-done.3, bf16[1280,2560]{1,0:T(8,128)(2,1)S(1)} %copy-done.3, ...), custom_call_target="tpu_custom_call" | custom-call | flops 3355443200 | bytes 2621440 | tf_op jit(solution)/shard_map/add_products/pallas_call | solution.py:357
  266.9 2.3 copy-done.9
  269.2 17.6 %collective-permute-done.15.refs_1_ = bf16[512,512]{1,0:T(8,128)(2,1)S(1)} collective-permute-done((bf16[512,512]{1,0:T(8,128)(2,1)}, bf16[512,512]{1,0:T(8,128)(2,1)S(1)}, u32[]{:S(2)}, u32[]{:S(2)}) %collective-permute-start.15) | collective-permute-done | bytes 524320 | tf_op jit(solution)/shard_map/ppermute | solution.py:396
  286.8 2.9 copy-done.2
  289.6 2.5 copy-done.10
  292.1 6.4 %add_products.7 = bf16[512,2560]{1,0:T(8,128)(2,1)} custom-call(s32[2]{0:T(128)S(1)} %copy-done.15, f32[512,2560]{1,0:T(8,128)S(1)} %copy-done.10, bf16[512,512]{1,0:T(8,128)(2,1)S(1)} %collective-permute-done.15.refs_1_, bf16[1280,2560]{1,0:T(8,128)(2,1)S(1)} %copy-done.2, bf16[1280,2560]{1,0:T(8,128)(2,1)S(1)} %copy-done.2, ...), custom_call_target="tpu_custom_call" | custom-call | flops 3355443200 | bytes 2621440 | tf_op jit(solution)/shard_map/add_products/pallas_call | solution.py:357
  (87 shorter events, 13.1 us)
Async XLA Ops:
  6.5 217.4 %all-gather.4.cloned.1.call-start = ((), (), s32[]{:S(2)}) async-start(), calls=%async_computation | async-start | bytes 7372800 | tf_op jit(solution)/shard_map/all_gather | solution.py:412
  7.7 24.9 %copy-start.19 = (bf16[160,2560]{1,0:T(8,128)(2,1)}, bf16[160,2560]{1,0:T(8,128)(2,1)S(1)}, u32[]{:S(2)}) copy-start(bf16[160,2560]{1,0:T(8,128)(2,1)S(1)} %constant_dynamic-slice_fusion) | copy-start | bytes 2457604
  7.7 24.9 %collective-permute-start.6 = (bf16[160,2560]{1,0:T(8,128)(2,1)S(1)}, bf16[160,2560]{1,0:T(8,128)(2,1)S(1)}, u32[]{:S(2)}, u32[]{:S(2)}) collective-permute-start(bf16[160,2560]{1,0:T(8,128)(2,1)S(1)} %constant_dynamic-slice_fusion), channel_id=1, source_target_pairs={{0,4},{4,0},{8,12},{12,8},{1,5},{5,1},{9,13},{13,9},{2,6},{6,2},{1... | collective-permute-start | bytes 2457608 | tf_op jit(solution)/shard_map/ppermute | solution.py:396
  33.6 221.9 %all-gather.6.cloned.1.call-start = ((), (), s32[]{:S(2)}) async-start(), calls=%async_computation.1 | async-start | bytes 7372800 | tf_op jit(solution)/shard_map/all_gather | solution.py:412
  33.6 6.3 %collective-permute-start.3 = (f32[8,128]{1,0:T(8,128)}, f32[8,128]{1,0:T(8,128)S(1)}, u32[]{:S(2)}, u32[]{:S(2)}) collective-permute-start(f32[8,128]{1,0:T(8,128)} %get-tuple-element.48), channel_id=1, source_target_pairs={{0,1},{1,0},{2,3},{3,2},{4,5},{5,4},{6,7},{7,6},{8,9},{9,8},{10,11... | collective-permute-start | bytes 12296 | tf_op jit(solution)/shard_map/ppermute | solution.py:396
  33.7 6.7 %collective-permute-start.4 = (f32[8,128]{1,0:T(8,128)}, f32[8,128]{1,0:T(8,128)S(1)}, u32[]{:S(2)}, u32[]{:S(2)}) collective-permute-start(f32[8,128]{1,0:T(8,128)} %get-tuple-element.48), channel_id=1, source_target_pairs={{0,2},{1,3},{2,0},{3,1},{4,6},{5,7},{6,4},{7,5},{8,10},{9,11},{10,... | collective-permute-start | bytes 12296 | tf_op jit(solution)/shard_map/ppermute | solution.py:396
  34.1 34.1 %collective-permute-start.5 = (f32[8,128]{1,0:T(8,128)}, f32[8,128]{1,0:T(8,128)S(1)}, u32[]{:S(2)}, u32[]{:S(2)}) collective-permute-start(f32[8,128]{1,0:T(8,128)} %get-tuple-element.48), channel_id=1, source_target_pairs={{0,3},{1,2},{2,1},{3,0},{4,7},{5,6},{6,5},{7,4},{8,11},{9,10},{10,... | collective-permute-start | bytes 12296 | tf_op jit(solution)/shard_map/ppermute | solution.py:396
  35.6 55.2 %collective-permute-start.10 = (bf16[160,2560]{1,0:T(8,128)(2,1)}, bf16[160,2560]{1,0:T(8,128)(2,1)S(1)}, u32[]{:S(2)}, u32[]{:S(2)}) collective-permute-start(bf16[160,2560]{1,0:T(8,128)(2,1)} %copy-done.19), channel_id=1, source_target_pairs={{0,8},{4,12},{8,0},{12,4},{1,9},{5,13},{9,1},{13,5},{2,10},{6,14},... | collective-permute-start | bytes 2457608 | tf_op jit(solution)/shard_map/ppermute | solution.py:396
  39.2 29.0 %collective-permute-start = (bf16[128,512]{1,0:T(8,128)(2,1)S(1)}, bf16[128,512]{1,0:T(8,128)(2,1)S(1)}, u32[]{:S(2)}, u32[]{:S(2)}) collective-permute-start(bf16[128,512]{1,0:T(8,128)(2,1)S(1)} %get-tuple-element.72), channel_id=1, source_target_pairs={{0,1},{1,0},{2,3},{3,2},{4,5},{5,4},{6,7},{7,6},{8,9},{9,8},{10,11... | collective-permute-start | bytes 393224 | tf_op jit(solution)/shard_map/ppermute | solution.py:396
  39.9 28.2 %copy-start.28 = (f32[8,128]{1,0:T(8,128)}, f32[8,128]{1,0:T(8,128)S(1)}, u32[]{:S(2)}) copy-start(f32[8,128]{1,0:T(8,128)S(1)} %collective-permute-done.3.l1_ref) | copy-start | bytes 12292
  39.9 28.3 %collective-permute-start.1 = (bf16[128,512]{1,0:T(8,128)(2,1)S(1)}, bf16[128,512]{1,0:T(8,128)(2,1)S(1)}, u32[]{:S(2)}, u32[]{:S(2)}) collective-permute-start(bf16[128,512]{1,0:T(8,128)(2,1)S(1)} %get-tuple-element.71), channel_id=1, source_target_pairs={{0,2},{1,3},{2,0},{3,1},{4,6},{5,7},{6,4},{7,5},{8,10},{9,11},{10,... | collective-permute-start | bytes 393224 | tf_op jit(solution)/shard_map/ppermute | solution.py:396
  40.4 27.7 %copy-start.29 = (f32[8,128]{1,0:T(8,128)}, f32[8,128]{1,0:T(8,128)S(1)}, u32[]{:S(2)}) copy-start(f32[8,128]{1,0:T(8,128)S(1)} %collective-permute-done.4.l2_ref) | copy-start | bytes 12292
  40.4 27.8 %collective-permute-start.2 = (bf16[128,512]{1,0:T(8,128)(2,1)S(1)}, bf16[128,512]{1,0:T(8,128)(2,1)S(1)}, u32[]{:S(2)}, u32[]{:S(2)}) collective-permute-start(bf16[128,512]{1,0:T(8,128)(2,1)S(1)} %get-tuple-element.70), channel_id=1, source_target_pairs={{0,3},{1,2},{2,1},{3,0},{4,7},{5,6},{6,5},{7,4},{8,11},{9,10},{10,... | collective-permute-start | bytes 393224 | tf_op jit(solution)/shard_map/ppermute | solution.py:396
  68.9 44.7 %copy-start.23 = (bf16[128,768]{1,0:T(8,128)(2,1)S(1)}, bf16[128,768]{1,0:T(8,128)(2,1)}, u32[]{:S(2)}) copy-start(bf16[128,768]{1,0:T(8,128)(2,1)} %get-tuple-element.57) | copy-start | bytes 589828
  68.9 44.7 %copy-start.24 = (bf16[128,768]{1,0:T(8,128)(2,1)S(1)}, bf16[128,768]{1,0:T(8,128)(2,1)}, u32[]{:S(2)}) copy-start(bf16[128,768]{1,0:T(8,128)(2,1)} %get-tuple-element.58) | copy-start | bytes 589828
  91.7 195.1 %all-gather.8.cloned.1.call-start = ((), (), s32[]{:S(2)}) async-start(), calls=%async_computation.2 | async-start | bytes 7372800 | tf_op jit(solution)/shard_map/all_gather | solution.py:412
  91.9 20.7 %collective-permute-start.16 = (bf16[160,2560]{1,0:T(8,128)(2,1)}, bf16[160,2560]{1,0:T(8,128)(2,1)S(1)}, u32[]{:S(2)}, u32[]{:S(2)}) collective-permute-start(bf16[160,2560]{1,0:T(8,128)(2,1)} %copy-done.16), channel_id=1, source_target_pairs={{0,4},{4,0},{8,12},{12,8},{1,5},{5,1},{9,13},{13,9},{2,6},{6,2},{1... | collective-permute-start | bytes 2457608 | tf_op jit(solution)/shard_map/ppermute | solution.py:396
  113.7 1.9 collective-permute-start.7
  113.8 11.8 %collective-permute-start.8 = (bf16[128,768]{1,0:T(8,128)(2,1)S(1)}, bf16[128,768]{1,0:T(8,128)(2,1)S(1)}, u32[]{:S(2)}, u32[]{:S(2)}) collective-permute-start(bf16[128,768]{1,0:T(8,128)(2,1)S(1)} %get-tuple-element.68), channel_id=1, source_target_pairs={{0,2},{1,3},{2,0},{3,1},{4,6},{5,7},{6,4},{7,5},{8,10},{9,11},{10,... | collective-permute-start | bytes 589832 | tf_op jit(solution)/shard_map/ppermute | solution.py:396
  114.3 18.5 %collective-permute-start.9 = (bf16[128,768]{1,0:T(8,128)(2,1)S(1)}, bf16[128,768]{1,0:T(8,128)(2,1)S(1)}, u32[]{:S(2)}, u32[]{:S(2)}) collective-permute-start(bf16[128,768]{1,0:T(8,128)(2,1)S(1)} %get-tuple-element.67), channel_id=1, source_target_pairs={{0,3},{1,2},{2,1},{3,0},{4,7},{5,6},{6,5},{7,4},{8,11},{9,10},{10,... | collective-permute-start | bytes 589832 | tf_op jit(solution)/shard_map/ppermute | solution.py:396
  115.6 17.2 %copy-start.20 = (bf16[128,768]{1,0:T(8,128)(2,1)}, bf16[128,768]{1,0:T(8,128)(2,1)S(1)}, u32[]{:S(2)}) copy-start(bf16[128,768]{1,0:T(8,128)(2,1)S(1)} %collective-permute-done.7.r1_ref) | copy-start | bytes 589828
  125.6 7.2 %copy-start.21 = (bf16[128,768]{1,0:T(8,128)(2,1)}, bf16[128,768]{1,0:T(8,128)(2,1)S(1)}, u32[]{:S(2)}) copy-start(bf16[128,768]{1,0:T(8,128)(2,1)S(1)} %collective-permute-done.8.r2_ref) | copy-start | bytes 589828
  133.5 39.7 %copy-start.12 = (bf16[512,512]{1,0:T(8,128)(2,1)S(1)}, bf16[512,512]{1,0:T(8,128)(2,1)}, u32[]{:S(2)}) copy-start(bf16[512,512]{1,0:T(8,128)(2,1)} %get-tuple-element.52.refs_1_) | copy-start | bytes 1572868
  133.5 39.7 %copy-start.15 = (s32[2]{0:T(128)S(1)}, s32[2]{0:T(128)}, u32[]{:S(2)}) copy-start(s32[2]{0:T(128)} %pad_add_fusion.who_ref) | copy-start | bytes 28
  167.8 56.1 %collective-permute-start.12 = (bf16[512,768]{1,0:T(8,128)(2,1)}, bf16[512,768]{1,0:T(8,128)(2,1)S(1)}, u32[]{:S(2)}, u32[]{:S(2)}) collective-permute-start(bf16[512,768]{1,0:T(8,128)(2,1)} %get-tuple-element.62), channel_id=1, source_target_pairs={{0,4},{4,0},{8,12},{12,8},{1,5},{5,1},{9,13},{13,9},{2,6},{6,2},{1... | collective-permute-start | bytes 2359304 | tf_op jit(solution)/shard_map/ppermute | solution.py:396
  169.7 53.4 %collective-permute-start.11 = (bf16[512,512]{1,0:T(8,128)(2,1)}, bf16[512,512]{1,0:T(8,128)(2,1)S(1)}, u32[]{:S(2)}, u32[]{:S(2)}) collective-permute-start(bf16[512,512]{1,0:T(8,128)(2,1)} %get-tuple-element.61), channel_id=1, source_target_pairs={{0,4},{4,0},{8,12},{12,8},{1,5},{5,1},{9,13},{13,9},{2,6},{6,2},{1... | collective-permute-start | bytes 1572872 | tf_op jit(solution)/shard_map/ppermute | solution.py:396
  169.9 85.6 %collective-permute-start.14 = (bf16[512,768]{1,0:T(8,128)(2,1)}, bf16[512,768]{1,0:T(8,128)(2,1)S(1)}, u32[]{:S(2)}, u32[]{:S(2)}) collective-permute-start(bf16[512,768]{1,0:T(8,128)(2,1)} %get-tuple-element.64), channel_id=1, source_target_pairs={{0,8},{4,12},{8,0},{12,4},{1,9},{5,13},{9,1},{13,5},{2,10},{6,14},... | collective-permute-start | bytes 2359304 | tf_op jit(solution)/shard_map/ppermute | solution.py:396
  169.9 85.6 %collective-permute-start.13 = (bf16[512,512]{1,0:T(8,128)(2,1)}, bf16[512,512]{1,0:T(8,128)(2,1)S(1)}, u32[]{:S(2)}, u32[]{:S(2)}) collective-permute-start(bf16[512,512]{1,0:T(8,128)(2,1)} %get-tuple-element.63), channel_id=1, source_target_pairs={{0,8},{4,12},{8,0},{12,4},{1,9},{5,13},{9,1},{13,5},{2,10},{6,14},... | collective-permute-start | bytes 1572872 | tf_op jit(solution)/shard_map/ppermute | solution.py:396
  172.8 113.9 %collective-permute-start.17 = (bf16[512,768]{1,0:T(8,128)(2,1)}, bf16[512,768]{1,0:T(8,128)(2,1)S(1)}, u32[]{:S(2)}, u32[]{:S(2)}) collective-permute-start(bf16[512,768]{1,0:T(8,128)(2,1)} %get-tuple-element.66), channel_id=1, source_target_pairs={{0,12},{4,8},{8,4},{12,0},{1,13},{5,9},{9,5},{13,1},{2,14},{6,10},... | collective-permute-start | bytes 2359304 | tf_op jit(solution)/shard_map/ppermute | solution.py:396
  173.2 2.9 copy-start
  176.1 4.1 %copy-start.4 = (bf16[2048,2560]{1,0:T(8,128)(2,1)S(1)}, bf16[2048,2560]{1,0:T(8,128)(2,1)}, u32[]{:S(2)}) copy-start(bf16[2048,2560]{1,0:T(8,128)(2,1)} %refs_0_.9) | copy-start | bytes 31457284
  223.9 62.9 %collective-permute-start.15 = (bf16[512,512]{1,0:T(8,128)(2,1)}, bf16[512,512]{1,0:T(8,128)(2,1)S(1)}, u32[]{:S(2)}, u32[]{:S(2)}) collective-permute-start(bf16[512,512]{1,0:T(8,128)(2,1)} %get-tuple-element.65), channel_id=1, source_target_pairs={{0,12},{4,8},{8,4},{12,0},{1,13},{5,9},{9,5},{13,1},{2,14},{6,10},... | collective-permute-start | bytes 1572872 | tf_op jit(solution)/shard_map/ppermute | solution.py:396
  (20 other events, 32.1 us)
Sparse Core Ops, SparseCore 0:
  33.7 49.4 all-gather.3
  91.8 52.8 all-gather.5
  146.6 45.3 all-gather.7

commit v5 on v4

--- a/solution.py
+++ b/solution.py
@@ -14,7 +14,7 @@
 STATE_CHUNKS = 4
 OUT_CHUNKS = 2
 OUT_AHEAD = 2
-SUM_MIB = 24
+SUM_MIB = 62
 F32 = jnp.float32
 BF16 = jnp.bfloat16
 
@@ -28,7 +28,7 @@
 
 
 def prep_kernel(n_tiles, x_ref, wbc_ref, wdt_ref, bias_ref, a_ref, *refs):
-    bc_ref, cum_ref, nexc_ref, dt_ref, tail1_ref, tail2_ref, log_ref, u_ref = refs[n_tiles:n_tiles + 8]
+    bc_ref, cum_ref, nexc_ref, dt_ref, tail1_ref, tail2_ref, u_ref = refs[n_tiles:n_tiles + 7]
     w_buf, par, pick = refs[-8:-5]
     heads = bias_ref.shape[1]
     row = lax.broadcasted_iota(jnp.int32, (CHUNK, LANES), 0)
@@ -36,7 +36,6 @@
 
     @pl.when(pl.program_id(0) == 0)
     def _():
-        log_ref[...] = jnp.zeros_like(log_ref)
         w_buf[...] = jnp.zeros_like(w_buf)
         par[...] = jnp.zeros_like(par)
         for k in range(3):
@@ -51,10 +50,7 @@
     x_val = x_ref[...]
     raw = lax.dot_general(x_val, w_buf[...], (((1,), (1,)), ((), ())), preferred_element_type=F32) + par[0:1, :]
 
-    def u_tile(i):
-        u_ref[:, i * 256:(i + 1) * 256] = jnp.dot(x_val, refs[i][...], preferred_element_type=F32).astype(BF16)
-
-    u_tile(0)
+    project_tile(u_ref, x_ref, refs[0], 0)
     dt_val = jnp.maximum(raw, 0.0) + jnp.log1p(jnp.exp(-jnp.abs(raw)))
     la_val = jnp.maximum(dt_val * par[1:2, :], -1000.0)
     tri = jnp.where(row >= lane, 1.0, 0.0).astype(BF16)
@@ -67,35 +63,32 @@
         second = rest.astype(BF16)
         third = (rest - second.astype(F32)).astype(BF16)
         sums.append(sum(jnp.dot(tri, t, preferred_element_type=F32) for t in (first, second, third)))
-    for i in range(1, n_tiles):
-        u_tile(i)
     one = jnp.where(lane < 3 * SLOT + 3, 1.0, 0.0)
     for part, cum in zip(parts, sums):
         cum_ref[part, :] = split3(cum, lane, one)
         nexc_ref[part, :] = split3(la_val[part, :] - cum, lane, one)
         dt_ref[part, :] = split3(dt_val[part, :], lane, 0.0)
-        log_ref[...] += cum[CHUNK - 1:CHUNK, :]
     bc_ref[...] = jnp.dot(x_val, wbc_ref[...], preferred_element_type=F32).astype(BF16)
     across = (((1,), (1,)), ((), ()))
     tail1_ref[...] = lax.dot_general(pick[...], cum_ref[...], across, preferred_element_type=F32).astype(BF16)
     tail2_ref[...] = lax.dot_general(pick[...], nexc_ref[...], across, preferred_element_type=F32).astype(BF16)
 
 
-def first_kernel(n_tiles, *refs):
+def first_kernel(n_tiles, who_ref, *refs):
     prep_kernel(n_tiles, *refs)
-    bc_ref, cum_ref, nexc_ref, dt_ref, _, _, _, u_ref = refs[5 + n_tiles:13 + n_tiles]
-    state_kernel(0, 2 * n_tiles, u_ref, bc_ref, cum_ref, nexc_ref, dt_ref, *refs[13 + n_tiles:-8], *refs[-5:])
-
-
-def next_kernel(first_head, n_tiles, x_ref, bc_ref, cum_ref, nexc_ref, dt_ref, *refs):
+    bc_ref, cum_ref, nexc_ref, dt_ref, _, _, u_ref = refs[5 + n_tiles:12 + n_tiles]
+    project = lambda t: project_tile(u_ref, refs[0], refs[5 + t], t) if t else None
+    state_kernel(0, 2 * n_tiles, project, u_ref, bc_ref, cum_ref, nexc_ref, dt_ref, *refs[12 + n_tiles:-8], who_ref, *refs[-5:])
+
+
+def next_kernel(first_head, n_tiles, who_ref, x_ref, bc_ref, cum_ref, nexc_ref, dt_ref, *refs):
     u_ref = refs[n_tiles + 1]
-    project_into(u_ref, x_ref[...], refs[:n_tiles])
-    state_kernel(first_head, 2 * n_tiles, u_ref, bc_ref, cum_ref, nexc_ref, dt_ref, *refs[n_tiles + 2:])
-
-
-def project_into(o_ref, x_val, w_refs):
-    for i, w_ref in enumerate(w_refs):
-        o_ref[:, i * 256:(i + 1) * 256] = jnp.dot(x_val, w_ref[...], preferred_element_type=F32).astype(BF16)
+    project = lambda t: project_tile(u_ref, x_ref, refs[t], t)
+    state_kernel(first_head, 2 * n_tiles, project, u_ref, bc_ref, cum_ref, nexc_ref, dt_ref, *refs[n_tiles + 2:-5], who_ref, *refs[-5:])
+
+
+def project_tile(o_ref, x_ref, w_ref, t):
+    o_ref[:, t * 256:(t + 1) * 256] = jnp.dot(x_ref[...], w_ref[...], preferred_element_type=F32).astype(BF16)
 
 
 def sum_kernel(n_tiles, n_pieces, acc_ref, *refs):
@@ -118,7 +111,7 @@
     return jnp.where(low, jnp.broadcast_to(cols[:, head:head + 1], low.shape), jnp.broadcast_to(cols[:, head + 1:head + 2], low.shape))
 
 
-def state_kernel(first_head, n_pairs, u_ref, bc_ref, cum_ref, nexc_ref, dt_ref, gloc_ref, suf_ref, sf_ref, sb_ref, ut_ref, vf_ref, g_acc, f_acc, suf_acc, v_buf, spread):
+def state_kernel(first_head, n_pairs, project, u_ref, bc_ref, cum_ref, nexc_ref, dt_ref, gloc_ref, suf_ref, s1_ref, s2_ref, s3_ref, ut_ref, vf_ref, who_ref, g_acc, f_acc, suf_acc, v_buf, spread):
     step = pl.program_id(0)
     width = n_pairs * LANES
 
@@ -129,51 +122,51 @@
         suf_acc[...] = jnp.zeros_like(suf_acc)
         spread[...] = spread_matrix(spread.shape, first_head, LANES // 2)
 
-    def terms_of(c, p):
-        rows = slice(c * CHUNK, (c + 1) * CHUNK)
-        wide = slice(p * LANES, min(p + 2, n_pairs) * LANES)
-        return [jnp.dot(r[rows, :], spread[:, wide], preferred_element_type=F32) for r in (cum_ref, nexc_ref, dt_ref)]
-
-    def finish(c, total):
-        rows = slice(c * CHUNK, (c + 1) * CHUNK)
-        suffix = suf_acc[...]
-        suf_ref[c, 0:1, :] = suffix[0:1, :]
-        suf_ref[c, 1:2, :] = total
-        sums = lax.dot_general(bc_ref[rows, :LANES], v_buf[rows, :], (((0,), (0,)), ((), ())), preferred_element_type=F32)
-        back = g_acc[...]
-        gloc_ref[c] = back
-        g_acc[...] = back * jnp.exp(total) + sums[:, :width]
-        f_acc[...] += sums[:, width:] * jnp.exp(suffix[0:1, :])
-        suf_acc[...] = suffix + total
-
-    order = [(c, p) for c in reversed(range(STATE_CHUNKS)) for p in range(0, n_pairs, 2)]
+    def terms_of(c, t):
+        rows = slice(c * CHUNK, (c + 1) * CHUNK)
+        return [jnp.dot(r[rows, :], spread[:, t * 256:(t + 1) * 256], preferred_element_type=F32) for r in (cum_ref, nexc_ref, dt_ref)]
+
+    project(0)
+    order = [(c, t) for t in range(n_pairs // 2) for c in reversed(range(STATE_CHUNKS))]
     ahead = terms_of(*order[0])
-    for i, (c, p0) in enumerate(order):
+    for i, (c, t) in enumerate(order):
         terms = ahead
         if i + 1 < len(order):
             ahead = terms_of(*order[i + 1])
-        rows = slice(c * CHUNK, (c + 1) * CHUNK)
-        if p0 == 0:
-            totals = []
-        for p in range(p0, min(p0 + 2, n_pairs)):
-            part = slice(p * LANES, (p + 1) * LANES)
-            half = slice((p - p0) * LANES, (p - p0 + 1) * LANES)
-            cum, nexc, dt_val = [t[:, half] for t in terms]
-            scaled = u_ref[rows, part].astype(F32) * dt_val
-            total = cum[CHUNK - 1:CHUNK, :]
-            totals.append(total)
-            ut_ref[rows, part] = scaled.astype(BF16)
-            v_buf[rows, part] = (scaled * jnp.exp(-nexc)).astype(BF16)
-            end = (scaled * jnp.exp(total - cum)).astype(BF16)
-            vf_ref[rows, part] = end
-            v_buf[rows, slice(width + p * LANES, width + (p + 1) * LANES)] = end
-        if p0 + 2 >= n_pairs:
-            finish(c, jnp.concatenate(totals, axis=1))
+        if c == STATE_CHUNKS - 1 and t + 1 < n_pairs // 2:
+            project(t + 1)
+        rows = slice(c * CHUNK, (c + 1) * CHUNK)
+        wide = slice(t * 256, (t + 1) * 256)
+        cum, nexc, dt_val = terms
+        scaled = u_ref[rows, wide].astype(F32) * dt_val
+        total = cum[CHUNK - 1:CHUNK, :]
+        suffix = suf_acc[:, wide]
+        ut_ref[rows, wide] = scaled.astype(BF16)
+        v_buf[c, :, t * 512:t * 512 + 256] = (scaled * jnp.exp(-nexc)).astype(BF16)
+        end = (scaled * jnp.exp(total - cum)).astype(BF16)
+        vf_ref[rows, wide] = end
+        v_buf[c, :, t * 512 + 256:(t + 1) * 512] = end
+        suf_ref[c, 0:1, wide] = suffix[0:1, :]
+        suf_ref[c, 1:2, wide] = total
+        suf_acc[:, wide] = suffix + total
+        sums = lax.dot_general(bc_ref[rows, :LANES], v_buf[c, :, t * 512:(t + 1) * 512], (((0,), (0,)), ((), ())), preferred_element_type=F32)
+        back = g_acc[:, wide]
+        gloc_ref[c, :, wide] = back
+        g_acc[:, wide] = back * jnp.exp(total) + sums[:, :256]
+        f_acc[:, wide] += sums[:, 256:] * jnp.exp(suffix[0:1, :])
 
     @pl.when(step == pl.num_programs(0) - 1)
     def _():
-        sf_ref[...] = f_acc[...].astype(BF16)
-        sb_ref[...] = g_acc[...].astype(BF16)
+        row = lax.broadcasted_iota(jnp.int32, (16, width), 0)
+        log = jnp.broadcast_to(suf_acc[0:1, :], (16, width))
+        first = log.astype(BF16).astype(F32)
+        second = (log - first).astype(BF16).astype(F32)
+        third = log - first - second
+        terms = jnp.where(row == 0, first, jnp.where(row == 1, second, jnp.where(row == 2, third, 0.0))).astype(BF16)
+        me = who_ref[1]
+        for s, s_ref in ((1, s1_ref), (2, s2_ref), (3, s3_ref)):
+            s_ref[LANES:LANES + 16, :] = terms
+            s_ref[0:LANES, :] = jnp.where(me < (me ^ s), f_acc[...], g_acc[...]).astype(BF16)
 
 
 def peer_weights(sp_index, logs):
@@ -191,24 +184,23 @@
     return fwd, bwd
 
 
-def out_kernel(first_head, n_pairs, who_ref, u_ref, x_ref, ut_ref, vf_ref, bc_ref, cum_ref, nexc_ref, tail1_ref, tail2_ref, gloc_ref, suf_ref, r1_ref, r2_ref, r3_ref, l1_ref, l2_ref, l3_ref, skip_ref, after_ref, *refs):
+def out_kernel(first_head, n_pairs, who_ref, u_ref, x_ref, ut_ref, vf_ref, bc_ref, cum_ref, nexc_ref, tail1_ref, tail2_ref, gloc_ref, suf_ref, r1_ref, r2_ref, r3_ref, skip_ref, after_ref, *refs):
     w_refs, (o0_ref, o1_ref, o2_ref, o3_ref, f_acc, hb_acc, skip_buf, g_buf, spread, pick, fwd_buf, bwd_buf, z_ref) = refs[:n_pairs // 2], refs[n_pairs // 2:]
     step = pl.program_id(0)
-    project_into(z_ref, x_ref[...], w_refs)
 
     @pl.when(step == 0)
     def _():
         low8 = lax.broadcasted_iota(jnp.int32, (8, LANES), 1) < LANES // 2
-        fwd, bwd = peer_weights(who_ref[1], [r[...] for r in (l1_ref, l2_ref, l3_ref)])
         got = (r1_ref, r2_ref, r3_ref)
+        logs = [r[LANES:LANES + 16, :].astype(F32) for r in got]
+        fwd, bwd = peer_weights(who_ref[1], [v[0:1, :] + v[1:2, :] + v[2:3, :] for v in logs])
         spread[...] = spread_matrix(spread.shape, first_head, LANES // 2)
         pick[...] = spread_matrix(pick.shape, first_head, LANES)
         for p in range(n_pairs):
             part = slice(p * LANES, (p + 1) * LANES)
-            over = lambda v: pair_cols(v, first_head + 2 * p, low8)
-            skip_buf[:, part] = 2.0 * over(jnp.broadcast_to(skip_ref[...], (8, skip_ref.shape[1])))
-            f_acc[:, part] = sum(got[s][:, part].astype(F32) * over(fwd[s])[0:1, :] for s in range(3))
-            hb_acc[:, part] = sum(got[s][:, part].astype(F32) * over(bwd[s])[0:1, :] for s in range(3))
+            skip_buf[:, part] = 2.0 * pair_cols(jnp.broadcast_to(skip_ref[...], (8, skip_ref.shape[1])), first_head + 2 * p, low8)
+        f_acc[...] = sum(got[s][0:LANES, :].astype(F32) * fwd[s] for s in range(3))
+        hb_acc[...] = sum(got[s][0:LANES, :].astype(F32) * bwd[s] for s in range(3))
 
     row = lax.broadcasted_iota(jnp.int32, (CHUNK, LANES), 0)
     lane = lax.broadcasted_iota(jnp.int32, (CHUNK, LANES), 1)
@@ -249,12 +241,15 @@
         y_val = jnp.exp(cum) * y_fwd + jnp.exp(suf_ref[c, 1:2, part] + nexc) * y_bwd
         return y_val + skip_buf[0:1, part] * u_ref[rows, part].astype(F32)
 
-    order = [(c, p) for c in range(OUT_CHUNKS) for p in range(n_pairs)]
+    order = [(c, 2 * t + h) for t in range(n_pairs // 2) for c in range(OUT_CHUNKS) for h in range(2)]
     ahead = [weights(*order[i]) for i in range(OUT_AHEAD)]
+    project_tile(z_ref, x_ref, w_refs[0], 0)
     for i, (c, p) in enumerate(order):
         mix = ahead.pop(0)
         if i + OUT_AHEAD < len(order):
             ahead.append(weights(*order[i + OUT_AHEAD]))
+        if c == 0 and p % 2 == 0 and p // 2 + 1 < n_pairs // 2:
+            project_tile(z_ref, x_ref, w_refs[p // 2 + 1], p // 2 + 1)
         y_val = passed(c, p)
         rows = slice(c * CHUNK, (c + 1) * CHUNK)
         part = slice(p * LANES, (p + 1) * LANES)
@@ -283,6 +278,7 @@
 
 
 ANY = pl.BlockSpec(memory_space=pl.ANY)
+SMEM = pl.BlockSpec(memory_space=pltpu.SMEM)
 
 
 def w_specs(w, first_tile, n_tiles):
@@ -291,14 +287,14 @@
 
 def state_parts(tokens, width, tok, at):
     n_chunks = tokens // CHUNK
-    whole = pl.BlockSpec((LANES, width), lambda i: (0, 0))
-    specs = [tok(width), pl.BlockSpec((STATE_CHUNKS, LANES, width), lambda i: (at(i), 0, 0)), pl.BlockSpec((STATE_CHUNKS, 8, width), lambda i: (at(i), 0, 0)), whole, whole, tok(width), tok(width)]
-    shapes = [jax.ShapeDtypeStruct((tokens, width), BF16), jax.ShapeDtypeStruct((n_chunks, LANES, width), F32), jax.ShapeDtypeStruct((n_chunks, 8, width), F32)] + [jax.ShapeDtypeStruct((LANES, width), BF16)] * 2 + [jax.ShapeDtypeStruct((tokens, width), BF16)] * 2
-    scratch = [pltpu.VMEM((LANES, width), F32), pltpu.VMEM((LANES, width), F32), pltpu.VMEM((8, width), F32), pltpu.VMEM((STATE_CHUNKS * CHUNK, 2 * width), BF16), pltpu.VMEM((LANES, width), BF16)]
+    whole = pl.BlockSpec((LANES + 16, width), lambda i: (0, 0))
+    specs = [tok(width), pl.BlockSpec((STATE_CHUNKS, LANES, width), lambda i: (at(i), 0, 0)), pl.BlockSpec((STATE_CHUNKS, 8, width), lambda i: (at(i), 0, 0)), whole, whole, whole, tok(width), tok(width)]
+    shapes = [jax.ShapeDtypeStruct((tokens, width), BF16), jax.ShapeDtypeStruct((n_chunks, LANES, width), F32), jax.ShapeDtypeStruct((n_chunks, 8, width), F32)] + [jax.ShapeDtypeStruct((LANES + 16, width), BF16)] * 3 + [jax.ShapeDtypeStruct((tokens, width), BF16)] * 2
+    scratch = [pltpu.VMEM((LANES, width), F32), pltpu.VMEM((LANES, width), F32), pltpu.VMEM((8, width), F32), pltpu.VMEM((STATE_CHUNKS, CHUNK, 2 * width), BF16), pltpu.VMEM((LANES, width), BF16)]
     return specs, shapes, scratch
 
 
-def first_group(x_blk, w_bc, w_dt_rows, bias, a_neg, w_x, n_tiles):
+def first_group(who, x_blk, w_bc, w_dt_rows, bias, a_neg, w_x, n_tiles):
     tokens, d_model = x_blk.shape
     tile = STATE_CHUNKS * CHUNK
     width = 256 * n_tiles
@@ -311,17 +307,17 @@
     return pl.pallas_call(
         functools.partial(first_kernel, n_tiles),
         grid=(tokens // tile,),
-        in_specs=[tok(d_model), whole(w_bc), whole(w_dt_rows), whole(bias), whole(a_neg)] + w_specs(w_x, 0, n_tiles),
-        out_specs=[tok(2 * LANES), tok(LANES), tok(LANES), tok(LANES), tail, tail, pl.BlockSpec((8, LANES), lambda i: (0, 0))] + specs,
-        out_shape=[jax.ShapeDtypeStruct((tokens, 2 * LANES), BF16)] + [jax.ShapeDtypeStruct((tokens, LANES), BF16)] * 3 + [jax.ShapeDtypeStruct((16 * heads, tokens), BF16)] * 2 + [jax.ShapeDtypeStruct((8, LANES), F32)] + shapes,
+        in_specs=[SMEM, tok(d_model), whole(w_bc), whole(w_dt_rows), whole(bias), whole(a_neg)] + w_specs(w_x, 0, n_tiles),
+        out_specs=[tok(2 * LANES), tok(LANES), tok(LANES), tok(LANES), tail, tail] + specs,
+        out_shape=[jax.ShapeDtypeStruct((tokens, 2 * LANES), BF16)] + [jax.ShapeDtypeStruct((tokens, LANES), BF16)] * 3 + [jax.ShapeDtypeStruct((16 * heads, tokens), BF16)] * 2 + shapes,
         scratch_shapes=[pltpu.VMEM((LANES, d_model), BF16), pltpu.VMEM((8, LANES), F32), pltpu.VMEM((16 * heads, LANES), BF16)] + scratch,
         compiler_params=params(),
         cost_estimate=cost(2 * tokens * d_model * (1024 + width), 2 * tokens * d_model),
         name="first_group",
-    )(x_blk, w_bc, w_dt_rows, bias, a_neg, *([w_x] * n_tiles))
-
-
-def next_group(x_blk, w_x, first_tile, n_tiles, bc, sums, after, first_head):
+    )(who, x_blk, w_bc, w_dt_rows, bias, a_neg, *([w_x] * n_tiles))
+
+
+def next_group(who, x_blk, w_x, first_tile, n_tiles, bc, sums, after, first_head):
     tokens, d_model = x_blk.shape
     tile = STATE_CHUNKS * CHUNK
     at = lambda i: tokens // tile - 1 - i
@@ -330,14 +326,14 @@
     return pl.pallas_call(
         functools.partial(next_kernel, first_head, n_tiles),
         grid=(tokens // tile,),
-        in_specs=[tok(d_model), tok(2 * LANES), tok(LANES), tok(LANES), tok(LANES)] + w_specs(w_x, first_tile, n_tiles) + [ANY],
+        in_specs=[SMEM, tok(d_model), tok(2 * LANES), tok(LANES), tok(LANES), tok(LANES)] + w_specs(w_x, first_tile, n_tiles) + [ANY],
         out_specs=specs,
         out_shape=shapes,
         scratch_shapes=scratch,
         compiler_params=params(),
         cost_estimate=cost(2 * tokens * d_model * (512 + 256 * n_tiles), 2 * tokens * d_model),
         name="next_group",
-    )(x_blk, bc, *sums, *([w_x] * n_tiles), after)
+    )(who, x_blk, bc, *sums, *([w_x] * n_tiles), after)
 
 
 def add_products(who, acc, pieces, out_dtype):
@@ -364,13 +360,13 @@
     )(who, *args)
 
 
-def chunk_outputs(who, u, x_blk, w_z, first_tile, bc, sums, tails, local, got, logs, skip, after, first_head, n_pairs):
+def chunk_outputs(who, u, x_blk, w_z, first_tile, bc, sums, tails, local, got, skip, after, first_head, n_pairs):
     tokens, width = u.shape
     n_steps = tokens // (OUT_CHUNKS * CHUNK)
     gloc, suf, scaled, ends = local
     tail = pl.BlockSpec((tails[0].shape[0], OUT_CHUNKS * CHUNK), lambda i, who: (0, i))
     tok = lambda w: pl.BlockSpec((OUT_CHUNKS * CHUNK, w), lambda i, who: (i, 0))
-    state = pl.BlockSpec((LANES, width), lambda i, who: (0, 0))
+    state = pl.BlockSpec((LANES + 16, width), lambda i, who: (0, 0))
     small = lambda a: pl.BlockSpec(a.shape, lambda i, who: (0, 0))
     rows_out = tokens // 4
     return pl.pallas_call(
@@ -378,7 +374,7 @@
         grid_spec=pltpu.PrefetchScalarGridSpec(
             num_scalar_prefetch=1,
             grid=(n_steps,),
-            in_specs=[tok(width), tok(x_blk.shape[1]), tok(width), tok(width)] + [tok(2 * LANES), tok(LANES), tok(LANES), tail, tail, pl.BlockSpec((OUT_CHUNKS, LANES, width), lambda i, who: (i, 0, 0)), pl.BlockSpec((OUT_CHUNKS, 8, width), lambda i, who: (i, 0, 0)), state, state, state] + [small(v) for v in logs] + [small(skip), ANY] + [pl.BlockSpec((w_z.shape[0], 256), functools.partial(lambda t, i, who: (0, t), first_tile + t), pipeline_mode=pl.Buffered(1)) for t in range(n_pairs // 2)],
+            in_specs=[tok(width), tok(x_blk.shape[1]), tok(width), tok(width)] + [tok(2 * LANES), tok(LANES), tok(LANES), tail, tail, pl.BlockSpec((OUT_CHUNKS, LANES, width), lambda i, who: (i, 0, 0)), pl.BlockSpec((OUT_CHUNKS, 8, width), lambda i, who: (i, 0, 0)), state, state, state] + [small(skip), ANY] + [pl.BlockSpec((w_z.shape[0], 256), functools.partial(lambda t, i, who: (0, t), first_tile + t), pipeline_mode=pl.Buffered(1)) for t in range(n_pairs // 2)],
             out_specs=[pl.BlockSpec((rows_out, width), lambda i, who: (0, 0))] * 4,
             scratch_shapes=[pltpu.VMEM((LANES, width), F32), pltpu.VMEM((LANES, width), F32), pltpu.VMEM((8, width), F32), pltpu.VMEM((OUT_CHUNKS * CHUNK, width), BF16), pltpu.VMEM((LANES, width), BF16), pltpu.VMEM((LANES, 2 * width), BF16)] + [pltpu.VMEM((OUT_CHUNKS, LANES, width), BF16)] * 2 + [pltpu.VMEM((OUT_CHUNKS * CHUNK, width), BF16)],
         ),
@@ -386,7 +382,7 @@
         compiler_params=params(),
         cost_estimate=cost(24 * tokens * width * 256, 8 * tokens * width),
         name="outputs",
-    )(who, u, x_blk, scaled, ends, bc, sums[0], sums[1], *tails, gloc, suf, *got, *logs, skip, after, *([w_z] * (n_pairs // 2)))
+    )(who, u, x_blk, scaled, ends, bc, sums[0], sums[1], *tails, gloc, suf, *got, skip, after, *([w_z] * (n_pairs // 2)))
 
 
 def solution(mesh):
@@ -418,34 +414,33 @@
         who = jnp.stack([tp_index, sp_index])
         skip = d_skip[None, :]
 
-        def exchange(s_fwd, s_bwd):
-            return [swap(jnp.where(sp_index < (sp_index ^ s), s_fwd, s_bwd), 'sp', s) for s in (1, 2, 3)]
+        def exchange(states):
+            return [swap(states[s - 1], 'sp', s) for s in (1, 2, 3)]
 
         def send(pieces):
             return [pieces[0]] + [swap(pieces[s], 'tp', s) for s in (1, 2, 3)]
 
-        bc, cum3, nexc3, dt3, tail1, tail2, block_log, u_a, gloc, suf, s_fwd, s_bwd, ut, vf = first_group(x_blk, w_bc, w_dt.T, dt_bias[None, :], a_neg[None, :], w_x, n_a)
+        bc, cum3, nexc3, dt3, tail1, tail2, u_a, gloc, suf, *states, ut, vf = first_group(who, x_blk, w_bc, w_dt.T, dt_bias[None, :], a_neg[None, :], w_x, n_a)
         local_a = (gloc, suf, ut, vf)
-        logs = [swap(block_log, 'sp', s) for s in (1, 2, 3)]
-        got_a = exchange(s_fwd, s_bwd)
-        one, = later((one,), block_log)
+        got_a = exchange(states)
+        one, = later((one,), bc)
         w_one = plane(one)
-        u_b, gloc, suf, s_fwd, s_bwd, ut, vf = next_group(x_blk, w_x, t_b, n_b, bc, (cum3, nexc3, dt3), one, head_b)
+        u_b, gloc, suf, *states, ut, vf = next_group(who, x_blk, w_x, t_b, n_b, bc, (cum3, nexc3, dt3), one, head_b)
         local_b = (gloc, suf, ut, vf)
-        got_b = exchange(s_fwd, s_bwd)
-        g_a = chunk_outputs(who, u_a, x_blk, w_z, t_a, bc, (cum3, nexc3), (tail1, tail2), local_a, got_a, logs, skip, u_b, 0, 2 * n_a)
+        got_b = exchange(states)
+        g_a = chunk_outputs(who, u_a, x_blk, w_z, t_a, bc, (cum3, nexc3), (tail1, tail2), local_a, got_a, skip, u_b, 0, 2 * n_a)
         got_g_a = send(g_a)
         two, = later((two,), g_a[0])
         three = swap(two, 'tp', 1)
         w_two = plane(two)
-        g_b = chunk_outputs(who, u_b, x_blk, w_z, t_b, bc, (cum3, nexc3), (tail1, tail2), local_b, got_b, logs, skip, two, head_b, 2 * n_b)
+        g_b = chunk_outputs(who, u_b, x_blk, w_z, t_b, bc, (cum3, nexc3), (tail1, tail2), local_b, got_b, skip, two, head_b, 2 * n_b)
         got_g_b = send(g_b)
         w_three = plane(three)
 
-        total = add_products(who, x_blk, [(got_g_a[0], w_out, t_a), (got_g_b[0], w_out, t_b)], F32)
-        total = add_products(who, total, [(got_g_a[1], w_one, t_a), (got_g_b[1], w_one, t_b)], F32)
-        total = add_products(who, total, [(got_g_a[2], w_two, t_a), (got_g_b[2], w_two, t_b)], F32)
-        return add_products(who, total, [(got_g_a[3], w_three, t_a), (got_g_b[3], w_three, t_b)], BF16)
+        total = add_products(who, x_blk, [(got_g_a[0], w_out, t_a), (got_g_b[0], w_out, t_b), (got_g_a[1], w_one, t_a)], F32)
+        total = add_products(who, total, [(got_g_a[2], w_two, t_a), (got_g_b[1], w_one, t_b)], F32)
+        total = add_products(who, total, [(got_g_b[2], w_two, t_b), (got_g_a[3], w_three, t_a)], F32)
+        return add_products(who, total, [(got_g_b[3], w_three, t_b)], BF16)
 
     in_specs = (P(('dp', 'sp'), None), P(None, 'tp'), P(None, 'tp'), P(None, None), P(None, 'tp'), P('tp'), P('tp'), P('tp'), P('tp', None))
     out_specs = P(('dp', 'sp', 'tp'), None)

time: 306 us -> 293 us (0.958)
  local copies, waits for them, and re-layouts: 38.3 us -> 7.8 us
  Pallas kernels: 131 us -> 142 us
  waiting for transfers between devices: 105 us -> 110 us
  starting transfers between devices: 15.9 us -> 19 us
    unnamed x62 -> x22, local copies, waits for them, and re-layouts: 37.1 us -> 6.61 us
    pallas_call x4, Pallas kernels: 24.2 us -> 43.7 us  [add_products(): pl.pallas_call(body, grid_spec=pltpu.PrefetchScalarGridSpec(num_scalar_pr...]
    pallas_call x2, Pallas kernels: 56.2 us -> 47.7 us  [chunk_outputs(): pl.pallas_call(functools.partial(out_kernel, first_head, n_pairs), grid_s...]
    ppermute x18 -> x15, waiting for transfers between devices: 105 us -> 110 us  [swap(): return lax.ppermute(val, axis, [(i, i ^ slot) for i in range(4)])]
    pallas_call x1, Pallas kernels: 26.4 us -> 23 us  [next_group(): pl.pallas_call(functools.partial(next_kernel, first_head, n_tiles), grid=...]
    pallas_call x1, Pallas kernels: 24.4 us -> 27.6 us  [first_group(): pl.pallas_call(functools.partial(first_kernel, n_tiles), grid=(tokens //...]
    ppermute x18 -> x15, starting transfers between devices: 15.6 us -> 18.8 us  [swap(): return lax.ppermute(val, axis, [(i, i ^ slot) for i in range(4)])]
  transfers between devices with their start and end apart: 21 -> 18, of which waited for: 6 -> 7; matrix products, arithmetic and copies ran while one was open for 1% -> 0% of each run, Pallas kernels for 41% -> 45%
where the time goes in v5:
time: 293 us; the launch traced here: 292 us
  Pallas kernels  142 us (48%)
  waiting for transfers between devices  110 us (38%)
  starting transfers between devices  19 us (6%)
  between operations  13.2 us (5%)
  local copies, waits for them, and re-layouts  7.8 us (3%)
    ppermute x15, waiting for transfers between devices, swap(): return lax.ppermute(val, axis, [(i, i ^ slot) for i in range(4)])  110 us
    pallas_call x2, Pallas kernels, chunk_outputs(): pl.pallas_call(functools.partial(out_kernel, first_head, n_pairs), grid_s...  47.7 us
    pallas_call x4, Pallas kernels, add_products(): pl.pallas_call(body, grid_spec=pltpu.PrefetchScalarGridSpec(num_scalar_pr...  43.7 us
    pallas_call x1, Pallas kernels, first_group(): pl.pallas_call(functools.partial(first_kernel, n_tiles), grid=(tokens //...  27.6 us
    pallas_call x1, Pallas kernels, next_group(): pl.pallas_call(functools.partial(next_kernel, first_head, n_tiles), grid=...  23 us
    ppermute x15, starting transfers between devices, swap(): return lax.ppermute(val, axis, [(i, i ^ slot) for i in range(4)])  18.8 us
    unnamed x22, local copies, waits for them, and re-layouts  6.61 us
  transfers between devices with their start and end apart: 18, of which 7 were waited for; matrix products, arithmetic and copies ran while one was open for 0% of the time, Pallas kernels for 45%

profile of v5, /device:TPU:12, one launch (start us, length us, event | category | flops | bytes accessed | tf_op | source)
XLA Modules:
  0.0 292.5 jit_solution(15059050824886560664)
XLA Ops:
  6.5 1.2 constant_dynamic-slice_fusion
  8.8 27.6 %first_group.1 = (bf16[2048,256]{1,0:T(8,128)(2,1)}, bf16[2048,128]{1,0:T(8,128)(2,1)}, bf16[2048,128]{1,0:T(8,128)(2,1)}, bf16[2048,128]{1,0:T(8,128)(2,1)}, bf...) custom-call(s32[2]{0:T(128)} %pad_add_fusion.who_ref, ...), custom_call_target="tpu_custom_call" | custom-call | flops 16106127360 | bytes 10485760 | tf_op jit(solution)/shard_map/first_group/pallas_call | solution.py:307
  36.5 0.9 copy-done.1
  37.4 2.7 collective-permute-start.7
  40.6 1.4 collective-permute-start.2
  42.0 23.0 %next_group.1 = (bf16[2048,768]{1,0:T(8,128)(2,1)}, f32[16,128,768]{2,1,0:T(8,128)}, f32[16,8,768]{2,1,0:T(8,128)}, bf16[144,768]{1,0:T(8,128)(2,1)}, bf16[144,7...) custom-call(s32[2]{0:T(128)} %pad_add_fusion.who_ref, ...), custom_call_target="tpu_custom_call" | custom-call | flops 13421772800 | bytes 10485760 | tf_op jit(solution)/shard_map/next_group/pallas_call | solution.py:326
  65.0 0.6 copy-done.9
  65.7 20.4 %outputs.2 = (bf16[512,512]{1,0:T(8,128)(2,1)}, bf16[512,512]{1,0:T(8,128)(2,1)}, bf16[512,512]{1,0:T(8,128)(2,1)}, bf16[512,512]{1,0:T(8,128)(2,1)}) custom-call(s32[2]{0:T(128)} %pad_add_fusion.who_ref, bf16[2048,512]{1,0:T(8,128)(2,1)} %get-tuple-element.37.u_ref, bf16[2048,2560]{1,0:T(8,128)(2,1)} %refs_0_.9, ...), custom_call_target="tpu_custom_call" | custom-call | flops 6442450944 | bytes 8388608 | tf_op jit(solution)/shard_map/outputs/pallas_call | solution.py:372
  86.1 0.9 copy-done
  87.2 1.8 collective-permute-start.13
  89.0 19.1 %collective-permute-done.13 = bf16[160,2560]{1,0:T(8,128)(2,1)S(1)} collective-permute-done((bf16[160,2560]{1,0:T(8,128)(2,1)}, bf16[160,2560]{1,0:T(8,128)(2,1)S(1)}, u32[]{:S(2)}, u32[]{:S(2)}) %collective-permute-start.13) | collective-permute-done | bytes 819232 | tf_op jit(solution)/shard_map/ppermute | solution.py:392
  108.1 0.9 copy-done.2
  109.6 1.3 collective-permute-start.6
  110.9 1.6 collective-permute-start.8
  112.5 9.4 %collective-permute-done.5.r2_ref = bf16[144,768]{1,0:T(8,128)(2,1)S(1)} collective-permute-done((bf16[144,768]{1,0:T(8,128)(2,1)}, bf16[144,768]{1,0:T(8,128)(2,1)S(1)}, u32[]{:S(2)}, u32[]{:S(2)}) %collective-permute-start.5) | collective-permute-done | bytes 221216 | tf_op jit(solution)/shard_map/ppermute | solution.py:392
  121.9 7.3 %collective-permute-done.6.r3_ref = bf16[144,768]{1,0:T(8,128)(2,1)S(1)} collective-permute-done((bf16[144,768]{1,0:T(8,128)(2,1)}, bf16[144,768]{1,0:T(8,128)(2,1)S(1)}, u32[]{:S(2)}, u32[]{:S(2)}) %collective-permute-start.6) | collective-permute-done | bytes 221216 | tf_op jit(solution)/shard_map/ppermute | solution.py:392
  129.2 0.7 copy-done.8
  129.9 27.3 %outputs.3 = (bf16[512,768]{1,0:T(8,128)(2,1)}, bf16[512,768]{1,0:T(8,128)(2,1)}, bf16[512,768]{1,0:T(8,128)(2,1)}, bf16[512,768]{1,0:T(8,128)(2,1)}) custom-call(s32[2]{0:T(128)} %pad_add_fusion.who_ref, bf16[2048,768]{1,0:T(8,128)(2,1)} %get-tuple-element.52.after_ref.u_ref, bf16[2048,2560]{1,0:T(8,128)(2,1)} %refs_0_.9, ...), custom_call_target="tpu_custom_call" | custom-call | flops 9663676416 | bytes 12582912 | tf_op jit(solution)/shard_map/outputs/pallas_call | solution.py:372
  157.2 3.5 %collective-permute-start.10 = (bf16[512,768]{1,0:T(8,128)(2,1)}, bf16[512,768]{1,0:T(8,128)(2,1)}, u32[]{:S(2)}, u32[]{:S(2)}) collective-permute-start(bf16[512,768]{1,0:T(8,128)(2,1)} %get-tuple-element.65), channel_id=1, source_target_pairs={{0,4},{4,0},{8,12},{12,8},{1,5},{5,1},{9,13},{13,9},{2,6},{6,2},{1... | collective-permute-start | bytes 2359304 | tf_op jit(solution)/shard_map/ppermute | solution.py:392
  160.8 2.9 collective-permute-start.11
  163.7 0.8 copy-done.5
  164.5 2.0 collective-permute-start.14
  166.5 12.4 %add_products.4.refs_0_ = f32[512,2560]{1,0:T(8,128)} custom-call(s32[2]{0:T(128)} %pad_add_fusion.who_ref, bf16[2048,2560]{1,0:T(8,128)(2,1)} %refs_0_.9, bf16[512,512]{1,0:T(8,128)(2,1)} %get-tuple-element.53.refs_1_, bf16[1280,2560]{1,0:T(8,128)(2,1)} %refs_7_.1, bf16[1280,2560]{1,0:T(8,128)(2,1)} %refs_7_.1, bf16[512,768]{1,0:T(8,128)(2,1)} %get-tuple-element.62.refs_4_, ...), custom_call_target="tpu_custom_call" | custom-call | flops 4697620480 | bytes 2621440 | tf_op jit(solution)/shard_map/add_products/pallas_call | solution.py:353
  178.9 7.7 %collective-permute-done.9.refs_1_ = bf16[512,512]{1,0:T(8,128)(2,1)} collective-permute-done((bf16[512,512]{1,0:T(8,128)(2,1)}, bf16[512,512]{1,0:T(8,128)(2,1)}, u32[]{:S(2)}, u32[]{:S(2)}) %collective-permute-start.9) | collective-permute-done | bytes 524320 | tf_op jit(solution)/shard_map/ppermute | solution.py:392
  186.6 4.4 %collective-permute-done.10.refs_4_ = bf16[512,768]{1,0:T(8,128)(2,1)} collective-permute-done((bf16[512,768]{1,0:T(8,128)(2,1)}, bf16[512,768]{1,0:T(8,128)(2,1)}, u32[]{:S(2)}, u32[]{:S(2)}) %collective-permute-start.10) | collective-permute-done | bytes 786464 | tf_op jit(solution)/shard_map/ppermute | solution.py:392
  191.0 11.2 %add_products.5.refs_0_ = f32[512,2560]{1,0:T(8,128)} custom-call(s32[2]{0:T(128)} %pad_add_fusion.who_ref, f32[512,2560]{1,0:T(8,128)} %add_products.4.refs_0_, bf16[512,512]{1,0:T(8,128)(2,1)} %collective-permute-done.9.refs_1_, bf16[1280,2560]{1,0:T(8,128)(2,1)} %all-gather.6.cloned.1.call-done.refs_2_.refs_3_.refs_4_, ...), custom_call_target="tpu_custom_call" | custom-call | flops 3355443200 | bytes 2621440 | tf_op jit(solution)/shard_map/add_products/pallas_call | solution.py:353
  202.2 57.5 %collective-permute-done.12.refs_5_ = bf16[512,512]{1,0:T(8,128)(2,1)} collective-permute-done((bf16[512,512]{1,0:T(8,128)(2,1)}, bf16[512,512]{1,0:T(8,128)(2,1)}, u32[]{:S(2)}, u32[]{:S(2)}) %collective-permute-start.12) | collective-permute-done | bytes 524320 | tf_op jit(solution)/shard_map/ppermute | solution.py:392
  259.7 0.9 copy-done.3
  260.6 11.1 %add_products.6.refs_0_ = f32[512,2560]{1,0:T(8,128)} custom-call(s32[2]{0:T(128)} %pad_add_fusion.who_ref, f32[512,2560]{1,0:T(8,128)} %add_products.5.refs_0_, bf16[512,768]{1,0:T(8,128)(2,1)} %copy-done.3, bf16[1280,2560]{1,0:T(8,128)(2,1)} %all-gather.6.cloned.1.call-done.refs_2_.refs_3_.refs_4_, ...), custom_call_target="tpu_custom_call" | custom-call | flops 3355443200 | bytes 2621440 | tf_op jit(solution)/shard_map/add_products/pallas_call | solution.py:353
  271.7 4.4 %collective-permute-done.14.refs_1_ = bf16[512,768]{1,0:T(8,128)(2,1)S(1)} collective-permute-done((bf16[512,768]{1,0:T(8,128)(2,1)}, bf16[512,768]{1,0:T(8,128)(2,1)S(1)}, u32[]{:S(2)}, u32[]{:S(2)}) %collective-permute-start.14) | collective-permute-done | bytes 786464 | tf_op jit(solution)/shard_map/ppermute | solution.py:392
  276.1 0.9 copy-done.4
  277.0 9.0 %add_products.7 = bf16[512,2560]{1,0:T(8,128)(2,1)} custom-call(s32[2]{0:T(128)} %pad_add_fusion.who_ref, f32[512,2560]{1,0:T(8,128)} %add_products.6.refs_0_, bf16[512,768]{1,0:T(8,128)(2,1)} %copy-done.4, bf16[1280,2560]{1,0:T(8,128)(2,1)} %all-gather.8.cloned.1.call-done.refs_6_.refs_7_.refs_2_.refs_3_.refs_4_, ...), custom_call_target="tpu_custom_call" | custom-call | flops 2013265920 | bytes 2621440 | tf_op jit(solution)/shard_map/add_products/pallas_call | solution.py:353
  (39 shorter events, 2.6 us)
Async XLA Ops:
  6.5 160.0 %all-gather.4.cloned.1.call-start = ((), (), s32[]{:S(2)}) async-start(), calls=%async_computation | async-start | bytes 7372800 | tf_op jit(solution)/shard_map/all_gather | solution.py:408
  7.7 28.7 %collective-permute-start.3 = (bf16[160,2560]{1,0:T(8,128)(2,1)S(1)}, bf16[160,2560]{1,0:T(8,128)(2,1)S(1)}, u32[]{:S(2)}, u32[]{:S(2)}) collective-permute-start(bf16[160,2560]{1,0:T(8,128)(2,1)S(1)} %constant_dynamic-slice_fusion), channel_id=1, source_target_pairs={{0,4},{4,0},{8,12},{12,8},{1,5},{5,1},{9,13},{13,9},{2,6},{6,2},{1... | collective-permute-start | bytes 2457608 | tf_op jit(solution)/shard_map/ppermute | solution.py:392
  36.5 0.9 copy-start.1
  37.4 153.6 %all-gather.6.cloned.1.call-start = ((), (), s32[]{:S(2)}) async-start(), calls=%async_computation.1 | async-start | bytes 7372800 | tf_op jit(solution)/shard_map/all_gather | solution.py:408
  37.4 48.6 %collective-permute-start.7 = (bf16[160,2560]{1,0:T(8,128)(2,1)S(1)}, bf16[160,2560]{1,0:T(8,128)(2,1)S(1)}, u32[]{:S(2)}, u32[]{:S(2)}) collective-permute-start(bf16[160,2560]{1,0:T(8,128)(2,1)S(1)} %constant_dynamic-slice_fusion), channel_id=1, source_target_pairs={{0,8},{4,12},{8,0},{12,4},{1,9},{5,13},{9,1},{13,5},{2,10},{6,14},... | collective-permute-start | bytes 2457608 | tf_op jit(solution)/shard_map/ppermute | solution.py:392
  40.1 24.9 %collective-permute-start = (bf16[144,512]{1,0:T(8,128)(2,1)}, bf16[144,512]{1,0:T(8,128)(2,1)S(1)}, u32[]{:S(2)}, u32[]{:S(2)}) collective-permute-start(bf16[144,512]{1,0:T(8,128)(2,1)} %get-tuple-element.47), channel_id=1, source_target_pairs={{0,1},{1,0},{2,3},{3,2},{4,5},{5,4},{6,7},{7,6},{8,9},{9,8},{10,11... | collective-permute-start | bytes 442376 | tf_op jit(solution)/shard_map/ppermute | solution.py:392
  40.1 24.9 %collective-permute-start.1 = (bf16[144,512]{1,0:T(8,128)(2,1)}, bf16[144,512]{1,0:T(8,128)(2,1)S(1)}, u32[]{:S(2)}, u32[]{:S(2)}) collective-permute-start(bf16[144,512]{1,0:T(8,128)(2,1)} %get-tuple-element.48), channel_id=1, source_target_pairs={{0,2},{1,3},{2,0},{3,1},{4,6},{5,7},{6,4},{7,5},{8,10},{9,11},{10,... | collective-permute-start | bytes 442376 | tf_op jit(solution)/shard_map/ppermute | solution.py:392
  40.6 24.4 %collective-permute-start.2 = (bf16[144,512]{1,0:T(8,128)(2,1)}, bf16[144,512]{1,0:T(8,128)(2,1)}, u32[]{:S(2)}, u32[]{:S(2)}) collective-permute-start(bf16[144,512]{1,0:T(8,128)(2,1)} %get-tuple-element.49), channel_id=1, source_target_pairs={{0,3},{1,2},{2,1},{3,0},{4,7},{5,6},{6,5},{7,4},{8,11},{9,10},{10,... | collective-permute-start | bytes 442376 | tf_op jit(solution)/shard_map/ppermute | solution.py:392
  65.0 0.7 copy-start.9
  65.0 0.7 copy-start.10
  86.1 0.9 copy-start
  87.0 172.7 %all-gather.8.cloned.1.call-start = ((), (), s32[]{:S(2)}) async-start(), calls=%async_computation.2 | async-start | bytes 7372800 | tf_op jit(solution)/shard_map/all_gather | solution.py:408
  87.2 20.9 %collective-permute-start.13 = (bf16[160,2560]{1,0:T(8,128)(2,1)}, bf16[160,2560]{1,0:T(8,128)(2,1)S(1)}, u32[]{:S(2)}, u32[]{:S(2)}) collective-permute-start(bf16[160,2560]{1,0:T(8,128)(2,1)} %copy-done), channel_id=1, source_target_pairs={{0,4},{4,0},{8,12},{12,8},{1,5},{5,1},{9,13},{13,9},{2,6},{6,2},{1... | collective-permute-start | bytes 2457608 | tf_op jit(solution)/shard_map/ppermute | solution.py:392
  108.1 0.9 copy-start.2
  109.0 3.5 %collective-permute-start.4 = (bf16[144,768]{1,0:T(8,128)(2,1)}, bf16[144,768]{1,0:T(8,128)(2,1)S(1)}, u32[]{:S(2)}, u32[]{:S(2)}) collective-permute-start(bf16[144,768]{1,0:T(8,128)(2,1)} %get-tuple-element.58), channel_id=1, source_target_pairs={{0,1},{1,0},{2,3},{3,2},{4,5},{5,4},{6,7},{7,6},{8,9},{9,8},{10,11... | collective-permute-start | bytes 663560 | tf_op jit(solution)/shard_map/ppermute | solution.py:392
  109.1 12.8 %collective-permute-start.5 = (bf16[144,768]{1,0:T(8,128)(2,1)}, bf16[144,768]{1,0:T(8,128)(2,1)S(1)}, u32[]{:S(2)}, u32[]{:S(2)}) collective-permute-start(bf16[144,768]{1,0:T(8,128)(2,1)} %get-tuple-element.59), channel_id=1, source_target_pairs={{0,2},{1,3},{2,0},{3,1},{4,6},{5,7},{6,4},{7,5},{8,10},{9,11},{10,... | collective-permute-start | bytes 663560 | tf_op jit(solution)/shard_map/ppermute | solution.py:392
  109.6 19.6 %collective-permute-start.6 = (bf16[144,768]{1,0:T(8,128)(2,1)}, bf16[144,768]{1,0:T(8,128)(2,1)S(1)}, u32[]{:S(2)}, u32[]{:S(2)}) collective-permute-start(bf16[144,768]{1,0:T(8,128)(2,1)} %get-tuple-element.60), channel_id=1, source_target_pairs={{0,3},{1,2},{2,1},{3,0},{4,7},{5,6},{6,5},{7,4},{8,11},{9,10},{10,... | collective-permute-start | bytes 663560 | tf_op jit(solution)/shard_map/ppermute | solution.py:392
  110.9 52.8 %collective-permute-start.8 = (bf16[512,512]{1,0:T(8,128)(2,1)}, bf16[512,512]{1,0:T(8,128)(2,1)S(1)}, u32[]{:S(2)}, u32[]{:S(2)}) collective-permute-start(bf16[512,512]{1,0:T(8,128)(2,1)} %get-tuple-element.63), channel_id=1, source_target_pairs={{0,4},{4,0},{8,12},{12,8},{1,5},{5,1},{9,13},{13,9},{2,6},{6,2},{1... | collective-permute-start | bytes 1572872 | tf_op jit(solution)/shard_map/ppermute | solution.py:392
  112.5 16.7 %copy-start.6 = (bf16[144,768]{1,0:T(8,128)(2,1)}, bf16[144,768]{1,0:T(8,128)(2,1)S(1)}, u32[]{:S(2)}) copy-start(bf16[144,768]{1,0:T(8,128)(2,1)S(1)} %collective-permute-done.4.r1_ref) | copy-start | bytes 663556
  121.9 7.3 %copy-start.7 = (bf16[144,768]{1,0:T(8,128)(2,1)}, bf16[144,768]{1,0:T(8,128)(2,1)S(1)}, u32[]{:S(2)}) copy-start(bf16[144,768]{1,0:T(8,128)(2,1)S(1)} %collective-permute-done.5.r2_ref) | copy-start | bytes 663556
  129.2 0.7 copy-start.8
  157.2 33.8 %collective-permute-start.10 = (bf16[512,768]{1,0:T(8,128)(2,1)}, bf16[512,768]{1,0:T(8,128)(2,1)}, u32[]{:S(2)}, u32[]{:S(2)}) collective-permute-start(bf16[512,768]{1,0:T(8,128)(2,1)} %get-tuple-element.65), channel_id=1, source_target_pairs={{0,4},{4,0},{8,12},{12,8},{1,5},{5,1},{9,13},{13,9},{2,6},{6,2},{1... | collective-permute-start | bytes 2359304 | tf_op jit(solution)/shard_map/ppermute | solution.py:392
  160.7 25.8 %collective-permute-start.9 = (bf16[512,512]{1,0:T(8,128)(2,1)}, bf16[512,512]{1,0:T(8,128)(2,1)}, u32[]{:S(2)}, u32[]{:S(2)}) collective-permute-start(bf16[512,512]{1,0:T(8,128)(2,1)} %get-tuple-element.64), channel_id=1, source_target_pairs={{0,8},{4,12},{8,0},{12,4},{1,9},{5,13},{9,1},{13,5},{2,10},{6,14},... | collective-permute-start | bytes 1572872 | tf_op jit(solution)/shard_map/ppermute | solution.py:392
  160.8 98.9 %collective-permute-start.11 = (bf16[512,768]{1,0:T(8,128)(2,1)}, bf16[512,768]{1,0:T(8,128)(2,1)S(1)}, u32[]{:S(2)}, u32[]{:S(2)}) collective-permute-start(bf16[512,768]{1,0:T(8,128)(2,1)} %get-tuple-element.66), channel_id=1, source_target_pairs={{0,8},{4,12},{8,0},{12,4},{1,9},{5,13},{9,1},{13,5},{2,10},{6,14},... | collective-permute-start | bytes 2359304 | tf_op jit(solution)/shard_map/ppermute | solution.py:392
  163.7 96.0 %collective-permute-start.12 = (bf16[512,512]{1,0:T(8,128)(2,1)}, bf16[512,512]{1,0:T(8,128)(2,1)}, u32[]{:S(2)}, u32[]{:S(2)}) collective-permute-start(bf16[512,512]{1,0:T(8,128)(2,1)} %get-tuple-element.67), channel_id=1, source_target_pairs={{0,12},{4,8},{8,4},{12,0},{1,13},{5,9},{9,5},{13,1},{2,14},{6,10},... | collective-permute-start | bytes 1572872 | tf_op jit(solution)/shard_map/ppermute | solution.py:392
  163.7 0.8 copy-start.5
  164.5 111.6 %collective-permute-start.14 = (bf16[512,768]{1,0:T(8,128)(2,1)}, bf16[512,768]{1,0:T(8,128)(2,1)S(1)}, u32[]{:S(2)}, u32[]{:S(2)}) collective-permute-start(bf16[512,768]{1,0:T(8,128)(2,1)} %get-tuple-element.68), channel_id=1, source_target_pairs={{0,12},{4,8},{8,4},{12,0},{1,13},{5,9},{9,5},{13,1},{2,14},{6,10},... | collective-permute-start | bytes 2359304 | tf_op jit(solution)/shard_map/ppermute | solution.py:392
  259.7 0.9 copy-start.3
  276.1 0.9 copy-start.4
Sparse Core Ops, SparseCore 0:
  37.5 47.4 all-gather.3
  87.1 54.0 all-gather.5
  143.2 45.4 all-gather.7

commit v6 on v5

--- a/solution.py
+++ b/solution.py
@@ -14,7 +14,7 @@
 STATE_CHUNKS = 4
 OUT_CHUNKS = 2
 OUT_AHEAD = 2
-SUM_MIB = 62
+SUM_MIB = 56
 F32 = jnp.float32
 BF16 = jnp.bfloat16
 
@@ -63,6 +63,8 @@
         second = rest.astype(BF16)
         third = (rest - second.astype(F32)).astype(BF16)
         sums.append(sum(jnp.dot(tri, t, preferred_element_type=F32) for t in (first, second, third)))
+    for t in range(1, n_tiles):
+        project_tile(u_ref, x_ref, refs[t], t)
     one = jnp.where(lane < 3 * SLOT + 3, 1.0, 0.0)
     for part, cum in zip(parts, sums):
         cum_ref[part, :] = split3(cum, lane, one)
@@ -77,8 +79,7 @@
 def first_kernel(n_tiles, who_ref, *refs):
     prep_kernel(n_tiles, *refs)
     bc_ref, cum_ref, nexc_ref, dt_ref, _, _, u_ref = refs[5 + n_tiles:12 + n_tiles]
-    project = lambda t: project_tile(u_ref, refs[0], refs[5 + t], t) if t else None
-    state_kernel(0, 2 * n_tiles, project, u_ref, bc_ref, cum_ref, nexc_ref, dt_ref, *refs[12 + n_tiles:-8], who_ref, *refs[-5:])
+    state_kernel(0, 2 * n_tiles, lambda t: None, u_ref, bc_ref, cum_ref, nexc_ref, dt_ref, *refs[12 + n_tiles:-8], who_ref, *refs[-5:])
 
 
 def next_kernel(first_head, n_tiles, who_ref, x_ref, bc_ref, cum_ref, nexc_ref, dt_ref, *refs):
@@ -439,8 +440,8 @@
 
         total = add_products(who, x_blk, [(got_g_a[0], w_out, t_a), (got_g_b[0], w_out, t_b), (got_g_a[1], w_one, t_a)], F32)
         total = add_products(who, total, [(got_g_a[2], w_two, t_a), (got_g_b[1], w_one, t_b)], F32)
-        total = add_products(who, total, [(got_g_b[2], w_two, t_b), (got_g_a[3], w_three, t_a)], F32)
-        return add_products(who, total, [(got_g_b[3], w_three, t_b)], BF16)
+        total = add_products(who, total, [(got_g_b[2], w_two, t_b)], F32)
+        return add_products(who, total, [(got_g_a[3], w_three, t_a), (got_g_b[3], w_three, t_b)], BF16)
 
     in_specs = (P(('dp', 'sp'), None), P(None, 'tp'), P(None, 'tp'), P(None, None), P(None, 'tp'), P('tp'), P('tp'), P('tp'), P('tp', None))
     out_specs = P(('dp', 'sp', 'tp'), None)

time: 293 us -> 291 us (level)
  Pallas kernels: 142 us -> 139 us
    pallas_call x1, Pallas kernels: 27.6 us -> 24.5 us  [first_group(): pl.pallas_call(functools.partial(first_kernel, n_tiles), grid=(tokens //...]
    unnamed x22 -> x26, local copies, waits for them, and re-layouts: 6.61 us -> 6.73 us
  transfers between devices with their start and end apart: 18 -> 18, of which waited for: 7 -> 8; matrix products, arithmetic and copies ran while one was open for 0% -> 0% of each run, Pallas kernels for 45% -> 44%
where the time goes in v6:
time: 291 us; the launch traced here: 290 us
  Pallas kernels  139 us (48%)
  waiting for transfers between devices  111 us (38%)
  starting transfers between devices  19 us (7%)
  between operations  13.2 us (5%)
  local copies, waits for them, and re-layouts  7.92 us (3%)
    ppermute x15, waiting for transfers between devices, swap(): return lax.ppermute(val, axis, [(i, i ^ slot) for i in range(4)])  111 us
    pallas_call x2, Pallas kernels, chunk_outputs(): pl.pallas_call(functools.partial(out_kernel, first_head, n_pairs), grid_s...  47.7 us
    pallas_call x4, Pallas kernels, add_products(): pl.pallas_call(body, grid_spec=pltpu.PrefetchScalarGridSpec(num_scalar_pr...  43.5 us
    pallas_call x1, Pallas kernels, first_group(): pl.pallas_call(functools.partial(first_kernel, n_tiles), grid=(tokens //...  24.5 us
    pallas_call x1, Pallas kernels, next_group(): pl.pallas_call(functools.partial(next_kernel, first_head, n_tiles), grid=...  23 us
    ppermute x15, starting transfers between devices, swap(): return lax.ppermute(val, axis, [(i, i ^ slot) for i in range(4)])  18.8 us
    unnamed x26, local copies, waits for them, and re-layouts  6.73 us
  transfers between devices with their start and end apart: 18, of which 8 were waited for; matrix products, arithmetic and copies ran while one was open for 0% of the time, Pallas kernels for 44%

profile of v6, /device:TPU:12, one launch (start us, length us, event | category | flops | bytes accessed | tf_op | source)
XLA Modules:
  0.0 290.4 jit_solution(11417997136137489620)
XLA Ops:
  6.5 1.2 constant_dynamic-slice_fusion
  8.9 24.5 %first_group.1 = (bf16[2048,256]{1,0:T(8,128)(2,1)}, bf16[2048,128]{1,0:T(8,128)(2,1)}, bf16[2048,128]{1,0:T(8,128)(2,1)}, bf16[2048,128]{1,0:T(8,128)(2,1)}, bf...) custom-call(s32[2]{0:T(128)} %pad_add_fusion.who_ref, ...), custom_call_target="tpu_custom_call" | custom-call | flops 16106127360 | bytes 10485760 | tf_op jit(solution)/shard_map/first_group/pallas_call | solution.py:308
  33.4 0.9 copy-done.1
  34.4 2.7 collective-permute-start.7
  37.6 1.3 collective-permute-start.2
  38.9 23.0 %next_group.1 = (bf16[2048,768]{1,0:T(8,128)(2,1)}, f32[16,128,768]{2,1,0:T(8,128)}, f32[16,8,768]{2,1,0:T(8,128)}, bf16[144,768]{1,0:T(8,128)(2,1)}, bf16[144,7...) custom-call(s32[2]{0:T(128)} %pad_add_fusion.who_ref, ...), custom_call_target="tpu_custom_call" | custom-call | flops 13421772800 | bytes 10485760 | tf_op jit(solution)/shard_map/next_group/pallas_call | solution.py:327
  62.7 20.4 %outputs.2 = (bf16[512,512]{1,0:T(8,128)(2,1)}, bf16[512,512]{1,0:T(8,128)(2,1)}, bf16[512,512]{1,0:T(8,128)(2,1)}, bf16[512,512]{1,0:T(8,128)(2,1)}) custom-call(s32[2]{0:T(128)} %pad_add_fusion.who_ref, bf16[2048,512]{1,0:T(8,128)(2,1)} %get-tuple-element.37.u_ref, bf16[2048,2560]{1,0:T(8,128)(2,1)} %refs_0_.9, ...), custom_call_target="tpu_custom_call" | custom-call | flops 6442450944 | bytes 8388608 | tf_op jit(solution)/shard_map/outputs/pallas_call | solution.py:373
  83.1 0.9 copy-done
  84.2 1.7 collective-permute-start.13
  86.0 19.1 %collective-permute-done.13 = bf16[160,2560]{1,0:T(8,128)(2,1)S(1)} collective-permute-done((bf16[160,2560]{1,0:T(8,128)(2,1)}, bf16[160,2560]{1,0:T(8,128)(2,1)S(1)}, u32[]{:S(2)}, u32[]{:S(2)}) %collective-permute-start.13) | collective-permute-done | bytes 819232 | tf_op jit(solution)/shard_map/ppermute | solution.py:393
  105.1 0.9 copy-done.2
  106.6 1.3 collective-permute-start.6
  107.9 1.6 collective-permute-start.8
  109.5 9.3 %collective-permute-done.5.r2_ref = bf16[144,768]{1,0:T(8,128)(2,1)S(1)} collective-permute-done((bf16[144,768]{1,0:T(8,128)(2,1)}, bf16[144,768]{1,0:T(8,128)(2,1)S(1)}, u32[]{:S(2)}, u32[]{:S(2)}) %collective-permute-start.5) | collective-permute-done | bytes 221216 | tf_op jit(solution)/shard_map/ppermute | solution.py:393
  118.9 7.3 %collective-permute-done.6.r3_ref = bf16[144,768]{1,0:T(8,128)(2,1)S(1)} collective-permute-done((bf16[144,768]{1,0:T(8,128)(2,1)}, bf16[144,768]{1,0:T(8,128)(2,1)S(1)}, u32[]{:S(2)}, u32[]{:S(2)}) %collective-permute-start.6) | collective-permute-done | bytes 221216 | tf_op jit(solution)/shard_map/ppermute | solution.py:393
  126.2 0.7 copy-done.10
  126.9 27.3 %outputs.3 = (bf16[512,768]{1,0:T(8,128)(2,1)}, bf16[512,768]{1,0:T(8,128)(2,1)}, bf16[512,768]{1,0:T(8,128)(2,1)}, bf16[512,768]{1,0:T(8,128)(2,1)}) custom-call(s32[2]{0:T(128)} %pad_add_fusion.who_ref, bf16[2048,768]{1,0:T(8,128)(2,1)} %get-tuple-element.52.after_ref.u_ref, bf16[2048,2560]{1,0:T(8,128)(2,1)} %refs_0_.9, ...), custom_call_target="tpu_custom_call" | custom-call | flops 9663676416 | bytes 12582912 | tf_op jit(solution)/shard_map/outputs/pallas_call | solution.py:373
  154.2 3.5 %collective-permute-start.10 = (bf16[512,768]{1,0:T(8,128)(2,1)}, bf16[512,768]{1,0:T(8,128)(2,1)S(1)}, u32[]{:S(2)}, u32[]{:S(2)}) collective-permute-start(bf16[512,768]{1,0:T(8,128)(2,1)} %get-tuple-element.65), channel_id=1, source_target_pairs={{0,4},{4,0},{8,12},{12,8},{1,5},{5,1},{9,13},{13,9},{2,6},{6,2},{1... | collective-permute-start | bytes 2359304 | tf_op jit(solution)/shard_map/ppermute | solution.py:393
  157.7 2.9 %collective-permute-start.11 = (bf16[512,768]{1,0:T(8,128)(2,1)}, bf16[512,768]{1,0:T(8,128)(2,1)S(1)}, u32[]{:S(2)}, u32[]{:S(2)}) collective-permute-start(bf16[512,768]{1,0:T(8,128)(2,1)} %get-tuple-element.66), channel_id=1, source_target_pairs={{0,8},{4,12},{8,0},{12,4},{1,9},{5,13},{9,1},{13,5},{2,10},{6,14},... | collective-permute-start | bytes 2359304 | tf_op jit(solution)/shard_map/ppermute | solution.py:393
  160.6 2.0 collective-permute-start.14
  162.7 12.5 %add_products.4.refs_0_ = f32[512,2560]{1,0:T(8,128)} custom-call(s32[2]{0:T(128)} %pad_add_fusion.who_ref, bf16[2048,2560]{1,0:T(8,128)(2,1)} %refs_0_.9, bf16[512,512]{1,0:T(8,128)(2,1)} %get-tuple-element.53.refs_1_, bf16[1280,2560]{1,0:T(8,128)(2,1)} %refs_7_.1, bf16[1280,2560]{1,0:T(8,128)(2,1)} %refs_7_.1, bf16[512,768]{1,0:T(8,128)(2,1)} %get-tuple-element.62.refs_4_, ...), custom_call_target="tpu_custom_call" | custom-call | flops 4697620480 | bytes 2621440 | tf_op jit(solution)/shard_map/add_products/pallas_call | solution.py:354
  175.1 8.5 %collective-permute-done.9.refs_1_ = bf16[512,512]{1,0:T(8,128)(2,1)} collective-permute-done((bf16[512,512]{1,0:T(8,128)(2,1)}, bf16[512,512]{1,0:T(8,128)(2,1)}, u32[]{:S(2)}, u32[]{:S(2)}) %collective-permute-start.9) | collective-permute-done | bytes 524320 | tf_op jit(solution)/shard_map/ppermute | solution.py:393
  183.7 4.4 %collective-permute-done.10.refs_4_ = bf16[512,768]{1,0:T(8,128)(2,1)S(1)} collective-permute-done((bf16[512,768]{1,0:T(8,128)(2,1)}, bf16[512,768]{1,0:T(8,128)(2,1)S(1)}, u32[]{:S(2)}, u32[]{:S(2)}) %collective-permute-start.10) | collective-permute-done | bytes 786464 | tf_op jit(solution)/shard_map/ppermute | solution.py:393
  188.1 0.9 copy-done.5
  189.0 11.1 %add_products.5.refs_0_ = f32[512,2560]{1,0:T(8,128)} custom-call(s32[2]{0:T(128)} %pad_add_fusion.who_ref, f32[512,2560]{1,0:T(8,128)} %add_products.4.refs_0_, bf16[512,512]{1,0:T(8,128)(2,1)} %collective-permute-done.9.refs_1_, bf16[1280,2560]{1,0:T(8,128)(2,1)} %all-gather.6.cloned.1.call-done.refs_2_.refs_3_.refs_4_, ...), custom_call_target="tpu_custom_call" | custom-call | flops 3355443200 | bytes 2621440 | tf_op jit(solution)/shard_map/add_products/pallas_call | solution.py:354
  200.1 43.3 %collective-permute-done.11.refs_1_ = bf16[512,768]{1,0:T(8,128)(2,1)S(1)} collective-permute-done((bf16[512,768]{1,0:T(8,128)(2,1)}, bf16[512,768]{1,0:T(8,128)(2,1)S(1)}, u32[]{:S(2)}, u32[]{:S(2)}) %collective-permute-start.11) | collective-permute-done | bytes 786464 | tf_op jit(solution)/shard_map/ppermute | solution.py:393
  243.4 0.9 copy-done.4
  244.3 10.0 %add_products.6.refs_0_ = f32[512,2560]{1,0:T(8,128)} custom-call(s32[2]{0:T(128)} %pad_add_fusion.who_ref, f32[512,2560]{1,0:T(8,128)} %add_products.5.refs_0_, bf16[512,768]{1,0:T(8,128)(2,1)} %copy-done.4, bf16[1280,2560]{1,0:T(8,128)(2,1)} %all-gather.6.cloned.1.call-done.refs_2_.refs_3_.refs_4_, ...), custom_call_target="tpu_custom_call" | custom-call | flops 2013265920 | bytes 2621440 | tf_op jit(solution)/shard_map/add_products/pallas_call | solution.py:354
  254.3 2.3 collective-permute-done.12.refs_1_
  256.5 16.6 %collective-permute-done.14.refs_4_ = bf16[512,768]{1,0:T(8,128)(2,1)S(1)} collective-permute-done((bf16[512,768]{1,0:T(8,128)(2,1)}, bf16[512,768]{1,0:T(8,128)(2,1)S(1)}, u32[]{:S(2)}, u32[]{:S(2)}) %collective-permute-start.14) | collective-permute-done | bytes 786464 | tf_op jit(solution)/shard_map/ppermute | solution.py:393
  273.1 0.9 copy-done.3
  274.0 9.9 %add_products.7 = bf16[512,2560]{1,0:T(8,128)(2,1)} custom-call(s32[2]{0:T(128)} %pad_add_fusion.who_ref, f32[512,2560]{1,0:T(8,128)} %add_products.6.refs_0_, bf16[512,512]{1,0:T(8,128)(2,1)} %copy-done.7, bf16[1280,2560]{1,0:T(8,128)(2,1)} %all-gather.8.cloned.1.call-done.refs_2_.refs_3_.refs_5_.refs_6_.refs_7_, ...), custom_call_target="tpu_custom_call" | custom-call | flops 3355443200 | bytes 2621440 | tf_op jit(solution)/shard_map/add_products/pallas_call | solution.py:354
  (43 shorter events, 3.4 us)
Async XLA Ops:
  6.5 156.1 %all-gather.4.cloned.1.call-start = ((), (), s32[]{:S(2)}) async-start(), calls=%async_computation | async-start | bytes 7372800 | tf_op jit(solution)/shard_map/all_gather | solution.py:409
  7.7 25.7 %collective-permute-start.3 = (bf16[160,2560]{1,0:T(8,128)(2,1)S(1)}, bf16[160,2560]{1,0:T(8,128)(2,1)S(1)}, u32[]{:S(2)}, u32[]{:S(2)}) collective-permute-start(bf16[160,2560]{1,0:T(8,128)(2,1)S(1)} %constant_dynamic-slice_fusion), channel_id=1, source_target_pairs={{0,4},{4,0},{8,12},{12,8},{1,5},{5,1},{9,13},{13,9},{2,6},{6,2},{1... | collective-permute-start | bytes 2457608 | tf_op jit(solution)/shard_map/ppermute | solution.py:393
  33.4 0.9 copy-start.1
  34.4 153.7 %all-gather.6.cloned.1.call-start = ((), (), s32[]{:S(2)}) async-start(), calls=%async_computation.1 | async-start | bytes 7372800 | tf_op jit(solution)/shard_map/all_gather | solution.py:409
  34.4 48.6 %collective-permute-start.7 = (bf16[160,2560]{1,0:T(8,128)(2,1)S(1)}, bf16[160,2560]{1,0:T(8,128)(2,1)S(1)}, u32[]{:S(2)}, u32[]{:S(2)}) collective-permute-start(bf16[160,2560]{1,0:T(8,128)(2,1)S(1)} %constant_dynamic-slice_fusion), channel_id=1, source_target_pairs={{0,8},{4,12},{8,0},{12,4},{1,9},{5,13},{9,1},{13,5},{2,10},{6,14},... | collective-permute-start | bytes 2457608 | tf_op jit(solution)/shard_map/ppermute | solution.py:393
  37.1 24.9 %collective-permute-start = (bf16[144,512]{1,0:T(8,128)(2,1)}, bf16[144,512]{1,0:T(8,128)(2,1)S(1)}, u32[]{:S(2)}, u32[]{:S(2)}) collective-permute-start(bf16[144,512]{1,0:T(8,128)(2,1)} %get-tuple-element.47), channel_id=1, source_target_pairs={{0,1},{1,0},{2,3},{3,2},{4,5},{5,4},{6,7},{7,6},{8,9},{9,8},{10,11... | collective-permute-start | bytes 442376 | tf_op jit(solution)/shard_map/ppermute | solution.py:393
  37.1 24.9 %collective-permute-start.1 = (bf16[144,512]{1,0:T(8,128)(2,1)}, bf16[144,512]{1,0:T(8,128)(2,1)S(1)}, u32[]{:S(2)}, u32[]{:S(2)}) collective-permute-start(bf16[144,512]{1,0:T(8,128)(2,1)} %get-tuple-element.48), channel_id=1, source_target_pairs={{0,2},{1,3},{2,0},{3,1},{4,6},{5,7},{6,4},{7,5},{8,10},{9,11},{10,... | collective-permute-start | bytes 442376 | tf_op jit(solution)/shard_map/ppermute | solution.py:393
  37.6 24.4 %collective-permute-start.2 = (bf16[144,512]{1,0:T(8,128)(2,1)}, bf16[144,512]{1,0:T(8,128)(2,1)}, u32[]{:S(2)}, u32[]{:S(2)}) collective-permute-start(bf16[144,512]{1,0:T(8,128)(2,1)} %get-tuple-element.49), channel_id=1, source_target_pairs={{0,3},{1,2},{2,1},{3,0},{4,7},{5,6},{6,5},{7,4},{8,11},{9,10},{10,... | collective-permute-start | bytes 442376 | tf_op jit(solution)/shard_map/ppermute | solution.py:393
  62.0 0.7 copy-start.11
  62.0 0.7 copy-start.12
  83.1 0.9 copy-start
  84.0 189.1 %all-gather.8.cloned.1.call-start = ((), (), s32[]{:S(2)}) async-start(), calls=%async_computation.2 | async-start | bytes 7372800 | tf_op jit(solution)/shard_map/all_gather | solution.py:409
  84.2 20.8 %collective-permute-start.13 = (bf16[160,2560]{1,0:T(8,128)(2,1)}, bf16[160,2560]{1,0:T(8,128)(2,1)S(1)}, u32[]{:S(2)}, u32[]{:S(2)}) collective-permute-start(bf16[160,2560]{1,0:T(8,128)(2,1)} %copy-done), channel_id=1, source_target_pairs={{0,4},{4,0},{8,12},{12,8},{1,5},{5,1},{9,13},{13,9},{2,6},{6,2},{1... | collective-permute-start | bytes 2457608 | tf_op jit(solution)/shard_map/ppermute | solution.py:393
  105.1 0.9 copy-start.2
  106.0 3.6 %collective-permute-start.4 = (bf16[144,768]{1,0:T(8,128)(2,1)}, bf16[144,768]{1,0:T(8,128)(2,1)S(1)}, u32[]{:S(2)}, u32[]{:S(2)}) collective-permute-start(bf16[144,768]{1,0:T(8,128)(2,1)} %get-tuple-element.58), channel_id=1, source_target_pairs={{0,1},{1,0},{2,3},{3,2},{4,5},{5,4},{6,7},{7,6},{8,9},{9,8},{10,11... | collective-permute-start | bytes 663560 | tf_op jit(solution)/shard_map/ppermute | solution.py:393
  106.0 12.8 %collective-permute-start.5 = (bf16[144,768]{1,0:T(8,128)(2,1)}, bf16[144,768]{1,0:T(8,128)(2,1)S(1)}, u32[]{:S(2)}, u32[]{:S(2)}) collective-permute-start(bf16[144,768]{1,0:T(8,128)(2,1)} %get-tuple-element.59), channel_id=1, source_target_pairs={{0,2},{1,3},{2,0},{3,1},{4,6},{5,7},{6,4},{7,5},{8,10},{9,11},{10,... | collective-permute-start | bytes 663560 | tf_op jit(solution)/shard_map/ppermute | solution.py:393
  106.6 19.5 %collective-permute-start.6 = (bf16[144,768]{1,0:T(8,128)(2,1)}, bf16[144,768]{1,0:T(8,128)(2,1)S(1)}, u32[]{:S(2)}, u32[]{:S(2)}) collective-permute-start(bf16[144,768]{1,0:T(8,128)(2,1)} %get-tuple-element.60), channel_id=1, source_target_pairs={{0,3},{1,2},{2,1},{3,0},{4,7},{5,6},{6,5},{7,4},{8,11},{9,10},{10,... | collective-permute-start | bytes 663560 | tf_op jit(solution)/shard_map/ppermute | solution.py:393
  107.9 52.7 %collective-permute-start.8 = (bf16[512,512]{1,0:T(8,128)(2,1)}, bf16[512,512]{1,0:T(8,128)(2,1)S(1)}, u32[]{:S(2)}, u32[]{:S(2)}) collective-permute-start(bf16[512,512]{1,0:T(8,128)(2,1)} %get-tuple-element.63), channel_id=1, source_target_pairs={{0,4},{4,0},{8,12},{12,8},{1,5},{5,1},{9,13},{13,9},{2,6},{6,2},{1... | collective-permute-start | bytes 1572872 | tf_op jit(solution)/shard_map/ppermute | solution.py:393
  109.5 16.7 %copy-start.8 = (bf16[144,768]{1,0:T(8,128)(2,1)}, bf16[144,768]{1,0:T(8,128)(2,1)S(1)}, u32[]{:S(2)}) copy-start(bf16[144,768]{1,0:T(8,128)(2,1)S(1)} %collective-permute-done.4.r1_ref) | copy-start | bytes 663556
  118.9 7.3 %copy-start.9 = (bf16[144,768]{1,0:T(8,128)(2,1)}, bf16[144,768]{1,0:T(8,128)(2,1)S(1)}, u32[]{:S(2)}) copy-start(bf16[144,768]{1,0:T(8,128)(2,1)S(1)} %collective-permute-done.5.r2_ref) | copy-start | bytes 663556
  126.2 0.7 copy-start.10
  154.2 33.9 %collective-permute-start.10 = (bf16[512,768]{1,0:T(8,128)(2,1)}, bf16[512,768]{1,0:T(8,128)(2,1)S(1)}, u32[]{:S(2)}, u32[]{:S(2)}) collective-permute-start(bf16[512,768]{1,0:T(8,128)(2,1)} %get-tuple-element.65), channel_id=1, source_target_pairs={{0,4},{4,0},{8,12},{12,8},{1,5},{5,1},{9,13},{13,9},{2,6},{6,2},{1... | collective-permute-start | bytes 2359304 | tf_op jit(solution)/shard_map/ppermute | solution.py:393
  157.7 25.9 %collective-permute-start.9 = (bf16[512,512]{1,0:T(8,128)(2,1)}, bf16[512,512]{1,0:T(8,128)(2,1)}, u32[]{:S(2)}, u32[]{:S(2)}) collective-permute-start(bf16[512,512]{1,0:T(8,128)(2,1)} %get-tuple-element.64), channel_id=1, source_target_pairs={{0,8},{4,12},{8,0},{12,4},{1,9},{5,13},{9,1},{13,5},{2,10},{6,14},... | collective-permute-start | bytes 1572872 | tf_op jit(solution)/shard_map/ppermute | solution.py:393
  157.7 85.7 %collective-permute-start.11 = (bf16[512,768]{1,0:T(8,128)(2,1)}, bf16[512,768]{1,0:T(8,128)(2,1)S(1)}, u32[]{:S(2)}, u32[]{:S(2)}) collective-permute-start(bf16[512,768]{1,0:T(8,128)(2,1)} %get-tuple-element.66), channel_id=1, source_target_pairs={{0,8},{4,12},{8,0},{12,4},{1,9},{5,13},{9,1},{13,5},{2,10},{6,14},... | collective-permute-start | bytes 2359304 | tf_op jit(solution)/shard_map/ppermute | solution.py:393
  160.6 95.9 %collective-permute-start.12 = (bf16[512,512]{1,0:T(8,128)(2,1)}, bf16[512,512]{1,0:T(8,128)(2,1)S(1)}, u32[]{:S(2)}, u32[]{:S(2)}) collective-permute-start(bf16[512,512]{1,0:T(8,128)(2,1)} %get-tuple-element.67), channel_id=1, source_target_pairs={{0,12},{4,8},{8,4},{12,0},{1,13},{5,9},{9,5},{13,1},{2,14},{6,10},... | collective-permute-start | bytes 1572872 | tf_op jit(solution)/shard_map/ppermute | solution.py:393
  160.6 2.0 copy-start.6
  160.6 112.5 %collective-permute-start.14 = (bf16[512,768]{1,0:T(8,128)(2,1)}, bf16[512,768]{1,0:T(8,128)(2,1)S(1)}, u32[]{:S(2)}, u32[]{:S(2)}) collective-permute-start(bf16[512,768]{1,0:T(8,128)(2,1)} %get-tuple-element.68), channel_id=1, source_target_pairs={{0,12},{4,8},{8,4},{12,0},{1,13},{5,9},{9,5},{13,1},{2,14},{6,10},... | collective-permute-start | bytes 2359304 | tf_op jit(solution)/shard_map/ppermute | solution.py:393
  188.1 0.9 copy-start.5
  243.4 0.9 copy-start.4
  256.5 16.6 %copy-start.7 = (bf16[512,512]{1,0:T(8,128)(2,1)}, bf16[512,512]{1,0:T(8,128)(2,1)S(1)}, u32[]{:S(2)}) copy-start(bf16[512,512]{1,0:T(8,128)(2,1)S(1)} %collective-permute-done.12.refs_1_) | copy-start | bytes 1572868
  273.1 0.9 copy-start.3
Sparse Core Ops, SparseCore 0:
  34.5 47.4 all-gather.3
  84.1 54.0 all-gather.5
  140.1 45.4 all-gather.7

commit v7 on v6

--- a/solution.py
+++ b/solution.py
@@ -410,8 +410,9 @@
 
         n_tiles = w_x.shape[1] // 256
         first = n_tiles * 2 // 5
-        (t_a, n_a), (t_b, n_b) = (0, first), (first, n_tiles - first)
-        head_b = first * 256 // head_dim
+        t_a, t_b, t_c = 0, first, first + 1
+        n_a, n_b, n_c = first, 1, n_tiles - first - 1
+        heads_tile = 256 // head_dim
         who = jnp.stack([tp_index, sp_index])
         skip = d_skip[None, :]
 
@@ -420,28 +421,41 @@
 
         def send(pieces):
             return [pieces[0]] + [swap(pieces[s], 'tp', s) for s in (1, 2, 3)]
+
+        def outputs(u, tile0, tiles, local, got, after):
+            return chunk_outputs(who, u, x_blk, w_z, tile0, bc, (cum3, nexc3), (tail1, tail2), local, got, skip, after, tile0 * heads_tile, 2 * tiles)
 
         bc, cum3, nexc3, dt3, tail1, tail2, u_a, gloc, suf, *states, ut, vf = first_group(who, x_blk, w_bc, w_dt.T, dt_bias[None, :], a_neg[None, :], w_x, n_a)
         local_a = (gloc, suf, ut, vf)
         got_a = exchange(states)
         one, = later((one,), bc)
         w_one = plane(one)
-        u_b, gloc, suf, *states, ut, vf = next_group(who, x_blk, w_x, t_b, n_b, bc, (cum3, nexc3, dt3), one, head_b)
+        u_b, gloc, suf, *states, ut, vf = next_group(who, x_blk, w_x, t_b, n_b, bc, (cum3, nexc3, dt3), one, t_b * heads_tile)
         local_b = (gloc, suf, ut, vf)
         got_b = exchange(states)
-        g_a = chunk_outputs(who, u_a, x_blk, w_z, t_a, bc, (cum3, nexc3), (tail1, tail2), local_a, got_a, skip, u_b, 0, 2 * n_a)
+        g_a = outputs(u_a, t_a, n_a, local_a, got_a, u_b)
         got_g_a = send(g_a)
-        two, = later((two,), g_a[0])
+        u_c, gloc, suf, *states, ut, vf = next_group(who, x_blk, w_x, t_c, n_c, bc, (cum3, nexc3, dt3), g_a[0], t_c * heads_tile)
+        local_c = (gloc, suf, ut, vf)
+        got_c = exchange(states)
+        two, = later((two,), u_c)
         three = swap(two, 'tp', 1)
         w_two = plane(two)
-        g_b = chunk_outputs(who, u_b, x_blk, w_z, t_b, bc, (cum3, nexc3), (tail1, tail2), local_b, got_b, skip, two, head_b, 2 * n_b)
+        g_b = outputs(u_b, t_b, n_b, local_b, got_b, two)
         got_g_b = send(g_b)
+        g_c = outputs(u_c, t_c, n_c, local_c, got_c, g_b[0])
+        got_g_c = send(g_c)
+        three, = later((three,), g_c[0])
         w_three = plane(three)
 
-        total = add_products(who, x_blk, [(got_g_a[0], w_out, t_a), (got_g_b[0], w_out, t_b), (got_g_a[1], w_one, t_a)], F32)
-        total = add_products(who, total, [(got_g_a[2], w_two, t_a), (got_g_b[1], w_one, t_b)], F32)
-        total = add_products(who, total, [(got_g_b[2], w_two, t_b)], F32)
-        return add_products(who, total, [(got_g_a[3], w_three, t_a), (got_g_b[3], w_three, t_b)], BF16)
+        def pieces(slot, w, which):
+            groups = {"a": (got_g_a, t_a), "b": (got_g_b, t_b), "c": (got_g_c, t_c)}
+            return [(groups[k][0][slot], w, groups[k][1]) for k in which]
+
+        total = add_products(who, x_blk, pieces(0, w_out, "abc") + pieces(1, w_one, "a"), F32)
+        total = add_products(who, total, pieces(2, w_two, "ab") + pieces(1, w_one, "b"), F32)
+        total = add_products(who, total, pieces(1, w_one, "c") + pieces(2, w_two, "c"), F32)
+        return add_products(who, total, pieces(3, w_three, "abc"), BF16)
 
     in_specs = (P(('dp', 'sp'), None), P(None, 'tp'), P(None, 'tp'), P(None, None), P(None, 'tp'), P('tp'), P('tp'), P('tp'), P('tp', None))
     out_specs = P(('dp', 'sp', 'tp'), None)

time: 291 us -> 270 us (0.928)
  the two profiles are of different devices: /device:TPU:12 before, /device:TPU:0 now
where the time goes in v7:
time: 270 us; the launch traced here: 266 us
  Pallas kernels  152 us (56%)
  waiting for transfers between devices  66.8 us (25%)
  starting transfers between devices  25 us (9%)
  between operations  13.4 us (5%)
  local copies, waits for them, and re-layouts  8.42 us (3%)
    ppermute x21, waiting for transfers between devices, swap(): return lax.ppermute(val, axis, [(i, i ^ slot) for i in range(4)])  66.7 us
    pallas_call x3, Pallas kernels, chunk_outputs(): pl.pallas_call(functools.partial(out_kernel, first_head, n_pairs), grid_s...  57.2 us
    pallas_call x4, Pallas kernels, add_products(): pl.pallas_call(body, grid_spec=pltpu.PrefetchScalarGridSpec(num_scalar_pr...  42.5 us
    pallas_call x2, Pallas kernels, next_group(): pl.pallas_call(functools.partial(next_kernel, first_head, n_tiles), grid=...  27.6 us
    ppermute x21, starting transfers between devices, swap(): return lax.ppermute(val, axis, [(i, i ^ slot) for i in range(4)])  24.8 us
    pallas_call x1, Pallas kernels, first_group(): pl.pallas_call(functools.partial(first_kernel, n_tiles), grid=(tokens //...  24.5 us
    unnamed x50, local copies, waits for them, and re-layouts  7.22 us
  transfers between devices with their start and end apart: 24, of which 6 were waited for; matrix products, arithmetic and copies ran while one was open for 0% of the time, Pallas kernels for 53%

profile of v7, /device:TPU:0, one launch (start us, length us, event | category | flops | bytes accessed | tf_op | source)
XLA Modules:
  0.0 266.1 jit_solution(5132703080192986833)
XLA Ops:
  6.5 1.2 constant_dynamic-slice_fusion
  7.7 3.1 %collective-permute-start.3 = (bf16[160,2560]{1,0:T(8,128)(2,1)S(1)}, bf16[160,2560]{1,0:T(8,128)(2,1)S(1)}, u32[]{:S(2)}, u32[]{:S(2)}) collective-permute-start(bf16[160,2560]{1,0:T(8,128)(2,1)S(1)} %constant_dynamic-slice_fusion), channel_id=1, source_target_pairs={{0,4},{4,0},{8,12},{12,8},{1,5},{5,1},{9,13},{13,9},{2,6},{6,2},{1... | collective-permute-start | bytes 2457608 | tf_op jit(solution)/shard_map/ppermute | solution.py:393
  10.9 0.7 pad_add_fusion.who_ref
  11.5 24.5 %first_group.1 = (bf16[2048,256]{1,0:T(8,128)(2,1)}, bf16[2048,128]{1,0:T(8,128)(2,1)}, bf16[2048,128]{1,0:T(8,128)(2,1)}, bf16[2048,128]{1,0:T(8,128)(2,1)}, bf...) custom-call(s32[2]{0:T(128)} %pad_add_fusion.who_ref, ...), custom_call_target="tpu_custom_call" | custom-call | flops 16106127360 | bytes 10485760 | tf_op jit(solution)/shard_map/first_group/pallas_call | solution.py:308
  36.1 0.9 copy-done.1
  37.0 2.7 collective-permute-start.7
  39.7 1.5 collective-permute-start.1
  41.5 12.0 %next_group.2 = (bf16[2048,256]{1,0:T(8,128)(2,1)}, f32[16,128,256]{2,1,0:T(8,128)}, f32[16,8,256]{2,1,0:T(8,128)}, bf16[144,256]{1,0:T(8,128)(2,1)}, bf16[144,2...) custom-call(s32[2]{0:T(128)} %pad_add_fusion.who_ref, ...), custom_call_target="tpu_custom_call" | custom-call | flops 8053063680 | bytes 10485760 | tf_op jit(solution)/shard_map/next_group/pallas_call | solution.py:327
  54.2 20.7 %outputs.3 = (bf16[512,512]{1,0:T(8,128)(2,1)}, bf16[512,512]{1,0:T(8,128)(2,1)}, bf16[512,512]{1,0:T(8,128)(2,1)}, bf16[512,512]{1,0:T(8,128)(2,1)}) custom-call(s32[2]{0:T(128)} %pad_add_fusion.who_ref, bf16[2048,512]{1,0:T(8,128)(2,1)} %get-tuple-element.50.u_ref, bf16[2048,2560]{1,0:T(8,128)(2,1)} %refs_0_.13, ...), custom_call_target="tpu_custom_call" | custom-call | flops 6442450944 | bytes 8388608 | tf_op jit(solution)/shard_map/outputs/pallas_call | solution.py:373
  75.0 15.6 %next_group.3 = (bf16[2048,512]{1,0:T(8,128)(2,1)}, f32[16,128,512]{2,1,0:T(8,128)}, f32[16,8,512]{2,1,0:T(8,128)}, bf16[144,512]{1,0:T(8,128)(2,1)}, bf16[144,5...) custom-call(s32[2]{0:T(128)} %pad_add_fusion.who_ref, ...), custom_call_target="tpu_custom_call" | custom-call | flops 10737418240 | bytes 10485760 | tf_op jit(solution)/shard_map/next_group/pallas_call | solution.py:327
  90.6 0.9 copy-done
  92.2 1.7 collective-permute-start.5
  94.6 1.6 collective-permute-start.9
  96.6 0.8 collective-permute-start.10
  97.5 0.7 collective-permute-done.6.r3_ref
  98.8 14.9 %outputs.4 = (bf16[512,256]{1,0:T(8,128)(2,1)}, bf16[512,256]{1,0:T(8,128)(2,1)}, bf16[512,256]{1,0:T(8,128)(2,1)}, bf16[512,256]{1,0:T(8,128)(2,1)}) custom-call(s32[2]{0:T(128)} %pad_add_fusion.who_ref, bf16[2048,256]{1,0:T(8,128)(2,1)} %get-tuple-element.65.after_ref.u_ref, bf16[2048,2560]{1,0:T(8,128)(2,1)} %refs_0_.13, ...), custom_call_target="tpu_custom_call" | custom-call | flops 3221225472 | bytes 4194304 | tf_op jit(solution)/shard_map/outputs/pallas_call | solution.py:373
  114.5 21.5 %outputs.5 = (bf16[512,512]{1,0:T(8,128)(2,1)}, bf16[512,512]{1,0:T(8,128)(2,1)}, bf16[512,512]{1,0:T(8,128)(2,1)}, bf16[512,512]{1,0:T(8,128)(2,1)}) custom-call(s32[2]{0:T(128)} %pad_add_fusion.who_ref, bf16[2048,512]{1,0:T(8,128)(2,1)} %get-tuple-element.74.u_ref, bf16[2048,2560]{1,0:T(8,128)(2,1)} %refs_0_.13, ...), custom_call_target="tpu_custom_call" | custom-call | flops 6442450944 | bytes 8388608 | tf_op jit(solution)/shard_map/outputs/pallas_call | solution.py:373
  136.1 0.9 copy-done.2
  137.7 1.4 collective-permute-start.14
  139.2 2.8 %collective-permute-start.12 = (bf16[512,512]{1,0:T(8,128)(2,1)}, bf16[512,512]{1,0:T(8,128)(2,1)S(1)}, u32[]{:S(2)}, u32[]{:S(2)}) collective-permute-start(bf16[512,512]{1,0:T(8,128)(2,1)} %get-tuple-element.86), channel_id=1, source_target_pairs={{0,8},{4,12},{8,0},{12,4},{1,9},{5,13},{9,1},{13,5},{2,10},{6,14},... | collective-permute-start | bytes 1572872 | tf_op jit(solution)/shard_map/ppermute | solution.py:393
  142.1 12.8 %collective-permute-done.13.refs_4_ = bf16[512,256]{1,0:T(8,128)(2,1)S(1)} collective-permute-done((bf16[512,256]{1,0:T(8,128)(2,1)S(1)}, bf16[512,256]{1,0:T(8,128)(2,1)S(1)}, u32[]{:S(2)}, u32[]{:S(2)}) %collective-permute-start.13) | collective-permute-done | bytes 262176 | tf_op jit(solution)/shard_map/ppermute | solution.py:393
  154.9 2.9 %collective-permute-start.15 = (bf16[512,512]{1,0:T(8,128)(2,1)}, bf16[512,512]{1,0:T(8,128)(2,1)S(1)}, u32[]{:S(2)}, u32[]{:S(2)}) collective-permute-start(bf16[512,512]{1,0:T(8,128)(2,1)} %get-tuple-element.89), channel_id=1, source_target_pairs={{0,4},{4,0},{8,12},{12,8},{1,5},{5,1},{9,13},{13,9},{2,6},{6,2},{1... | collective-permute-start | bytes 1572872 | tf_op jit(solution)/shard_map/ppermute | solution.py:393
  157.8 15.1 %collective-permute-done.14.refs_6_ = bf16[512,256]{1,0:T(8,128)(2,1)S(1)} collective-permute-done((bf16[512,256]{1,0:T(8,128)(2,1)S(1)}, bf16[512,256]{1,0:T(8,128)(2,1)S(1)}, u32[]{:S(2)}, u32[]{:S(2)}) %collective-permute-start.14) | collective-permute-done | bytes 262176 | tf_op jit(solution)/shard_map/ppermute | solution.py:393
  173.0 0.7 copy-done.10
  173.7 1.3 collective-permute-start.20
  175.0 11.5 %add_products.4.refs_0_ = f32[512,2560]{1,0:T(8,128)} custom-call(s32[2]{0:T(128)} %pad_add_fusion.who_ref, bf16[2048,2560]{1,0:T(8,128)(2,1)} %refs_0_.13, bf16[512,512]{1,0:T(8,128)(2,1)} %get-tuple-element.66.refs_2_.refs_1_, bf16[1280,2560]{1,0:T(8,128)(2,1)} %refs_8_.1, bf16[1280,2560]{1,0:T(8,128)(2,1)} %refs_8_.1, ...), custom_call_target="tpu_custom_call" | custom-call | flops 4697620480 | bytes 2621440 | tf_op jit(solution)/shard_map/add_products/pallas_call | solution.py:354
  186.6 2.6 collective-permute-start.19
  189.2 10.4 %add_products.5.refs_0_ = f32[512,2560]{1,0:T(8,128)} custom-call(s32[2]{0:T(128)} %pad_add_fusion.who_ref, f32[512,2560]{1,0:T(8,128)} %add_products.4.refs_0_, bf16[512,512]{1,0:T(8,128)(2,1)} %copy-done.5, bf16[1280,2560]{1,0:T(8,128)(2,1)} %all-gather.6.cloned.1.call-done.refs_2_.refs_3_.refs_5_.refs_6_, ...), custom_call_target="tpu_custom_call" | custom-call | flops 2684354560 | bytes 2621440 | tf_op jit(solution)/shard_map/add_products/pallas_call | solution.py:354
  199.6 37.5 %collective-permute-done.16.refs_4_ = bf16[512,512]{1,0:T(8,128)(2,1)S(1)} collective-permute-done((bf16[512,512]{1,0:T(8,128)(2,1)}, bf16[512,512]{1,0:T(8,128)(2,1)S(1)}, u32[]{:S(2)}, u32[]{:S(2)}) %collective-permute-start.16) | collective-permute-done | bytes 524320 | tf_op jit(solution)/shard_map/ppermute | solution.py:393
  237.2 0.8 copy-done.8
  237.9 10.7 %add_products.6.refs_0_ = f32[512,2560]{1,0:T(8,128)} custom-call(s32[2]{0:T(128)} %pad_add_fusion.who_ref, f32[512,2560]{1,0:T(8,128)} %add_products.5.refs_0_, bf16[512,512]{1,0:T(8,128)(2,1)} %copy-done.6, bf16[1280,2560]{1,0:T(8,128)(2,1)} %all-gather.4.cloned.1.call-done.refs_10_.refs_11_.refs_7_.refs_2_.refs_3_, ...), custom_call_target="tpu_custom_call" | custom-call | flops 2684354560 | bytes 2621440 | tf_op jit(solution)/shard_map/add_products/pallas_call | solution.py:354
  249.7 9.9 %add_products.7 = bf16[512,2560]{1,0:T(8,128)(2,1)} custom-call(s32[2]{0:T(128)} %pad_add_fusion.who_ref, f32[512,2560]{1,0:T(8,128)} %add_products.6.refs_0_, bf16[512,512]{1,0:T(8,128)(2,1)} %copy-done.3, bf16[1280,2560]{1,0:T(8,128)(2,1)} %all-gather.8.cloned.1.call-done.refs_2_.refs_3_.refs_5_.refs_7_.refs_8_, ...), custom_call_target="tpu_custom_call" | custom-call | flops 3355443200 | bytes 2621440 | tf_op jit(solution)/shard_map/add_products/pallas_call | solution.py:354
  (81 shorter events, 6.4 us)
Async XLA Ops:
  6.5 168.5 %all-gather.4.cloned.1.call-start = ((), (), s32[]{:S(2)}) async-start(), calls=%async_computation | async-start | bytes 7372800 | tf_op jit(solution)/shard_map/all_gather | solution.py:409
  7.7 28.3 %collective-permute-start.3 = (bf16[160,2560]{1,0:T(8,128)(2,1)S(1)}, bf16[160,2560]{1,0:T(8,128)(2,1)S(1)}, u32[]{:S(2)}, u32[]{:S(2)}) collective-permute-start(bf16[160,2560]{1,0:T(8,128)(2,1)S(1)} %constant_dynamic-slice_fusion), channel_id=1, source_target_pairs={{0,4},{4,0},{8,12},{12,8},{1,5},{5,1},{9,13},{13,9},{2,6},{6,2},{1... | collective-permute-start | bytes 2457608 | tf_op jit(solution)/shard_map/ppermute | solution.py:393
  37.0 152.2 %all-gather.6.cloned.1.call-start = ((), (), s32[]{:S(2)}) async-start(), calls=%async_computation.1 | async-start | bytes 7372800 | tf_op jit(solution)/shard_map/all_gather | solution.py:409
  37.0 53.6 %collective-permute-start.7 = (bf16[160,2560]{1,0:T(8,128)(2,1)S(1)}, bf16[160,2560]{1,0:T(8,128)(2,1)S(1)}, u32[]{:S(2)}, u32[]{:S(2)}) collective-permute-start(bf16[160,2560]{1,0:T(8,128)(2,1)S(1)} %constant_dynamic-slice_fusion), channel_id=1, source_target_pairs={{0,8},{4,12},{8,0},{12,4},{1,9},{5,13},{9,1},{13,5},{2,10},{6,14},... | collective-permute-start | bytes 2457608 | tf_op jit(solution)/shard_map/ppermute | solution.py:393
  39.7 13.8 %collective-permute-start = (bf16[144,512]{1,0:T(8,128)(2,1)}, bf16[144,512]{1,0:T(8,128)(2,1)S(1)}, u32[]{:S(2)}, u32[]{:S(2)}) collective-permute-start(bf16[144,512]{1,0:T(8,128)(2,1)} %get-tuple-element.60), channel_id=1, source_target_pairs={{0,1},{1,0},{2,3},{3,2},{4,5},{5,4},{6,7},{7,6},{8,9},{9,8},{10,11... | collective-permute-start | bytes 442376 | tf_op jit(solution)/shard_map/ppermute | solution.py:393
  39.7 13.8 %collective-permute-start.1 = (bf16[144,512]{1,0:T(8,128)(2,1)}, bf16[144,512]{1,0:T(8,128)(2,1)S(1)}, u32[]{:S(2)}, u32[]{:S(2)}) collective-permute-start(bf16[144,512]{1,0:T(8,128)(2,1)} %get-tuple-element.61), channel_id=1, source_target_pairs={{0,2},{1,3},{2,0},{3,1},{4,6},{5,7},{6,4},{7,5},{8,10},{9,11},{10,... | collective-permute-start | bytes 442376 | tf_op jit(solution)/shard_map/ppermute | solution.py:393
  41.2 12.3 %collective-permute-start.2 = (bf16[144,512]{1,0:T(8,128)(2,1)}, bf16[144,512]{1,0:T(8,128)(2,1)}, u32[]{:S(2)}, u32[]{:S(2)}) collective-permute-start(bf16[144,512]{1,0:T(8,128)(2,1)} %get-tuple-element.62), channel_id=1, source_target_pairs={{0,3},{1,2},{2,1},{3,0},{4,7},{5,6},{6,5},{7,4},{8,11},{9,10},{10,... | collective-permute-start | bytes 442376 | tf_op jit(solution)/shard_map/ppermute | solution.py:393
  75.0 16.8 %copy-start.24 = (bf16[144,256]{1,0:T(8,128)(2,1)S(1)}, bf16[144,256]{1,0:T(8,128)(2,1)}, u32[]{:S(2)}) copy-start(bf16[144,256]{1,0:T(8,128)(2,1)} %get-tuple-element.71) | copy-start | bytes 221188
  75.0 17.2 %copy-start.23 = (bf16[144,256]{1,0:T(8,128)(2,1)S(1)}, bf16[144,256]{1,0:T(8,128)(2,1)}, u32[]{:S(2)}) copy-start(bf16[144,256]{1,0:T(8,128)(2,1)} %get-tuple-element.72) | copy-start | bytes 221188
  75.0 18.9 %copy-start.22 = (bf16[144,256]{1,0:T(8,128)(2,1)S(1)}, bf16[144,256]{1,0:T(8,128)(2,1)}, u32[]{:S(2)}) copy-start(bf16[144,256]{1,0:T(8,128)(2,1)} %get-tuple-element.73) | copy-start | bytes 221188
  91.6 157.2 %all-gather.8.cloned.1.call-start = ((), (), s32[]{:S(2)}) async-start(), calls=%async_computation.2 | async-start | bytes 7372800 | tf_op jit(solution)/shard_map/all_gather | solution.py:409
  91.8 2.8 %collective-permute-start.4 = (bf16[144,256]{1,0:T(8,128)(2,1)S(1)}, bf16[144,256]{1,0:T(8,128)(2,1)S(1)}, u32[]{:S(2)}, u32[]{:S(2)}) collective-permute-start(bf16[144,256]{1,0:T(8,128)(2,1)S(1)} %copy-done.24), channel_id=1, source_target_pairs={{0,1},{1,0},{2,3},{3,2},{4,5},{5,4},{6,7},{7,6},{8,9},{9,8},{10,11... | collective-permute-start | bytes 221192 | tf_op jit(solution)/shard_map/ppermute | solution.py:393
  92.2 4.4 %collective-permute-start.5 = (bf16[144,256]{1,0:T(8,128)(2,1)S(1)}, bf16[144,256]{1,0:T(8,128)(2,1)S(1)}, u32[]{:S(2)}, u32[]{:S(2)}) collective-permute-start(bf16[144,256]{1,0:T(8,128)(2,1)S(1)} %copy-done.23), channel_id=1, source_target_pairs={{0,2},{1,3},{2,0},{3,1},{4,6},{5,7},{6,4},{7,5},{8,10},{9,11},{10,... | collective-permute-start | bytes 221192 | tf_op jit(solution)/shard_map/ppermute | solution.py:393
  93.9 4.3 %collective-permute-start.6 = (bf16[144,256]{1,0:T(8,128)(2,1)S(1)}, bf16[144,256]{1,0:T(8,128)(2,1)S(1)}, u32[]{:S(2)}, u32[]{:S(2)}) collective-permute-start(bf16[144,256]{1,0:T(8,128)(2,1)S(1)} %copy-done.22), channel_id=1, source_target_pairs={{0,3},{1,2},{2,1},{3,0},{4,7},{5,6},{6,5},{7,4},{8,11},{9,10},{10,... | collective-permute-start | bytes 221192 | tf_op jit(solution)/shard_map/ppermute | solution.py:393
  93.9 42.2 %collective-permute-start.18 = (bf16[160,2560]{1,0:T(8,128)(2,1)}, bf16[160,2560]{1,0:T(8,128)(2,1)S(1)}, u32[]{:S(2)}, u32[]{:S(2)}) collective-permute-start(bf16[160,2560]{1,0:T(8,128)(2,1)} %copy-done), channel_id=1, source_target_pairs={{0,4},{4,0},{8,12},{12,8},{1,5},{5,1},{9,13},{13,9},{2,6},{6,2},{1... | collective-permute-start | bytes 2457608 | tf_op jit(solution)/shard_map/ppermute | solution.py:393
  94.3 19.5 %collective-permute-start.8 = (bf16[144,512]{1,0:T(8,128)(2,1)}, bf16[144,512]{1,0:T(8,128)(2,1)S(1)}, u32[]{:S(2)}, u32[]{:S(2)}) collective-permute-start(bf16[144,512]{1,0:T(8,128)(2,1)} %get-tuple-element.81), channel_id=1, source_target_pairs={{0,1},{1,0},{2,3},{3,2},{4,5},{5,4},{6,7},{7,6},{8,9},{9,8},{10,11... | collective-permute-start | bytes 442376 | tf_op jit(solution)/shard_map/ppermute | solution.py:393
  94.6 3.6 %copy-start.17 = (bf16[144,256]{1,0:T(8,128)(2,1)}, bf16[144,256]{1,0:T(8,128)(2,1)S(1)}, u32[]{:S(2)}) copy-start(bf16[144,256]{1,0:T(8,128)(2,1)S(1)} %collective-permute-done.4.r1_ref) | copy-start | bytes 221188
  94.6 19.2 %collective-permute-start.9 = (bf16[144,512]{1,0:T(8,128)(2,1)}, bf16[144,512]{1,0:T(8,128)(2,1)S(1)}, u32[]{:S(2)}, u32[]{:S(2)}) collective-permute-start(bf16[144,512]{1,0:T(8,128)(2,1)} %get-tuple-element.82), channel_id=1, source_target_pairs={{0,2},{1,3},{2,0},{3,1},{4,6},{5,7},{6,4},{7,5},{8,10},{9,11},{10,... | collective-permute-start | bytes 442376 | tf_op jit(solution)/shard_map/ppermute | solution.py:393
  96.6 17.2 %collective-permute-start.10 = (bf16[144,512]{1,0:T(8,128)(2,1)}, bf16[144,512]{1,0:T(8,128)(2,1)S(1)}, u32[]{:S(2)}, u32[]{:S(2)}) collective-permute-start(bf16[144,512]{1,0:T(8,128)(2,1)} %get-tuple-element.83), channel_id=1, source_target_pairs={{0,3},{1,2},{2,1},{3,0},{4,7},{5,6},{6,5},{7,4},{8,11},{9,10},{10,... | collective-permute-start | bytes 442376 | tf_op jit(solution)/shard_map/ppermute | solution.py:393
  114.5 22.5 %copy-start.21 = (bf16[512,256]{1,0:T(8,128)(2,1)S(1)}, bf16[512,256]{1,0:T(8,128)(2,1)}, u32[]{:S(2)}) copy-start(bf16[512,256]{1,0:T(8,128)(2,1)} %get-tuple-element.87) | copy-start | bytes 786436
  114.5 23.2 %copy-start.20 = (bf16[512,256]{1,0:T(8,128)(2,1)S(1)}, bf16[512,256]{1,0:T(8,128)(2,1)}, u32[]{:S(2)}) copy-start(bf16[512,256]{1,0:T(8,128)(2,1)} %get-tuple-element.88) | copy-start | bytes 786436
  137.0 36.0 %collective-permute-start.11 = (bf16[512,512]{1,0:T(8,128)(2,1)}, bf16[512,512]{1,0:T(8,128)(2,1)S(1)}, u32[]{:S(2)}, u32[]{:S(2)}) collective-permute-start(bf16[512,512]{1,0:T(8,128)(2,1)} %get-tuple-element.85), channel_id=1, source_target_pairs={{0,4},{4,0},{8,12},{12,8},{1,5},{5,1},{9,13},{13,9},{2,6},{6,2},{1... | collective-permute-start | bytes 1572872 | tf_op jit(solution)/shard_map/ppermute | solution.py:393
  137.1 17.8 %collective-permute-start.13 = (bf16[512,256]{1,0:T(8,128)(2,1)S(1)}, bf16[512,256]{1,0:T(8,128)(2,1)S(1)}, u32[]{:S(2)}, u32[]{:S(2)}) collective-permute-start(bf16[512,256]{1,0:T(8,128)(2,1)S(1)} %copy-done.21), channel_id=1, source_target_pairs={{0,8},{4,12},{8,0},{12,4},{1,9},{5,13},{9,1},{13,5},{2,10},{6,14},... | collective-permute-start | bytes 786440 | tf_op jit(solution)/shard_map/ppermute | solution.py:393
  137.7 35.2 %collective-permute-start.14 = (bf16[512,256]{1,0:T(8,128)(2,1)S(1)}, bf16[512,256]{1,0:T(8,128)(2,1)S(1)}, u32[]{:S(2)}, u32[]{:S(2)}) collective-permute-start(bf16[512,256]{1,0:T(8,128)(2,1)S(1)} %copy-done.20), channel_id=1, source_target_pairs={{0,4},{4,0},{8,12},{12,8},{1,5},{5,1},{9,13},{13,9},{2,6},{6,2},{1... | collective-permute-start | bytes 786440 | tf_op jit(solution)/shard_map/ppermute | solution.py:393
  139.2 47.5 %collective-permute-start.12 = (bf16[512,512]{1,0:T(8,128)(2,1)}, bf16[512,512]{1,0:T(8,128)(2,1)S(1)}, u32[]{:S(2)}, u32[]{:S(2)}) collective-permute-start(bf16[512,512]{1,0:T(8,128)(2,1)} %get-tuple-element.86), channel_id=1, source_target_pairs={{0,8},{4,12},{8,0},{12,4},{1,9},{5,13},{9,1},{13,5},{2,10},{6,14},... | collective-permute-start | bytes 1572872 | tf_op jit(solution)/shard_map/ppermute | solution.py:393
  142.0 106.7 %collective-permute-start.17 = (bf16[512,512]{1,0:T(8,128)(2,1)}, bf16[512,512]{1,0:T(8,128)(2,1)S(1)}, u32[]{:S(2)}, u32[]{:S(2)}) collective-permute-start(bf16[512,512]{1,0:T(8,128)(2,1)} %get-tuple-element.91), channel_id=1, source_target_pairs={{0,12},{4,8},{8,4},{12,0},{1,13},{5,9},{9,5},{13,1},{2,14},{6,10},... | collective-permute-start | bytes 1572872 | tf_op jit(solution)/shard_map/ppermute | solution.py:393
  154.9 31.6 %copy-start.9 = (bf16[512,256]{1,0:T(8,128)(2,1)}, bf16[512,256]{1,0:T(8,128)(2,1)S(1)}, u32[]{:S(2)}) copy-start(bf16[512,256]{1,0:T(8,128)(2,1)S(1)} %collective-permute-done.13.refs_4_) | copy-start | bytes 786436
  154.9 44.7 %collective-permute-start.15 = (bf16[512,512]{1,0:T(8,128)(2,1)}, bf16[512,512]{1,0:T(8,128)(2,1)S(1)}, u32[]{:S(2)}, u32[]{:S(2)}) collective-permute-start(bf16[512,512]{1,0:T(8,128)(2,1)} %get-tuple-element.89), channel_id=1, source_target_pairs={{0,4},{4,0},{8,12},{12,8},{1,5},{5,1},{9,13},{13,9},{2,6},{6,2},{1... | collective-permute-start | bytes 1572872 | tf_op jit(solution)/shard_map/ppermute | solution.py:393
  172.9 64.2 %collective-permute-start.16 = (bf16[512,512]{1,0:T(8,128)(2,1)}, bf16[512,512]{1,0:T(8,128)(2,1)S(1)}, u32[]{:S(2)}, u32[]{:S(2)}) collective-permute-start(bf16[512,512]{1,0:T(8,128)(2,1)} %get-tuple-element.90), channel_id=1, source_target_pairs={{0,8},{4,12},{8,0},{12,4},{1,9},{5,13},{9,1},{13,5},{2,10},{6,14},... | collective-permute-start | bytes 1572872 | tf_op jit(solution)/shard_map/ppermute | solution.py:393
  173.7 75.0 %collective-permute-start.20 = (bf16[512,512]{1,0:T(8,128)(2,1)}, bf16[512,512]{1,0:T(8,128)(2,1)S(1)}, u32[]{:S(2)}, u32[]{:S(2)}) collective-permute-start(bf16[512,512]{1,0:T(8,128)(2,1)} %get-tuple-element.94), channel_id=1, source_target_pairs={{0,12},{4,8},{8,4},{12,0},{1,13},{5,9},{9,5},{13,1},{2,14},{6,10},... | collective-permute-start | bytes 1572872 | tf_op jit(solution)/shard_map/ppermute | solution.py:393
  186.6 62.0 %collective-permute-start.19 = (bf16[512,256]{1,0:T(8,128)(2,1)}, bf16[512,256]{1,0:T(8,128)(2,1)S(1)}, u32[]{:S(2)}, u32[]{:S(2)}) collective-permute-start(bf16[512,256]{1,0:T(8,128)(2,1)} %get-tuple-element.93), channel_id=1, source_target_pairs={{0,12},{4,8},{8,4},{12,0},{1,13},{5,9},{9,5},{13,1},{2,14},{6,10},... | collective-permute-start | bytes 786440 | tf_op jit(solution)/shard_map/ppermute | solution.py:393
  199.6 37.5 %copy-start.6 = (bf16[512,512]{1,0:T(8,128)(2,1)}, bf16[512,512]{1,0:T(8,128)(2,1)S(1)}, u32[]{:S(2)}) copy-start(bf16[512,512]{1,0:T(8,128)(2,1)S(1)} %collective-permute-done.15.refs_1_) | copy-start | bytes 1572868
  (17 other events, 16.4 us)
Sparse Core Ops, SparseCore 0:
  37.1 46.7 all-gather.3
  91.7 47.4 all-gather.5
  141.0 46.4 all-gather.7

commit v8 on v7

--- a/solution.py
+++ b/solution.py
@@ -435,18 +435,18 @@
         got_b = exchange(states)
         g_a = outputs(u_a, t_a, n_a, local_a, got_a, u_b)
         got_g_a = send(g_a)
-        u_c, gloc, suf, *states, ut, vf = next_group(who, x_blk, w_x, t_c, n_c, bc, (cum3, nexc3, dt3), g_a[0], t_c * heads_tile)
+        two, = later((two,), g_a[0])
+        three = swap(two, 'tp', 1)
+        w_two = plane(two)
+        u_c, gloc, suf, *states, ut, vf = next_group(who, x_blk, w_x, t_c, n_c, bc, (cum3, nexc3, dt3), two, t_c * heads_tile)
         local_c = (gloc, suf, ut, vf)
         got_c = exchange(states)
-        two, = later((two,), u_c)
-        three = swap(two, 'tp', 1)
-        w_two = plane(two)
-        g_b = outputs(u_b, t_b, n_b, local_b, got_b, two)
+        g_b = outputs(u_b, t_b, n_b, local_b, got_b, u_c)
         got_g_b = send(g_b)
-        g_c = outputs(u_c, t_c, n_c, local_c, got_c, g_b[0])
+        three, = later((three,), g_b[0])
+        w_three = plane(three)
+        g_c = outputs(u_c, t_c, n_c, local_c, got_c, three)
         got_g_c = send(g_c)
-        three, = later((three,), g_c[0])
-        w_three = plane(three)
 
         def pieces(slot, w, which):
             groups = {"a": (got_g_a, t_a), "b": (got_g_b, t_b), "c": (got_g_c, t_c)}
@@ -454,8 +454,8 @@
 
         total = add_products(who, x_blk, pieces(0, w_out, "abc") + pieces(1, w_one, "a"), F32)
         total = add_products(who, total, pieces(2, w_two, "ab") + pieces(1, w_one, "b"), F32)
-        total = add_products(who, total, pieces(1, w_one, "c") + pieces(2, w_two, "c"), F32)
-        return add_products(who, total, pieces(3, w_three, "abc"), BF16)
+        total = add_products(who, total, pieces(1, w_one, "c") + pieces(3, w_three, "ab"), F32)
+        return add_products(who, total, pieces(2, w_two, "c") + pieces(3, w_three, "c"), BF16)
 
     in_specs = (P(('dp', 'sp'), None), P(None, 'tp'), P(None, 'tp'), P(None, None), P(None, 'tp'), P('tp'), P('tp'), P('tp'), P('tp', None))
     out_specs = P(('dp', 'sp', 'tp'), None)

time: 270 us -> 253 us (0.937)
  the two profiles are of different devices: /device:TPU:0 before, /device:TPU:14 now
where the time goes in v8:
time: 253 us; the launch traced here: 252 us
  Pallas kernels  152 us (60%)
  waiting for transfers between devices  54.3 us (21%)
  starting transfers between devices  24 us (9%)
  between operations  13.4 us (5%)
  local copies, waits for them, and re-layouts  7.74 us (3%)
    pallas_call x3, Pallas kernels, chunk_outputs(): pl.pallas_call(functools.partial(out_kernel, first_head, n_pairs), grid_s...  57 us
    ppermute x21, waiting for transfers between devices, swap(): return lax.ppermute(val, axis, [(i, i ^ slot) for i in range(4)])  54.2 us
    pallas_call x4, Pallas kernels, add_products(): pl.pallas_call(body, grid_spec=pltpu.PrefetchScalarGridSpec(num_scalar_pr...  42.9 us
    pallas_call x2, Pallas kernels, next_group(): pl.pallas_call(functools.partial(next_kernel, first_head, n_tiles), grid=...  27.5 us
    pallas_call x1, Pallas kernels, first_group(): pl.pallas_call(functools.partial(first_kernel, n_tiles), grid=(tokens //...  24.5 us
    ppermute x21, starting transfers between devices, swap(): return lax.ppermute(val, axis, [(i, i ^ slot) for i in range(4)])  23.7 us
    unnamed x42, local copies, waits for them, and re-layouts  6.54 us
  transfers between devices with their start and end apart: 24, of which 5 were waited for; matrix products, arithmetic and copies ran while one was open for 0% of the time, Pallas kernels for 56%

profile of v8, /device:TPU:14, one launch (start us, length us, event | category | flops | bytes accessed | tf_op | source)
XLA Modules:
  0.0 251.8 jit_solution(16967428722016927081)
XLA Ops:
  6.5 1.2 constant_dynamic-slice_fusion
  8.3 0.6 pad_add_fusion.who_ref
  8.9 24.5 %first_group.1 = (bf16[2048,256]{1,0:T(8,128)(2,1)}, bf16[2048,128]{1,0:T(8,128)(2,1)}, bf16[2048,128]{1,0:T(8,128)(2,1)}, bf16[2048,128]{1,0:T(8,128)(2,1)}, bf...) custom-call(s32[2]{0:T(128)} %pad_add_fusion.who_ref, ...), custom_call_target="tpu_custom_call" | custom-call | flops 16106127360 | bytes 10485760 | tf_op jit(solution)/shard_map/first_group/pallas_call | solution.py:308
  33.4 0.9 copy-done.1
  34.4 2.6 %collective-permute-start.7 = (bf16[160,2560]{1,0:T(8,128)(2,1)S(1)}, bf16[160,2560]{1,0:T(8,128)(2,1)S(1)}, u32[]{:S(2)}, u32[]{:S(2)}) collective-permute-start(bf16[160,2560]{1,0:T(8,128)(2,1)S(1)} %constant_dynamic-slice_fusion), channel_id=1, source_target_pairs={{0,8},{4,12},{8,0},{12,4},{1,9},{5,13},{9,1},{13,5},{2,10},{6,14},... | collective-permute-start | bytes 2457608 | tf_op jit(solution)/shard_map/ppermute | solution.py:393
  37.6 1.3 collective-permute-start.2
  38.9 12.0 %next_group.2 = (bf16[2048,256]{1,0:T(8,128)(2,1)}, f32[16,128,256]{2,1,0:T(8,128)}, f32[16,8,256]{2,1,0:T(8,128)}, bf16[144,256]{1,0:T(8,128)(2,1)}, bf16[144,2...) custom-call(s32[2]{0:T(128)} %pad_add_fusion.who_ref, ...), custom_call_target="tpu_custom_call" | custom-call | flops 8053063680 | bytes 10485760 | tf_op jit(solution)/shard_map/next_group/pallas_call | solution.py:327
  51.6 20.9 %outputs.3 = (bf16[512,512]{1,0:T(8,128)(2,1)}, bf16[512,512]{1,0:T(8,128)(2,1)}, bf16[512,512]{1,0:T(8,128)(2,1)}, bf16[512,512]{1,0:T(8,128)(2,1)}) custom-call(s32[2]{0:T(128)} %pad_add_fusion.who_ref, bf16[2048,512]{1,0:T(8,128)(2,1)} %get-tuple-element.50.u_ref, bf16[2048,2560]{1,0:T(8,128)(2,1)} %refs_0_.13, ...), custom_call_target="tpu_custom_call" | custom-call | flops 6442450944 | bytes 8388608 | tf_op jit(solution)/shard_map/outputs/pallas_call | solution.py:373
  72.5 0.9 copy-done.2
  73.7 1.7 collective-permute-start.11
  76.0 1.3 collective-permute-start.6
  77.3 15.5 %next_group.3 = (bf16[2048,512]{1,0:T(8,128)(2,1)}, f32[16,128,512]{2,1,0:T(8,128)}, f32[16,8,512]{2,1,0:T(8,128)}, bf16[144,512]{1,0:T(8,128)(2,1)}, bf16[144,5...) custom-call(s32[2]{0:T(128)} %pad_add_fusion.who_ref, ...), custom_call_target="tpu_custom_call" | custom-call | flops 10737418240 | bytes 10485760 | tf_op jit(solution)/shard_map/next_group/pallas_call | solution.py:327
  93.5 15.6 %outputs.4 = (bf16[512,256]{1,0:T(8,128)(2,1)}, bf16[512,256]{1,0:T(8,128)(2,1)}, bf16[512,256]{1,0:T(8,128)(2,1)}, bf16[512,256]{1,0:T(8,128)(2,1)}) custom-call(s32[2]{0:T(128)} %pad_add_fusion.who_ref, bf16[2048,256]{1,0:T(8,128)(2,1)} %get-tuple-element.65.after_ref.u_ref, bf16[2048,2560]{1,0:T(8,128)(2,1)} %refs_0_.13, ...), custom_call_target="tpu_custom_call" | custom-call | flops 3221225472 | bytes 4194304 | tf_op jit(solution)/shard_map/outputs/pallas_call | solution.py:373
  109.1 0.9 copy-done
  110.8 1.5 collective-permute-start.9
  112.7 2.6 %collective-permute-start.13 = (bf16[512,512]{1,0:T(8,128)(2,1)}, bf16[512,512]{1,0:T(8,128)(2,1)S(1)}, u32[]{:S(2)}, u32[]{:S(2)}) collective-permute-start(bf16[512,512]{1,0:T(8,128)(2,1)} %get-tuple-element.87), channel_id=1, source_target_pairs={{0,8},{4,12},{8,0},{12,4},{1,9},{5,13},{9,1},{13,5},{2,10},{6,14},... | collective-permute-start | bytes 1572872 | tf_op jit(solution)/shard_map/ppermute | solution.py:393
  115.3 3.6 %collective-permute-done.10.r3_ref = bf16[144,512]{1,0:T(8,128)(2,1)S(1)} collective-permute-done((bf16[144,512]{1,0:T(8,128)(2,1)S(1)}, bf16[144,512]{1,0:T(8,128)(2,1)S(1)}, u32[]{:S(2)}, u32[]{:S(2)}) %collective-permute-start.10) | collective-permute-done | bytes 147488 | tf_op jit(solution)/shard_map/ppermute | solution.py:393
  118.9 1.6 collective-permute-start.17
  120.5 0.7 copy-done.12
  121.2 0.9 collective-permute-start.14
  122.0 3.8 %collective-permute-done.9.r2_ref = bf16[144,512]{1,0:T(8,128)(2,1)} collective-permute-done((bf16[144,512]{1,0:T(8,128)(2,1)}, bf16[144,512]{1,0:T(8,128)(2,1)}, u32[]{:S(2)}, u32[]{:S(2)}) %collective-permute-start.9) | collective-permute-done | bytes 147488 | tf_op jit(solution)/shard_map/ppermute | solution.py:393
  126.2 20.5 %outputs.5 = (bf16[512,512]{1,0:T(8,128)(2,1)}, bf16[512,512]{1,0:T(8,128)(2,1)}, bf16[512,512]{1,0:T(8,128)(2,1)}, bf16[512,512]{1,0:T(8,128)(2,1)}) custom-call(s32[2]{0:T(128)} %pad_add_fusion.who_ref, bf16[2048,512]{1,0:T(8,128)(2,1)} %get-tuple-element.75.after_ref.u_ref, bf16[2048,2560]{1,0:T(8,128)(2,1)} %refs_0_.13, ...), custom_call_target="tpu_custom_call" | custom-call | flops 6442450944 | bytes 8388608 | tf_op jit(solution)/shard_map/outputs/pallas_call | solution.py:373
  146.7 25.3 %collective-permute-done.14.refs_4_ = bf16[512,256]{1,0:T(8,128)(2,1)S(1)} collective-permute-done((bf16[512,256]{1,0:T(8,128)(2,1)}, bf16[512,256]{1,0:T(8,128)(2,1)S(1)}, u32[]{:S(2)}, u32[]{:S(2)}) %collective-permute-start.14) | collective-permute-done | bytes 262176 | tf_op jit(solution)/shard_map/ppermute | solution.py:393
  172.1 4.6 %collective-permute-start.16 = (bf16[512,512]{1,0:T(8,128)(2,1)}, bf16[512,512]{1,0:T(8,128)(2,1)S(1)}, u32[]{:S(2)}, u32[]{:S(2)}) collective-permute-start(bf16[512,512]{1,0:T(8,128)(2,1)} %get-tuple-element.90), channel_id=1, source_target_pairs={{0,4},{4,0},{8,12},{12,8},{1,5},{5,1},{9,13},{13,9},{2,6},{6,2},{1... | collective-permute-start | bytes 1572872 | tf_op jit(solution)/shard_map/ppermute | solution.py:393
  176.8 11.6 %add_products.4.refs_0_ = f32[512,2560]{1,0:T(8,128)} custom-call(s32[2]{0:T(128)} %pad_add_fusion.who_ref, bf16[2048,2560]{1,0:T(8,128)(2,1)} %refs_0_.13, bf16[512,512]{1,0:T(8,128)(2,1)} %get-tuple-element.66.refs_1_, bf16[1280,2560]{1,0:T(8,128)(2,1)} %refs_8_.1, bf16[1280,2560]{1,0:T(8,128)(2,1)} %refs_8_.1, ...), custom_call_target="tpu_custom_call" | custom-call | flops 4697620480 | bytes 2621440 | tf_op jit(solution)/shard_map/add_products/pallas_call | solution.py:354
  188.8 1.9 collective-permute-start.20
  190.8 10.4 %add_products.5.refs_0_ = f32[512,2560]{1,0:T(8,128)} custom-call(s32[2]{0:T(128)} %pad_add_fusion.who_ref, f32[512,2560]{1,0:T(8,128)} %add_products.4.refs_0_, bf16[512,512]{1,0:T(8,128)(2,1)} %copy-done.4, bf16[1280,2560]{1,0:T(8,128)(2,1)} %all-gather.6.cloned.1.call-done.refs_2_.refs_3_.refs_5_, ...), custom_call_target="tpu_custom_call" | custom-call | flops 2684354560 | bytes 2621440 | tf_op jit(solution)/shard_map/add_products/pallas_call | solution.py:354
  202.3 11.1 %add_products.6.refs_0_ = f32[512,2560]{1,0:T(8,128)} custom-call(s32[2]{0:T(128)} %pad_add_fusion.who_ref, f32[512,2560]{1,0:T(8,128)} %add_products.5.refs_0_, bf16[512,512]{1,0:T(8,128)(2,1)} %copy-done.6, bf16[1280,2560]{1,0:T(8,128)(2,1)} %all-gather.4.cloned.1.call-done.refs_10_.refs_11_.refs_7_.refs_2_.refs_3_, ...), custom_call_target="tpu_custom_call" | custom-call | flops 3355443200 | bytes 2621440 | tf_op jit(solution)/shard_map/add_products/pallas_call | solution.py:354
  213.4 10.4 %collective-permute-done.19.refs_1_ = bf16[512,512]{1,0:T(8,128)(2,1)S(1)} collective-permute-done((bf16[512,512]{1,0:T(8,128)(2,1)}, bf16[512,512]{1,0:T(8,128)(2,1)S(1)}, u32[]{:S(2)}, u32[]{:S(2)}) %collective-permute-start.19) | collective-permute-done | bytes 524320 | tf_op jit(solution)/shard_map/ppermute | solution.py:393
  223.7 11.1 %collective-permute-done.20.refs_4_ = bf16[512,512]{1,0:T(8,128)(2,1)S(1)} collective-permute-done((bf16[512,512]{1,0:T(8,128)(2,1)}, bf16[512,512]{1,0:T(8,128)(2,1)S(1)}, u32[]{:S(2)}, u32[]{:S(2)}) %collective-permute-start.20) | collective-permute-done | bytes 524320 | tf_op jit(solution)/shard_map/ppermute | solution.py:393
  234.8 0.8 copy-done.8
  235.6 9.7 %add_products.7 = bf16[512,2560]{1,0:T(8,128)(2,1)} custom-call(s32[2]{0:T(128)} %pad_add_fusion.who_ref, f32[512,2560]{1,0:T(8,128)} %add_products.6.refs_0_, bf16[512,512]{1,0:T(8,128)(2,1)} %copy-done.7, bf16[1280,2560]{1,0:T(8,128)(2,1)} %all-gather.6.cloned.1.call-done.refs_2_.refs_3_.refs_5_, ...), custom_call_target="tpu_custom_call" | custom-call | flops 2684354560 | bytes 2621440 | tf_op jit(solution)/shard_map/add_products/pallas_call | solution.py:354
  (73 shorter events, 6.3 us)
Async XLA Ops:
  6.5 170.2 %all-gather.4.cloned.1.call-start = ((), (), s32[]{:S(2)}) async-start(), calls=%async_computation | async-start | bytes 7372800 | tf_op jit(solution)/shard_map/all_gather | solution.py:409
  7.7 25.7 %collective-permute-start.3 = (bf16[160,2560]{1,0:T(8,128)(2,1)S(1)}, bf16[160,2560]{1,0:T(8,128)(2,1)S(1)}, u32[]{:S(2)}, u32[]{:S(2)}) collective-permute-start(bf16[160,2560]{1,0:T(8,128)(2,1)S(1)} %constant_dynamic-slice_fusion), channel_id=1, source_target_pairs={{0,4},{4,0},{8,12},{12,8},{1,5},{5,1},{9,13},{13,9},{2,6},{6,2},{1... | collective-permute-start | bytes 2457608 | tf_op jit(solution)/shard_map/ppermute | solution.py:393
  34.3 156.4 %all-gather.6.cloned.1.call-start = ((), (), s32[]{:S(2)}) async-start(), calls=%async_computation.1 | async-start | bytes 7372800 | tf_op jit(solution)/shard_map/all_gather | solution.py:409
  34.4 38.1 %collective-permute-start.7 = (bf16[160,2560]{1,0:T(8,128)(2,1)S(1)}, bf16[160,2560]{1,0:T(8,128)(2,1)S(1)}, u32[]{:S(2)}, u32[]{:S(2)}) collective-permute-start(bf16[160,2560]{1,0:T(8,128)(2,1)S(1)} %constant_dynamic-slice_fusion), channel_id=1, source_target_pairs={{0,8},{4,12},{8,0},{12,4},{1,9},{5,13},{9,1},{13,5},{2,10},{6,14},... | collective-permute-start | bytes 2457608 | tf_op jit(solution)/shard_map/ppermute | solution.py:393
  37.0 13.9 %collective-permute-start = (bf16[144,512]{1,0:T(8,128)(2,1)}, bf16[144,512]{1,0:T(8,128)(2,1)S(1)}, u32[]{:S(2)}, u32[]{:S(2)}) collective-permute-start(bf16[144,512]{1,0:T(8,128)(2,1)} %get-tuple-element.60), channel_id=1, source_target_pairs={{0,1},{1,0},{2,3},{3,2},{4,5},{5,4},{6,7},{7,6},{8,9},{9,8},{10,11... | collective-permute-start | bytes 442376 | tf_op jit(solution)/shard_map/ppermute | solution.py:393
  37.0 13.9 %collective-permute-start.1 = (bf16[144,512]{1,0:T(8,128)(2,1)}, bf16[144,512]{1,0:T(8,128)(2,1)S(1)}, u32[]{:S(2)}, u32[]{:S(2)}) collective-permute-start(bf16[144,512]{1,0:T(8,128)(2,1)} %get-tuple-element.61), channel_id=1, source_target_pairs={{0,2},{1,3},{2,0},{3,1},{4,6},{5,7},{6,4},{7,5},{8,10},{9,11},{10,... | collective-permute-start | bytes 442376 | tf_op jit(solution)/shard_map/ppermute | solution.py:393
  37.6 13.4 %collective-permute-start.2 = (bf16[144,512]{1,0:T(8,128)(2,1)}, bf16[144,512]{1,0:T(8,128)(2,1)}, u32[]{:S(2)}, u32[]{:S(2)}) collective-permute-start(bf16[144,512]{1,0:T(8,128)(2,1)} %get-tuple-element.62), channel_id=1, source_target_pairs={{0,3},{1,2},{2,1},{3,0},{4,7},{5,6},{6,5},{7,4},{8,11},{9,10},{10,... | collective-permute-start | bytes 442376 | tf_op jit(solution)/shard_map/ppermute | solution.py:393
  51.6 24.3 %copy-start.20 = (bf16[144,256]{1,0:T(8,128)(2,1)S(1)}, bf16[144,256]{1,0:T(8,128)(2,1)}, u32[]{:S(2)}) copy-start(bf16[144,256]{1,0:T(8,128)(2,1)} %get-tuple-element.73) | copy-start | bytes 221188
  73.5 127.8 %all-gather.8.cloned.1.call-start = ((), (), s32[]{:S(2)}) async-start(), calls=%async_computation.2 | async-start | bytes 7372800 | tf_op jit(solution)/shard_map/all_gather | solution.py:409
  73.7 35.4 %collective-permute-start.11 = (bf16[160,2560]{1,0:T(8,128)(2,1)}, bf16[160,2560]{1,0:T(8,128)(2,1)S(1)}, u32[]{:S(2)}, u32[]{:S(2)}) collective-permute-start(bf16[160,2560]{1,0:T(8,128)(2,1)} %copy-done.2), channel_id=1, source_target_pairs={{0,4},{4,0},{8,12},{12,8},{1,5},{5,1},{9,13},{13,9},{2,6},{6,2},{1... | collective-permute-start | bytes 2457608 | tf_op jit(solution)/shard_map/ppermute | solution.py:393
  75.4 17.4 %collective-permute-start.4 = (bf16[144,256]{1,0:T(8,128)(2,1)}, bf16[144,256]{1,0:T(8,128)(2,1)S(1)}, u32[]{:S(2)}, u32[]{:S(2)}) collective-permute-start(bf16[144,256]{1,0:T(8,128)(2,1)} %get-tuple-element.71), channel_id=1, source_target_pairs={{0,1},{1,0},{2,3},{3,2},{4,5},{5,4},{6,7},{7,6},{8,9},{9,8},{10,11... | collective-permute-start | bytes 221192 | tf_op jit(solution)/shard_map/ppermute | solution.py:393
  75.4 17.4 %collective-permute-start.5 = (bf16[144,256]{1,0:T(8,128)(2,1)}, bf16[144,256]{1,0:T(8,128)(2,1)S(1)}, u32[]{:S(2)}, u32[]{:S(2)}) collective-permute-start(bf16[144,256]{1,0:T(8,128)(2,1)} %get-tuple-element.72), channel_id=1, source_target_pairs={{0,2},{1,3},{2,0},{3,1},{4,6},{5,7},{6,4},{7,5},{8,10},{9,11},{10,... | collective-permute-start | bytes 221192 | tf_op jit(solution)/shard_map/ppermute | solution.py:393
  76.0 16.9 %collective-permute-start.6 = (bf16[144,256]{1,0:T(8,128)(2,1)S(1)}, bf16[144,256]{1,0:T(8,128)(2,1)S(1)}, u32[]{:S(2)}, u32[]{:S(2)}) collective-permute-start(bf16[144,256]{1,0:T(8,128)(2,1)S(1)} %copy-done.20), channel_id=1, source_target_pairs={{0,3},{1,2},{2,1},{3,0},{4,7},{5,6},{6,5},{7,4},{8,11},{9,10},{10,... | collective-permute-start | bytes 221192 | tf_op jit(solution)/shard_map/ppermute | solution.py:393
  93.5 16.6 %copy-start.19 = (bf16[144,512]{1,0:T(8,128)(2,1)S(1)}, bf16[144,512]{1,0:T(8,128)(2,1)}, u32[]{:S(2)}) copy-start(bf16[144,512]{1,0:T(8,128)(2,1)} %get-tuple-element.83) | copy-start | bytes 442372
  93.5 17.0 %copy-start.18 = (bf16[144,512]{1,0:T(8,128)(2,1)S(1)}, bf16[144,512]{1,0:T(8,128)(2,1)}, u32[]{:S(2)}) copy-start(bf16[144,512]{1,0:T(8,128)(2,1)} %get-tuple-element.81) | copy-start | bytes 442372
  110.1 8.8 %collective-permute-start.10 = (bf16[144,512]{1,0:T(8,128)(2,1)S(1)}, bf16[144,512]{1,0:T(8,128)(2,1)S(1)}, u32[]{:S(2)}, u32[]{:S(2)}) collective-permute-start(bf16[144,512]{1,0:T(8,128)(2,1)S(1)} %copy-done.19), channel_id=1, source_target_pairs={{0,3},{1,2},{2,1},{3,0},{4,7},{5,6},{6,5},{7,4},{8,11},{9,10},{10,... | collective-permute-start | bytes 442376 | tf_op jit(solution)/shard_map/ppermute | solution.py:393
  110.5 10.0 %collective-permute-start.8 = (bf16[144,512]{1,0:T(8,128)(2,1)S(1)}, bf16[144,512]{1,0:T(8,128)(2,1)S(1)}, u32[]{:S(2)}, u32[]{:S(2)}) collective-permute-start(bf16[144,512]{1,0:T(8,128)(2,1)S(1)} %copy-done.18), channel_id=1, source_target_pairs={{0,1},{1,0},{2,3},{3,2},{4,5},{5,4},{6,7},{7,6},{8,9},{9,8},{10,11... | collective-permute-start | bytes 442376 | tf_op jit(solution)/shard_map/ppermute | solution.py:393
  110.8 15.0 %collective-permute-start.9 = (bf16[144,512]{1,0:T(8,128)(2,1)}, bf16[144,512]{1,0:T(8,128)(2,1)}, u32[]{:S(2)}, u32[]{:S(2)}) collective-permute-start(bf16[144,512]{1,0:T(8,128)(2,1)} %get-tuple-element.82), channel_id=1, source_target_pairs={{0,2},{1,3},{2,0},{3,1},{4,6},{5,7},{6,4},{7,5},{8,10},{9,11},{10,... | collective-permute-start | bytes 442376 | tf_op jit(solution)/shard_map/ppermute | solution.py:393
  112.3 59.8 %collective-permute-start.12 = (bf16[512,512]{1,0:T(8,128)(2,1)}, bf16[512,512]{1,0:T(8,128)(2,1)S(1)}, u32[]{:S(2)}, u32[]{:S(2)}) collective-permute-start(bf16[512,512]{1,0:T(8,128)(2,1)} %get-tuple-element.86), channel_id=1, source_target_pairs={{0,4},{4,0},{8,12},{12,8},{1,5},{5,1},{9,13},{13,9},{2,6},{6,2},{1... | collective-permute-start | bytes 1572872 | tf_op jit(solution)/shard_map/ppermute | solution.py:393
  112.7 76.1 %collective-permute-start.13 = (bf16[512,512]{1,0:T(8,128)(2,1)}, bf16[512,512]{1,0:T(8,128)(2,1)S(1)}, u32[]{:S(2)}, u32[]{:S(2)}) collective-permute-start(bf16[512,512]{1,0:T(8,128)(2,1)} %get-tuple-element.87), channel_id=1, source_target_pairs={{0,8},{4,12},{8,0},{12,4},{1,9},{5,13},{9,1},{13,5},{2,10},{6,14},... | collective-permute-start | bytes 1572872 | tf_op jit(solution)/shard_map/ppermute | solution.py:393
  118.9 7.3 %copy-start.11 = (bf16[144,512]{1,0:T(8,128)(2,1)}, bf16[144,512]{1,0:T(8,128)(2,1)S(1)}, u32[]{:S(2)}) copy-start(bf16[144,512]{1,0:T(8,128)(2,1)S(1)} %collective-permute-done.10.r3_ref) | copy-start | bytes 442372
  118.9 82.3 %collective-permute-start.17 = (bf16[512,512]{1,0:T(8,128)(2,1)}, bf16[512,512]{1,0:T(8,128)(2,1)S(1)}, u32[]{:S(2)}, u32[]{:S(2)}) collective-permute-start(bf16[512,512]{1,0:T(8,128)(2,1)} %get-tuple-element.91), channel_id=1, source_target_pairs={{0,12},{4,8},{8,4},{12,0},{1,13},{5,9},{9,5},{13,1},{2,14},{6,10},... | collective-permute-start | bytes 1572872 | tf_op jit(solution)/shard_map/ppermute | solution.py:393
  121.2 50.9 %collective-permute-start.14 = (bf16[512,256]{1,0:T(8,128)(2,1)}, bf16[512,256]{1,0:T(8,128)(2,1)S(1)}, u32[]{:S(2)}, u32[]{:S(2)}) collective-permute-start(bf16[512,256]{1,0:T(8,128)(2,1)} %get-tuple-element.88), channel_id=1, source_target_pairs={{0,8},{4,12},{8,0},{12,4},{1,9},{5,13},{9,1},{13,5},{2,10},{6,14},... | collective-permute-start | bytes 786440 | tf_op jit(solution)/shard_map/ppermute | solution.py:393
  125.8 62.6 %collective-permute-start.15 = (bf16[512,256]{1,0:T(8,128)(2,1)}, bf16[512,256]{1,0:T(8,128)(2,1)}, u32[]{:S(2)}, u32[]{:S(2)}) collective-permute-start(bf16[512,256]{1,0:T(8,128)(2,1)} %get-tuple-element.89), channel_id=1, source_target_pairs={{0,4},{4,0},{8,12},{12,8},{1,5},{5,1},{9,13},{13,9},{2,6},{6,2},{1... | collective-permute-start | bytes 786440 | tf_op jit(solution)/shard_map/ppermute | solution.py:393
  172.0 16.4 %copy-start.9 = (bf16[512,256]{1,0:T(8,128)(2,1)}, bf16[512,256]{1,0:T(8,128)(2,1)S(1)}, u32[]{:S(2)}) copy-start(bf16[512,256]{1,0:T(8,128)(2,1)S(1)} %collective-permute-done.14.refs_4_) | copy-start | bytes 786436
  172.0 29.2 %collective-permute-start.18 = (bf16[512,256]{1,0:T(8,128)(2,1)}, bf16[512,256]{1,0:T(8,128)(2,1)S(1)}, u32[]{:S(2)}, u32[]{:S(2)}) collective-permute-start(bf16[512,256]{1,0:T(8,128)(2,1)} %get-tuple-element.92), channel_id=1, source_target_pairs={{0,12},{4,8},{8,4},{12,0},{1,13},{5,9},{9,5},{13,1},{2,14},{6,10},... | collective-permute-start | bytes 786440 | tf_op jit(solution)/shard_map/ppermute | solution.py:393
  172.1 4.6 %copy-start.5 = (bf16[512,512]{1,0:T(8,128)(2,1)}, bf16[512,512]{1,0:T(8,128)(2,1)S(1)}, u32[]{:S(2)}) copy-start(bf16[512,512]{1,0:T(8,128)(2,1)S(1)} %collective-permute-done.12.refs_9_) | copy-start | bytes 1572868
  172.1 29.1 %collective-permute-start.16 = (bf16[512,512]{1,0:T(8,128)(2,1)}, bf16[512,512]{1,0:T(8,128)(2,1)S(1)}, u32[]{:S(2)}, u32[]{:S(2)}) collective-permute-start(bf16[512,512]{1,0:T(8,128)(2,1)} %get-tuple-element.90), channel_id=1, source_target_pairs={{0,4},{4,0},{8,12},{12,8},{1,5},{5,1},{9,13},{13,9},{2,6},{6,2},{1... | collective-permute-start | bytes 1572872 | tf_op jit(solution)/shard_map/ppermute | solution.py:393
  188.4 35.3 %collective-permute-start.19 = (bf16[512,512]{1,0:T(8,128)(2,1)}, bf16[512,512]{1,0:T(8,128)(2,1)S(1)}, u32[]{:S(2)}, u32[]{:S(2)}) collective-permute-start(bf16[512,512]{1,0:T(8,128)(2,1)} %get-tuple-element.93), channel_id=1, source_target_pairs={{0,8},{4,12},{8,0},{12,4},{1,9},{5,13},{9,1},{13,5},{2,10},{6,14},... | collective-permute-start | bytes 1572872 | tf_op jit(solution)/shard_map/ppermute | solution.py:393
  188.8 1.9 copy-start.4
  188.8 46.0 %collective-permute-start.20 = (bf16[512,512]{1,0:T(8,128)(2,1)}, bf16[512,512]{1,0:T(8,128)(2,1)S(1)}, u32[]{:S(2)}, u32[]{:S(2)}) collective-permute-start(bf16[512,512]{1,0:T(8,128)(2,1)} %get-tuple-element.94), channel_id=1, source_target_pairs={{0,12},{4,8},{8,4},{12,0},{1,13},{5,9},{9,5},{13,1},{2,14},{6,10},... | collective-permute-start | bytes 1572872 | tf_op jit(solution)/shard_map/ppermute | solution.py:393
  223.7 11.1 %copy-start.7 = (bf16[512,512]{1,0:T(8,128)(2,1)}, bf16[512,512]{1,0:T(8,128)(2,1)S(1)}, u32[]{:S(2)}) copy-start(bf16[512,512]{1,0:T(8,128)(2,1)S(1)} %collective-permute-done.19.refs_1_) | copy-start | bytes 1572868
  (13 other events, 10.1 us)
Sparse Core Ops, SparseCore 0:
  34.5 47.5 all-gather.3
  83.9 54.8 all-gather.5
  140.7 45.6 all-gather.7
